TPU v7x, 8 devices: a whole 2x2x1 slice. The times are simulated.
8 devices in a mesh: dp: 1 (over z), row: 2 (over y), col: 4 (over x, core).
Axes of the slice: x: 2, y: 2, z: 1, core: 2. Of those that a mesh axis runs over, the one named last changes fastest.
Arguments:
- pair_rep: bfloat16 [512, 512, 128], P(('dp', 'row'), 'col')
- res_mask: int32 [512], P('dp')
- ln_gamma: float32 [128], replicated
- ln_beta: float32 [128], replicated
- w_q: bfloat16 [128, 128], replicated
- w_k: bfloat16 [128, 128], replicated
- w_v: bfloat16 [128, 128], replicated
- w_b: bfloat16 [128, 4], replicated
- w_g: bfloat16 [128, 128], replicated
- w_o: bfloat16 [128, 128], replicated
Outputs:
- output: bfloat16 [512, 512, 128], P(('dp', 'row'), 'col')
All inputs are finite; a program needn't handle non-finite values.
Results may differ from a plain program's by a relative error of at most 0.0072822.
Values are sent between devices in bfloat16 or wider.
A program may use at most 1 GiB of HBM per device.

v0:
```python
import functools

import jax
import jax.numpy as jnp
from jax import lax
from jax.experimental import pallas as pl
from jax.experimental.pallas import tpu as pltpu
from jax.sharding import PartitionSpec as P


LN_EPS = 1e-5
CHUNKS = (32, 64, 32, 32, 32, 32, 16, 16)
NORM_ROWS = 32
ATTEND_ROWS = 16
GROUP = 8
SCORE_BOUND = 1e8
VALUE_BOUND = 1e20
SUM_RANGE = (1e-10, 1e15)
NN = (((1,), (0,)), ((), ()))
NT = (((1,), (1,)), ((), ()))
f32, bf16 = jnp.float32, jnp.bfloat16
dot = functools.partial(lax.dot_general, preferred_element_type=f32)
VMEM_LIMIT = pltpu.CompilerParams(vmem_limit_bytes=67043328)


def whole(shape):
    return pl.BlockSpec(shape, lambda *_: (0,) * len(shape))


def plan_kernel(heads, sizes, mask_ref, gamma_ref, beta_ref, wq_ref, wk_ref, wv_ref, wb_ref, wg_ref, info_ref, wkv_ref, wqg_ref):
    chan = gamma_ref.shape[1]
    dim = chan // heads
    row_idx, col_idx = lax.axis_index('row'), lax.axis_index('col')
    wkv_ref[:, :chan], wkv_ref[:, chan:] = wk_ref[...], wv_ref[...]
    wqg_ref[:, :chan], wqg_ref[:, chan:] = wq_ref[...], wg_ref[...]
    reach = jnp.broadcast_to(jnp.abs(gamma_ref[...]) * chan ** 0.5 + jnp.abs(beta_ref[...]), (8, chan)) * 1.05
    q = jnp.dot(reach, jnp.abs(wq_ref[...].astype(f32)), preferred_element_type=f32) * dim ** -0.5
    k = jnp.dot(reach, jnp.abs(wk_ref[...].astype(f32)), preferred_element_type=f32)
    v = jnp.dot(reach, jnp.abs(wv_ref[...].astype(f32)), preferred_element_type=f32)
    b = jnp.dot(reach, jnp.abs(wb_ref[...].astype(f32)), preferred_element_type=f32)
    s_bound = (jnp.sum(q * k) + jnp.sum(b)) * 1.1
    v_bound = jnp.max(v) * 1.1
    length = jnp.sum(mask_ref[...].astype(f32)).astype(jnp.int32)
    used = jnp.where(length <= sizes[0], sizes[0], sizes[1])
    info_ref[0] = col_idx
    info_ref[1] = 2 * row_idx + (col_idx & 1)
    info_ref[2] = length
    info_ref[3] = jnp.where((s_bound < SCORE_BOUND) & (v_bound < VALUE_BOUND), used, sizes[2])


def make_plan(heads, sizes, *args):
    chan = args[1].shape[1]
    return pl.pallas_call(
        functools.partial(plan_kernel, heads, sizes),
        in_specs=[whole(x.shape) for x in args],
        out_specs=[pl.BlockSpec(memory_space=pltpu.SMEM), whole((chan, 2 * chan)), whole((chan, 2 * chan))],
        out_shape=[jax.ShapeDtypeStruct((4,), jnp.int32)] + [jax.ShapeDtypeStruct((chan, 2 * chan), bf16)] * 2,
        compiler_params=VMEM_LIMIT,
        name="plan",
    )(*args)


def norm_kernel(places, z_ref, gamma_ref, beta_ref, wb_ref, *out_refs):
    rows, cols, chan = z_ref.shape
    b_ref = out_refs[len(places)]
    heads = b_ref.shape[1]
    z = z_ref[...].reshape(rows * cols, chan)
    ones = jnp.full((chan, chan), 1.0 / chan, bf16)
    centered = z.astype(f32) - dot(z, ones, NN)
    var = jnp.mean(centered * centered, axis=-1, keepdims=True)
    a = (centered * lax.rsqrt(var + LN_EPS) * gamma_ref[...] + beta_ref[...]).astype(bf16)
    blocks = a.reshape(rows, cols, chan)
    i = pl.program_id(0)
    for out_ref, (lo, steps, offset) in zip(out_refs, places):
        @pl.when((i >= lo) & (i < lo + steps))
        def _():
            out_ref[...] = blocks[offset:offset + out_ref.shape[0]]
    for out_ref in out_refs[len(places) + 1:]:
        out_ref[...] = blocks
    wb = jnp.concatenate([wb_ref[...].astype(f32), jnp.zeros((chan, chan - heads), f32)], axis=1).T[:8].astype(bf16)
    b = dot(wb, a, NT)
    for r in range(rows):
        b_ref[r] = b[:heads, r * cols:(r + 1) * cols].astype(bf16)


def normalize(z, gamma, beta, w_b, start, chunks, joined):
    cols, chan = z.shape[1:]
    heads = w_b.shape[1]
    step = NORM_ROWS
    first = start // step
    rows = sum(chunks)
    places, specs = [], []
    for i, c in enumerate(chunks):
        lo, offset = divmod(sum(chunks[:i]), step)
        steps = max(c // step, 1)
        places.append((lo, steps, offset))
        specs.append(pl.BlockSpec((min(step, c), cols, chan), lambda i, lo=lo, steps=steps: (jnp.clip(i - lo, 0, steps - 1), 0, 0)))
    specs.append(pl.BlockSpec((step, heads, cols), lambda i: (i, 0, 0)))
    shapes = [jax.ShapeDtypeStruct((c, cols, chan), bf16) for c in chunks] + [jax.ShapeDtypeStruct((rows, heads, cols), bf16)]
    if joined:
        specs.append(pl.BlockSpec((step, cols, chan), lambda i: (i, 0, 0)))
        shapes.append(jax.ShapeDtypeStruct((rows, cols, chan), bf16))
    return pl.pallas_call(
        functools.partial(norm_kernel, places),
        grid=(rows // step,),
        in_specs=[
            pl.BlockSpec((step, cols, chan), lambda i: (first + i, 0, 0)),
            whole((1, chan)), whole((1, chan)), whole(w_b.shape),
        ],
        out_specs=specs,
        out_shape=shapes,
        compiler_params=VMEM_LIMIT,
        cost_estimate=pl.CostEstimate(flops=rows * cols * chan * 300, bytes_accessed=rows * cols * chan * 4, transcendentals=0),
        name="norm",
    )(z, gamma, beta, w_b)


def bias_kernel(info_ref, *refs):
    parts, out_ref = refs[:-1], refs[-1]
    queries, heads, cols = parts[0].shape
    base, length = info_ref[1], info_ref[2]
    for m, part in enumerate(parts):
        first = pl.multiple_of((base ^ m) * cols, cols)
        key = first + lax.broadcasted_iota(jnp.int32, (cols, queries), 0)
        key_bias = jnp.where(key < length, 0.0, -1e9).astype(f32)
        b = part[...].astype(f32)
        for h in range(heads):
            out_ref[pl.ds(first, cols), h * queries:(h + 1) * queries] = b[:, h, :].T + key_bias


def lay_bias(info, parts):
    queries, heads, cols = parts[0].shape
    shape = (len(parts) * cols, heads * queries)
    return pl.pallas_call(
        bias_kernel,
        grid_spec=pltpu.PrefetchScalarGridSpec(
            num_scalar_prefetch=1, grid=(1,),
            in_specs=[whole(p.shape) for p in parts], out_specs=whole(shape),
        ),
        out_shape=jax.ShapeDtypeStruct(shape, f32),
        compiler_params=VMEM_LIMIT,
        name="bias",
    )(info, *parts)


def attend_kernel(heads, sizes, info_ref, *refs):
    blocks = refs[:4]
    z_ref, bias_ref, wkv_ref, wqg_ref, wo_ref = refs[4:9]
    out_ref, k_s, vt_s, q_s, g_s, p_s, l_s, o_s = refs[-8:]
    step, cols, chan = z_ref.shape
    dim = chan // heads
    col, used = info_ref[0], info_ref[3]

    @pl.when(pl.program_id(0) == 0)
    def _():
        q_s[...] = jnp.zeros_like(q_s)

    def project(i, carry):
        rows = pl.ds(GROUP * i, GROUP)
        for p, ref in enumerate(blocks):
            first = pl.multiple_of((col ^ p) * cols, cols)
            kv = dot(ref[rows].reshape(GROUP * cols, chan), wkv_ref[...], NN).astype(bf16)
            k_s[rows, pl.ds(first, cols), :] = kv[:, :chan].reshape(GROUP, cols, chan)
            v = kv[:, chan:].reshape(GROUP, cols, chan)
            for r in range(GROUP):
                vt_s[GROUP * i + r, :, pl.ds(first, cols)] = v[r].T
        qg = dot(blocks[0][rows].reshape(GROUP * cols, chan), wqg_ref[...], NN)
        q = (qg[:, :chan] * dim ** -0.5).astype(bf16).reshape(GROUP, cols, chan)
        for r in range(GROUP):
            q_t = q[r].T
            for h in range(heads):
                q_s[GROUP * i + r, h * dim:(h + 1) * dim, h * cols:(h + 1) * cols] = q_t[h * dim:(h + 1) * dim]
        g_s[rows] = jax.nn.sigmoid(qg[:, chan:]).reshape(GROUP, cols, chan)
        return carry

    lax.fori_loop(0, step // GROUP, project, 0)

    def run(keys, shift):
        def weigh(r, slot):
            s = dot(k_s[r, :keys, :], q_s[r], NN) + bias_ref[:keys, :]
            e = jnp.exp(s - jnp.max(s, axis=0, keepdims=True) if shift else s)
            l_s[r] = jnp.sum(e, axis=0, keepdims=True)
            p_s[slot, :keys, :] = e.astype(bf16)

        def mix(r, slot):
            o = dot(vt_s[r, :, :keys], p_s[slot, :keys, :], NN)
            inv = 1.0 / l_s[r]
            for h in range(heads):
                part = o[h * dim:(h + 1) * dim, h * cols:(h + 1) * cols]
                o_s[r, h * dim:(h + 1) * dim, :] = part * inv[:, h * cols:(h + 1) * cols]

        def pair(i, carry):
            r = 2 * i
            weigh(r, 0)
            mix(lax.rem(r + step - 1, step), 1)
            weigh(r + 1, 1)
            mix(r, 0)
            return carry

        def single(r, carry):
            weigh(r, 0)
            mix(r, 0)
            return carry

        if shift:
            lax.fori_loop(0, step, single, 0)
        else:
            lax.fori_loop(0, step // 2, pair, 0)
            mix(step - 1, 1)

    for keys in sizes[:-1]:
        pl.when(used == keys)(functools.partial(run, keys, False))
    l = l_s[...]
    fine = (used < sizes[-1]) & (jnp.min(l) > SUM_RANGE[0]) & (jnp.max(l) < SUM_RANGE[1])
    pl.when(jnp.logical_not(fine))(functools.partial(run, sizes[-1], True))

    def finish(i, carry):
        rows = pl.ds(GROUP * i, GROUP)
        gated = jnp.concatenate([(o_s[GROUP * i + r].T * g_s[GROUP * i + r]).astype(bf16) for r in range(GROUP)], axis=0)
        update = dot(gated, wo_ref[...], NN).reshape(GROUP, cols, chan)
        out_ref[rows] = (z_ref[rows].astype(f32) + update).astype(bf16)
        return carry

    lax.fori_loop(0, step // GROUP, finish, 0)


def attend(heads, sizes, info, blocks, skips, z, bias, weights, prev, start, rows):
    cols, chan = z.shape[1:]
    step = ATTEND_ROWS
    first = start // step
    keys = 4 * cols
    here = [pl.BlockSpec((step, cols, chan), lambda i, _, skip=skip: (skip // step + i, 0, 0)) for skip in skips]
    there = pl.BlockSpec((step, cols, chan), lambda i, _: (first + i, 0, 0))
    args = [info] + list(blocks) + [z, bias] + list(weights)
    specs = here + [there, whole(bias.shape)] + [whole(w.shape) for w in weights]
    alias = {}
    if prev is not None:
        alias = {len(args): 0}
        args.append(prev)
        specs.append(pl.BlockSpec(memory_space=pl.ANY))
    return pl.pallas_call(
        functools.partial(attend_kernel, heads, sizes),
        grid_spec=pltpu.PrefetchScalarGridSpec(
            num_scalar_prefetch=1, grid=(rows // step,), in_specs=specs, out_specs=there,
            scratch_shapes=[
                pltpu.VMEM((step, keys, chan), bf16),
                pltpu.VMEM((step, chan, keys), bf16),
                pltpu.VMEM((step, chan, heads * cols), bf16),
                pltpu.VMEM((step, cols, chan), f32),
                pltpu.VMEM((2, keys, heads * cols), bf16),
                pltpu.VMEM((step, 1, heads * cols), f32),
                pltpu.VMEM((step, chan, cols), f32),
            ],
        ),
        out_shape=jax.ShapeDtypeStruct(z.shape, z.dtype),
        input_output_aliases=alias,
        compiler_params=VMEM_LIMIT,
        cost_estimate=pl.CostEstimate(flops=rows * cols * chan * 8000, bytes_accessed=rows * cols * chan * 12, transcendentals=0),
        name="attend",
    )(*args)


def solution(mesh):
    tile_spec = P(('dp', 'row'), 'col', None)
    num_rows, num_cols = mesh.shape['row'], mesh.shape['col']
    x_pairs = [(c, c ^ 2) for c in range(num_cols)]
    core_pairs = [(c, c ^ 1) for c in range(num_cols)]

    def bias_pairs(m):
        pairs = []
        for r in range(num_rows):
            for c in range(num_cols):
                e = c ^ m
                pairs.append((r * num_cols + c, (e >> 1) * num_cols + 2 * r + (e & 1)))
        return pairs

    def inner(z, res_mask, ln_gamma, ln_beta, w_q, w_k, w_v, w_b, w_g, w_o):
        row_len, cols, chan = z.shape
        heads = w_b.shape[1]
        sizes = (3 * cols, 7 * cols // 2, 4 * cols)
        col_idx = lax.axis_index('col')
        gamma, beta = ln_gamma.reshape(1, chan), ln_beta.reshape(1, chan)
        starts = [sum(CHUNKS[:i]) for i in range(len(CHUNKS))]
        head = normalize(z, gamma, beta, w_b, 0, CHUNKS[:1], False)
        *tail, tail_bias, rest = normalize(z, gamma, beta, w_b, CHUNKS[0], CHUNKS[1:], True)
        own = [head[0]] + tail
        halves = jnp.concatenate([head[1], tail_bias], axis=0).reshape(2, row_len // 2, heads, cols)
        info, w_kv, w_qg = make_plan(heads, sizes, res_mask.reshape(4, cols), gamma, beta, w_q, w_k, w_v, w_b, w_g)
        weights = (w_kv, w_qg, w_o)

        parts = []
        for m in range(4):
            half = lax.dynamic_index_in_dim(halves, (col_idx ^ m) & 1, 0, keepdims=False)
            parts.append(lax.ppermute(half, ('row', 'col'), bias_pairs(m)))
        bias = lay_bias(info, parts)
        far, near = [], []
        for a in own:
            far.append(lax.ppermute(a, 'col', x_pairs))
        for a in (own[0], rest):
            near.append(lax.ppermute(a, 'col', core_pairs))
        out = None
        for i, (start, rows) in enumerate(zip(starts, CHUNKS)):
            diag = lax.ppermute(far[i], 'col', core_pairs)
            out = attend(heads, sizes, info, (own[i], near[min(i, 1)], far[i], diag), (0, start - CHUNKS[0] if i else 0, 0, 0), z, bias, weights, out, start, rows)
        return out

    return jax.shard_map(inner, mesh=mesh, in_specs=(tile_spec, P('dp'), P(), P(), P(), P(), P(), P(), P(), P()), out_specs=tile_spec, check_vma=False)
```

profile of v0, /device:TPU:0, one launch (start us, length us, event | category | flops | bytes accessed | tf_op | source)
XLA Modules:
  0.0 306.4 jit_solution(2515939068445557330)
XLA Ops:
  0.0 1.4 copy.18.wb_ref
  1.4 15.5 %norm.2 = (bf16[64,128,128]{2,1,0:T(8,128)(2,1)}, bf16[32,128,128]{2,1,0:T(8,128)(2,1)}, bf16[32,128,128]{2,1,0:T(8,128)(2,1)}, bf16[32,128,128]{2,1,0:T(8,128)(...) custom-call(bf16[256,128,128]{2,1,0:T(8,128)(2,1)} %refs_4_.15, ...), custom_call_target="tpu_custom_call" | custom-call | flops 1101004800 | bytes 14680064 | tf_op jit(solution)/shard_map/norm/pallas_call | solution.py:103
  16.9 0.8 collective-permute-start
  17.7 2.5 collective-permute-start.17
  20.2 3.1 %norm.3 = (bf16[32,128,128]{2,1,0:T(8,128)(2,1)}, bf16[32,4,128]{2,1,0:T(4,128)(2,1)}) custom-call(bf16[256,128,128]{2,1,0:T(8,128)(2,1)} %refs_4_.15, f32[1,128]{1,0:T(1,128)} %bitcast.14, f32[1,128]{1,0:T(1,128)} %bitcast.17, bf16[128,4]{1,0:T(8,128)(2,1)} %copy.18.wb_ref), custom_call_target="tpu_custom_call" | custom-call | flops 157286400 | bytes 2097152 | tf_op jit(solution)/shard_map/norm/pallas_call | solution.py:103
  23.3 1.1 pad_maximum_fusion
  24.6 1.3 collective-permute-start.3
  26.2 4.6 %collective-permute-start.5 = (bf16[128,4,128]{2,1,0:T(4,128)(2,1)S(1)}, bf16[128,4,128]{2,1,0:T(4,128)(2,1)}, u32[]{:S(2)}, u32[]{:S(2)}) collective-permute-start(bf16[128,4,128]{2,1,0:T(4,128)(2,1)S(1)} %get-tuple-element.34), channel_id=1, source_target_pairs={{0,4},{1,5},{2,0},{3,1},{4,6},{5,7},{6,2},{7,3}} | collective-permute-start | bytes 393224 | tf_op jit(solution)/shard_map/ppermute | solution.py:294
  30.7 39.8 %collective-permute-start.6 = (bf16[128,4,128]{2,1,0:T(4,128)(2,1)S(1)}, bf16[128,4,128]{2,1,0:T(4,128)(2,1)}, u32[]{:S(2)}, u32[]{:S(2)}) collective-permute-start(bf16[128,4,128]{2,1,0:T(4,128)(2,1)S(1)} %get-tuple-element.33), channel_id=1, source_target_pairs={{0,5},{1,4},{2,1},{3,0},{4,7},{5,6},{6,3},{7,2}} | collective-permute-start | bytes 393224 | tf_op jit(solution)/shard_map/ppermute | solution.py:294
  70.6 4.1 %collective-permute-start.7 = (bf16[16,128,128]{2,1,0:T(8,128)(2,1)}, bf16[16,128,128]{2,1,0:T(8,128)(2,1)}, u32[]{:S(2)}, u32[]{:S(2)}) collective-permute-start(bf16[16,128,128]{2,1,0:T(8,128)(2,1)} %get-tuple-element.26.refs_0_), channel_id=1, source_target_pairs={{0,2},{1,3},{2,0},{3,1},{4,6},{5,7},{6,4},{7,5}} | collective-permute-start | bytes 1572872 | tf_op jit(solution)/shard_map/ppermute | solution.py:298
  74.6 0.8 collective-permute-done.5.refs_2_
  75.4 2.4 collective-permute-done.6.refs_3_
  78.1 11.4 %collective-permute-done.7.refs_2_ = bf16[16,128,128]{2,1,0:T(8,128)(2,1)} collective-permute-done((bf16[16,128,128]{2,1,0:T(8,128)(2,1)}, bf16[16,128,128]{2,1,0:T(8,128)(2,1)}, u32[]{:S(2)}, u32[]{:S(2)}) %collective-permute-start.7) | collective-permute-done | bytes 524320 | tf_op jit(solution)/shard_map/ppermute | solution.py:298
  89.5 0.3 collective-permute-start.15
  89.7 22.2 %collective-permute-done.20.refs_2_ = bf16[32,128,128]{2,1,0:T(8,128)(2,1)} collective-permute-done((bf16[32,128,128]{2,1,0:T(8,128)(2,1)}, bf16[32,128,128]{2,1,0:T(8,128)(2,1)}, u32[]{:S(2)}, u32[]{:S(2)}) %collective-permute-start.20) | collective-permute-done | bytes 1048608 | tf_op jit(solution)/shard_map/ppermute | solution.py:298
  112.2 22.2 %collective-permute-done.15.refs_2_ = bf16[32,128,128]{2,1,0:T(8,128)(2,1)} collective-permute-done((bf16[32,128,128]{2,1,0:T(8,128)(2,1)}, bf16[32,128,128]{2,1,0:T(8,128)(2,1)}, u32[]{:S(2)}, u32[]{:S(2)}) %collective-permute-start.15) | collective-permute-done | bytes 1048608 | tf_op jit(solution)/shard_map/ppermute | solution.py:298
  134.4 0.3 collective-permute-start.11
  134.7 1.7 plan.1
  136.4 3.7 %bias.1.refs_5_ = f32[512,512]{1,0:T(8,128)} custom-call(s32[4]{0:T(128)} %get-tuple-element.19.info_ref, bf16[128,4,128]{2,1,0:T(4,128)(2,1)} %collective-permute-done.3.refs_0_, bf16[128,4,128]{2,1,0:T(4,128)(2,1)} %collective-permute-done.4.refs_1_, bf16[128,4,128]{2,1,0:T(4,128)(2,1)} %collective-permute-done.5.refs_2_, ...), custom_call_target="tpu_custom_call" | custom-call | tf_op jit(solution)/shard_map/bias/pallas_call | solution.py:134
  140.0 16.9 %collective-permute-done.13.refs_2_ = bf16[32,128,128]{2,1,0:T(8,128)(2,1)} collective-permute-done((bf16[32,128,128]{2,1,0:T(8,128)(2,1)}, bf16[32,128,128]{2,1,0:T(8,128)(2,1)}, u32[]{:S(2)}, u32[]{:S(2)}) %collective-permute-start.13) | collective-permute-done | bytes 1048608 | tf_op jit(solution)/shard_map/ppermute | solution.py:298
  157.2 17.8 %attend.8.refs_9_ = bf16[256,128,128]{2,1,0:T(8,128)(2,1)} custom-call(s32[4]{0:T(128)} %get-tuple-element.19.info_ref, bf16[32,128,128]{2,1,0:T(8,128)(2,1)} %get-tuple-element.32.refs_0_, bf16[32,128,128]{2,1,0:T(8,128)(2,1)} %collective-permute-done.19.refs_1_, bf16[32,128,128]{2,1,0:T(8,128)(2,1)} %collective-permute-done.20.refs_2_, ...), custom_call_target="tpu_custom_call" | custom-call | flops 4194304000 | bytes 6291456 | tf_op jit(solution)/shard_map/attend/pallas_call | solution.py:241
  175.0 4.4 %collective-permute-done.11.refs_2_ = bf16[32,128,128]{2,1,0:T(8,128)(2,1)} collective-permute-done((bf16[32,128,128]{2,1,0:T(8,128)(2,1)}, bf16[32,128,128]{2,1,0:T(8,128)(2,1)}, u32[]{:S(2)}, u32[]{:S(2)}) %collective-permute-start.11) | collective-permute-done | bytes 1048608 | tf_op jit(solution)/shard_map/ppermute | solution.py:298
  179.6 0.5 collective-permute-start.12
  180.1 31.7 %attend.9.refs_9_ = bf16[256,128,128]{2,1,0:T(8,128)(2,1)} custom-call(s32[4]{0:T(128)} %get-tuple-element.19.info_ref, bf16[64,128,128]{2,1,0:T(8,128)(2,1)} %get-tuple-element.31.refs_0_, bf16[224,128,128]{2,1,0:T(8,128)(2,1)} %collective-permute-done.refs_1_, ...), custom_call_target="tpu_custom_call", output_to_operand_aliasing={{}: (10, {})} | custom-call | flops 8388608000 | bytes 12582912 | tf_op jit(solution)/shard_map/attend/pallas_call | solution.py:241
  211.9 1.0 collective-permute-done.1.refs_2_
  212.9 0.5 collective-permute-start.2
  213.4 17.9 %attend.10.refs_9_ = bf16[256,128,128]{2,1,0:T(8,128)(2,1)} custom-call(s32[4]{0:T(128)} %get-tuple-element.19.info_ref, bf16[32,128,128]{2,1,0:T(8,128)(2,1)} %get-tuple-element.30.refs_0_, bf16[224,128,128]{2,1,0:T(8,128)(2,1)} %collective-permute-done.refs_1_, ...), custom_call_target="tpu_custom_call", output_to_operand_aliasing={{}: (10, {})} | custom-call | flops 4194304000 | bytes 6291456 | tf_op jit(solution)/shard_map/attend/pallas_call | solution.py:241
  231.3 18.1 %attend.11.refs_9_ = bf16[256,128,128]{2,1,0:T(8,128)(2,1)} custom-call(s32[4]{0:T(128)} %get-tuple-element.19.info_ref, bf16[32,128,128]{2,1,0:T(8,128)(2,1)} %get-tuple-element.29.refs_0_, bf16[224,128,128]{2,1,0:T(8,128)(2,1)} %collective-permute-done.refs_1_, ...), custom_call_target="tpu_custom_call", output_to_operand_aliasing={{}: (10, {})} | custom-call | flops 4194304000 | bytes 6291456 | tf_op jit(solution)/shard_map/attend/pallas_call | solution.py:241
  249.4 17.9 %attend.12.refs_9_ = bf16[256,128,128]{2,1,0:T(8,128)(2,1)} custom-call(s32[4]{0:T(128)} %get-tuple-element.19.info_ref, bf16[32,128,128]{2,1,0:T(8,128)(2,1)} %get-tuple-element.28.refs_0_, bf16[224,128,128]{2,1,0:T(8,128)(2,1)} %collective-permute-done.refs_1_, ...), custom_call_target="tpu_custom_call", output_to_operand_aliasing={{}: (10, {})} | custom-call | flops 4194304000 | bytes 6291456 | tf_op jit(solution)/shard_map/attend/pallas_call | solution.py:241
  267.2 17.9 %attend.13.refs_9_ = bf16[256,128,128]{2,1,0:T(8,128)(2,1)} custom-call(s32[4]{0:T(128)} %get-tuple-element.19.info_ref, bf16[32,128,128]{2,1,0:T(8,128)(2,1)} %get-tuple-element.27.refs_0_, bf16[224,128,128]{2,1,0:T(8,128)(2,1)} %collective-permute-done.refs_1_, ...), custom_call_target="tpu_custom_call", output_to_operand_aliasing={{}: (10, {})} | custom-call | flops 4194304000 | bytes 6291456 | tf_op jit(solution)/shard_map/attend/pallas_call | solution.py:241
  285.1 10.8 %attend.14.refs_9_ = bf16[256,128,128]{2,1,0:T(8,128)(2,1)} custom-call(s32[4]{0:T(128)} %get-tuple-element.19.info_ref, bf16[16,128,128]{2,1,0:T(8,128)(2,1)} %get-tuple-element.26.refs_0_, bf16[224,128,128]{2,1,0:T(8,128)(2,1)} %collective-permute-done.refs_1_, ...), custom_call_target="tpu_custom_call", output_to_operand_aliasing={{}: (10, {})} | custom-call | flops 2097152000 | bytes 3145728 | tf_op jit(solution)/shard_map/attend/pallas_call | solution.py:241
  295.9 10.5 %attend.15 = bf16[256,128,128]{2,1,0:T(8,128)(2,1)} custom-call(s32[4]{0:T(128)} %get-tuple-element.19.info_ref, bf16[16,128,128]{2,1,0:T(8,128)(2,1)} %get-tuple-element.20.refs_0_, bf16[224,128,128]{2,1,0:T(8,128)(2,1)} %collective-permute-done.refs_1_, bf16[16,128,128]{2,1,0:T(8,128)(2,1)} %collective-permute-done.1.refs_2_, ...), custom_call_target="tpu_custom_call", output_to_operand_aliasing={{}: (10, {})} | custom-call | flops 2097152000 | bytes 3145728 | tf_op jit(solution)/shard_map/attend/pallas_call | solution.py:241
  (27 shorter events, 1.5 us)
Async XLA Ops:
  16.9 162.8 %collective-permute-start = (bf16[224,128,128]{2,1,0:T(8,128)(2,1)}, bf16[224,128,128]{2,1,0:T(8,128)(2,1)}, u32[]{:S(2)}, u32[]{:S(2)}) collective-permute-start(bf16[224,128,128]{2,1,0:T(8,128)(2,1)} %get-tuple-element.21), channel_id=1, source_target_pairs={{0,1},{1,0},{2,3},{3,2},{4,5},{5,4},{6,7},{7,6}} | collective-permute-start | bytes 22020104 | tf_op jit(solution)/shard_map/ppermute | solution.py:300
  17.7 72.0 %collective-permute-start.17 = (bf16[64,128,128]{2,1,0:T(8,128)(2,1)}, bf16[64,128,128]{2,1,0:T(8,128)(2,1)}, u32[]{:S(2)}, u32[]{:S(2)}) collective-permute-start(bf16[64,128,128]{2,1,0:T(8,128)(2,1)} %get-tuple-element.31.refs_0_), channel_id=1, source_target_pairs={{0,2},{1,3},{2,0},{3,1},{4,6},{5,7},{6,4},{7,5}} | collective-permute-start | bytes 6291464 | tf_op jit(solution)/shard_map/ppermute | solution.py:298
  24.6 6.1 %collective-permute-start.3 = (bf16[128,4,128]{2,1,0:T(4,128)(2,1)S(1)}, bf16[128,4,128]{2,1,0:T(4,128)(2,1)}, u32[]{:S(2)}, u32[]{:S(2)}) collective-permute-start(bf16[128,4,128]{2,1,0:T(4,128)(2,1)S(1)} %get-tuple-element.36), channel_id=1, source_target_pairs={{0,0},{1,1},{2,4},{3,5},{4,2},{5,3},{6,6},{7,7}} | collective-permute-start | bytes 393224 | tf_op jit(solution)/shard_map/ppermute | solution.py:294
  26.0 44.6 %collective-permute-start.4 = (bf16[128,4,128]{2,1,0:T(4,128)(2,1)S(1)}, bf16[128,4,128]{2,1,0:T(4,128)(2,1)}, u32[]{:S(2)}, u32[]{:S(2)}) collective-permute-start(bf16[128,4,128]{2,1,0:T(4,128)(2,1)S(1)} %get-tuple-element.35), channel_id=1, source_target_pairs={{0,1},{1,0},{2,5},{3,4},{4,3},{5,2},{6,7},{7,6}} | collective-permute-start | bytes 393224 | tf_op jit(solution)/shard_map/ppermute | solution.py:294
  26.2 49.3 %collective-permute-start.5 = (bf16[128,4,128]{2,1,0:T(4,128)(2,1)S(1)}, bf16[128,4,128]{2,1,0:T(4,128)(2,1)}, u32[]{:S(2)}, u32[]{:S(2)}) collective-permute-start(bf16[128,4,128]{2,1,0:T(4,128)(2,1)S(1)} %get-tuple-element.34), channel_id=1, source_target_pairs={{0,4},{1,5},{2,0},{3,1},{4,6},{5,7},{6,2},{7,3}} | collective-permute-start | bytes 393224 | tf_op jit(solution)/shard_map/ppermute | solution.py:294
  30.7 47.1 %collective-permute-start.6 = (bf16[128,4,128]{2,1,0:T(4,128)(2,1)S(1)}, bf16[128,4,128]{2,1,0:T(4,128)(2,1)}, u32[]{:S(2)}, u32[]{:S(2)}) collective-permute-start(bf16[128,4,128]{2,1,0:T(4,128)(2,1)S(1)} %get-tuple-element.33), channel_id=1, source_target_pairs={{0,5},{1,4},{2,1},{3,0},{4,7},{5,6},{6,3},{7,2}} | collective-permute-start | bytes 393224 | tf_op jit(solution)/shard_map/ppermute | solution.py:294
  70.6 18.9 %collective-permute-start.7 = (bf16[16,128,128]{2,1,0:T(8,128)(2,1)}, bf16[16,128,128]{2,1,0:T(8,128)(2,1)}, u32[]{:S(2)}, u32[]{:S(2)}) collective-permute-start(bf16[16,128,128]{2,1,0:T(8,128)(2,1)} %get-tuple-element.26.refs_0_), channel_id=1, source_target_pairs={{0,2},{1,3},{2,0},{3,1},{4,6},{5,7},{6,4},{7,5}} | collective-permute-start | bytes 1572872 | tf_op jit(solution)/shard_map/ppermute | solution.py:298
  75.4 36.5 %collective-permute-start.20 = (bf16[32,128,128]{2,1,0:T(8,128)(2,1)}, bf16[32,128,128]{2,1,0:T(8,128)(2,1)}, u32[]{:S(2)}, u32[]{:S(2)}) collective-permute-start(bf16[32,128,128]{2,1,0:T(8,128)(2,1)} %get-tuple-element.32.refs_0_), channel_id=1, source_target_pairs={{0,2},{1,3},{2,0},{3,1},{4,6},{5,7},{6,4},{7,5}} | collective-permute-start | bytes 3145736 | tf_op jit(solution)/shard_map/ppermute | solution.py:298
  77.8 34.4 %collective-permute-start.19 = (bf16[32,128,128]{2,1,0:T(8,128)(2,1)}, bf16[32,128,128]{2,1,0:T(8,128)(2,1)}, u32[]{:S(2)}, u32[]{:S(2)}) collective-permute-start(bf16[32,128,128]{2,1,0:T(8,128)(2,1)} %get-tuple-element.32.refs_0_), channel_id=1, source_target_pairs={{0,1},{1,0},{2,3},{3,2},{4,5},{5,4},{6,7},{7,6}} | collective-permute-start | bytes 3145736 | tf_op jit(solution)/shard_map/ppermute | solution.py:300
  89.5 44.9 %collective-permute-start.15 = (bf16[32,128,128]{2,1,0:T(8,128)(2,1)}, bf16[32,128,128]{2,1,0:T(8,128)(2,1)}, u32[]{:S(2)}, u32[]{:S(2)}) collective-permute-start(bf16[32,128,128]{2,1,0:T(8,128)(2,1)} %get-tuple-element.30.refs_0_), channel_id=1, source_target_pairs={{0,2},{1,3},{2,0},{3,1},{4,6},{5,7},{6,4},{7,5}} | collective-permute-start | bytes 3145736 | tf_op jit(solution)/shard_map/ppermute | solution.py:298
  89.7 89.9 %collective-permute-start.18 = (bf16[64,128,128]{2,1,0:T(8,128)(2,1)}, bf16[64,128,128]{2,1,0:T(8,128)(2,1)}, u32[]{:S(2)}, u32[]{:S(2)}) collective-permute-start(bf16[64,128,128]{2,1,0:T(8,128)(2,1)} %collective-permute-done.17.refs_2_), channel_id=1, source_target_pairs={{0,1},{1,0},{2,3},{3,2},{4,5},{5,4},{6,7},{7,6}} | collective-permute-start | bytes 6291464 | tf_op jit(solution)/shard_map/ppermute | solution.py:303
  112.0 44.9 %collective-permute-start.13 = (bf16[32,128,128]{2,1,0:T(8,128)(2,1)}, bf16[32,128,128]{2,1,0:T(8,128)(2,1)}, u32[]{:S(2)}, u32[]{:S(2)}) collective-permute-start(bf16[32,128,128]{2,1,0:T(8,128)(2,1)} %get-tuple-element.29.refs_0_), channel_id=1, source_target_pairs={{0,2},{1,3},{2,0},{3,1},{4,6},{5,7},{6,4},{7,5}} | collective-permute-start | bytes 3145736 | tf_op jit(solution)/shard_map/ppermute | solution.py:298
  112.2 44.9 %collective-permute-start.21 = (bf16[32,128,128]{2,1,0:T(8,128)(2,1)}, bf16[32,128,128]{2,1,0:T(8,128)(2,1)}, u32[]{:S(2)}, u32[]{:S(2)}) collective-permute-start(bf16[32,128,128]{2,1,0:T(8,128)(2,1)} %collective-permute-done.20.refs_2_), channel_id=1, source_target_pairs={{0,1},{1,0},{2,3},{3,2},{4,5},{5,4},{6,7},{7,6}} | collective-permute-start | bytes 3145736 | tf_op jit(solution)/shard_map/ppermute | solution.py:303
  134.4 44.9 %collective-permute-start.11 = (bf16[32,128,128]{2,1,0:T(8,128)(2,1)}, bf16[32,128,128]{2,1,0:T(8,128)(2,1)}, u32[]{:S(2)}, u32[]{:S(2)}) collective-permute-start(bf16[32,128,128]{2,1,0:T(8,128)(2,1)} %get-tuple-element.28.refs_0_), channel_id=1, source_target_pairs={{0,2},{1,3},{2,0},{3,1},{4,6},{5,7},{6,4},{7,5}} | collective-permute-start | bytes 3145736 | tf_op jit(solution)/shard_map/ppermute | solution.py:298
  156.9 56.0 %collective-permute-start.9 = (bf16[32,128,128]{2,1,0:T(8,128)(2,1)}, bf16[32,128,128]{2,1,0:T(8,128)(2,1)}, u32[]{:S(2)}, u32[]{:S(2)}) collective-permute-start(bf16[32,128,128]{2,1,0:T(8,128)(2,1)} %get-tuple-element.27.refs_0_), channel_id=1, source_target_pairs={{0,2},{1,3},{2,0},{3,1},{4,6},{5,7},{6,4},{7,5}} | collective-permute-start | bytes 3145736 | tf_op jit(solution)/shard_map/ppermute | solution.py:298
  157.2 56.2 %collective-permute-start.16 = (bf16[32,128,128]{2,1,0:T(8,128)(2,1)}, bf16[32,128,128]{2,1,0:T(8,128)(2,1)}, u32[]{:S(2)}, u32[]{:S(2)}) collective-permute-start(bf16[32,128,128]{2,1,0:T(8,128)(2,1)} %collective-permute-done.15.refs_2_), channel_id=1, source_target_pairs={{0,1},{1,0},{2,3},{3,2},{4,5},{5,4},{6,7},{7,6}} | collective-permute-start | bytes 3145736 | tf_op jit(solution)/shard_map/ppermute | solution.py:303
  179.4 33.5 %collective-permute-start.1 = (bf16[16,128,128]{2,1,0:T(8,128)(2,1)}, bf16[16,128,128]{2,1,0:T(8,128)(2,1)}, u32[]{:S(2)}, u32[]{:S(2)}) collective-permute-start(bf16[16,128,128]{2,1,0:T(8,128)(2,1)} %get-tuple-element.20.refs_0_), channel_id=1, source_target_pairs={{0,2},{1,3},{2,0},{3,1},{4,6},{5,7},{6,4},{7,5}} | collective-permute-start | bytes 1572872 | tf_op jit(solution)/shard_map/ppermute | solution.py:298
  179.6 51.6 %collective-permute-start.14 = (bf16[32,128,128]{2,1,0:T(8,128)(2,1)}, bf16[32,128,128]{2,1,0:T(8,128)(2,1)}, u32[]{:S(2)}, u32[]{:S(2)}) collective-permute-start(bf16[32,128,128]{2,1,0:T(8,128)(2,1)} %collective-permute-done.13.refs_2_), channel_id=1, source_target_pairs={{0,1},{1,0},{2,3},{3,2},{4,5},{5,4},{6,7},{7,6}} | collective-permute-start | bytes 3145736 | tf_op jit(solution)/shard_map/ppermute | solution.py:303
  179.6 69.7 %collective-permute-start.12 = (bf16[32,128,128]{2,1,0:T(8,128)(2,1)}, bf16[32,128,128]{2,1,0:T(8,128)(2,1)}, u32[]{:S(2)}, u32[]{:S(2)}) collective-permute-start(bf16[32,128,128]{2,1,0:T(8,128)(2,1)} %collective-permute-done.11.refs_2_), channel_id=1, source_target_pairs={{0,1},{1,0},{2,3},{3,2},{4,5},{5,4},{6,7},{7,6}} | collective-permute-start | bytes 3145736 | tf_op jit(solution)/shard_map/ppermute | solution.py:303
  212.9 72.2 %collective-permute-start.8 = (bf16[16,128,128]{2,1,0:T(8,128)(2,1)}, bf16[16,128,128]{2,1,0:T(8,128)(2,1)}, u32[]{:S(2)}, u32[]{:S(2)}) collective-permute-start(bf16[16,128,128]{2,1,0:T(8,128)(2,1)} %collective-permute-done.7.refs_2_), channel_id=1, source_target_pairs={{0,1},{1,0},{2,3},{3,2},{4,5},{5,4},{6,7},{7,6}} | collective-permute-start | bytes 1572872 | tf_op jit(solution)/shard_map/ppermute | solution.py:303
  212.9 83.1 %collective-permute-start.2 = (bf16[16,128,128]{2,1,0:T(8,128)(2,1)}, bf16[16,128,128]{2,1,0:T(8,128)(2,1)}, u32[]{:S(2)}, u32[]{:S(2)}) collective-permute-start(bf16[16,128,128]{2,1,0:T(8,128)(2,1)} %collective-permute-done.1.refs_2_), channel_id=1, source_target_pairs={{0,1},{1,0},{2,3},{3,2},{4,5},{5,4},{6,7},{7,6}} | collective-permute-start | bytes 1572872 | tf_op jit(solution)/shard_map/ppermute | solution.py:303
  213.4 53.9 %collective-permute-start.10 = (bf16[32,128,128]{2,1,0:T(8,128)(2,1)}, bf16[32,128,128]{2,1,0:T(8,128)(2,1)}, u32[]{:S(2)}, u32[]{:S(2)}) collective-permute-start(bf16[32,128,128]{2,1,0:T(8,128)(2,1)} %collective-permute-done.9.refs_2_), channel_id=1, source_target_pairs={{0,1},{1,0},{2,3},{3,2},{4,5},{5,4},{6,7},{7,6}} | collective-permute-start | bytes 3145736 | tf_op jit(solution)/shard_map/ppermute | solution.py:303
where the time goes:
time: 307 us; the launch traced here: 306 us
  Pallas kernels  167 us (54%)
  waiting for transfers between devices  81.3 us (26%)
  starting transfers between devices  55.9 us (18%)
    pallas_call x8, Pallas kernels, attend(): pl.pallas_call(functools.partial(attend_kernel, heads, sizes), grid_spec=...  143 us
    ppermute x8, waiting for transfers between devices, inner(): far.append(lax.ppermute(a, 'col', x_pairs))  78 us
    ppermute x4, starting transfers between devices, inner(): parts.append(lax.ppermute(half, ('row', 'col'), bias_pairs(m)))  45.9 us
    pallas_call x2, Pallas kernels, normalize(): pl.pallas_call(functools.partial(norm_kernel, places), grid=(rows // step...  18.6 us
    ppermute x8, starting transfers between devices, inner(): far.append(lax.ppermute(a, 'col', x_pairs))  7.84 us
  transfers between devices with their start and end apart: 22, of which 8 were waited for; matrix products, arithmetic and copies ran while one was open for 0% of the time, Pallas kernels for 46%

commit v1 on v0

--- a/solution.py
+++ b/solution.py
@@ -9,10 +9,12 @@
 
 
 LN_EPS = 1e-5
-CHUNKS = (32, 64, 32, 32, 32, 32, 16, 16)
-NORM_ROWS = 32
+CHUNKS = (16, 48, 48, 48, 32, 32, 32)
+NORM_ROWS = 16
 ATTEND_ROWS = 16
-GROUP = 8
+GROUP = 16
+ATTEND_VMEM = (57 * 1024 * 1024, 40 * 1024 * 1024)
+SMALL_VMEM = pltpu.CompilerParams(vmem_limit_bytes=24 * 1024 * 1024)
 SCORE_BOUND = 1e8
 VALUE_BOUND = 1e20
 SUM_RANGE = (1e-10, 1e15)
@@ -37,7 +39,7 @@
     q = jnp.dot(reach, jnp.abs(wq_ref[...].astype(f32)), preferred_element_type=f32) * dim ** -0.5
     k = jnp.dot(reach, jnp.abs(wk_ref[...].astype(f32)), preferred_element_type=f32)
     v = jnp.dot(reach, jnp.abs(wv_ref[...].astype(f32)), preferred_element_type=f32)
-    b = jnp.dot(reach, jnp.abs(wb_ref[...].astype(f32)), preferred_element_type=f32)
+    b = reach[:1] * jnp.sum(jnp.abs(wb_ref[...].astype(f32)), axis=0, keepdims=True)
     s_bound = (jnp.sum(q * k) + jnp.sum(b)) * 1.1
     v_bound = jnp.max(v) * 1.1
     length = jnp.sum(mask_ref[...].astype(f32)).astype(jnp.int32)
@@ -55,7 +57,7 @@
         in_specs=[whole(x.shape) for x in args],
         out_specs=[pl.BlockSpec(memory_space=pltpu.SMEM), whole((chan, 2 * chan)), whole((chan, 2 * chan))],
         out_shape=[jax.ShapeDtypeStruct((4,), jnp.int32)] + [jax.ShapeDtypeStruct((chan, 2 * chan), bf16)] * 2,
-        compiler_params=VMEM_LIMIT,
+        compiler_params=SMALL_VMEM,
         name="plan",
     )(*args)
 
@@ -63,7 +65,6 @@
 def norm_kernel(places, z_ref, gamma_ref, beta_ref, wb_ref, *out_refs):
     rows, cols, chan = z_ref.shape
     b_ref = out_refs[len(places)]
-    heads = b_ref.shape[1]
     z = z_ref[...].reshape(rows * cols, chan)
     ones = jnp.full((chan, chan), 1.0 / chan, bf16)
     centered = z.astype(f32) - dot(z, ones, NN)
@@ -77,15 +78,14 @@
             out_ref[...] = blocks[offset:offset + out_ref.shape[0]]
     for out_ref in out_refs[len(places) + 1:]:
         out_ref[...] = blocks
-    wb = jnp.concatenate([wb_ref[...].astype(f32), jnp.zeros((chan, chan - heads), f32)], axis=1).T[:8].astype(bf16)
-    b = dot(wb, a, NT)
+    b = dot(wb_ref[...], a, NT)
     for r in range(rows):
-        b_ref[r] = b[:heads, r * cols:(r + 1) * cols].astype(bf16)
-
-
-def normalize(z, gamma, beta, w_b, start, chunks, joined):
+        b_ref[r] = b[:, r * cols:(r + 1) * cols].astype(bf16)
+
+
+def normalize(z, gamma, beta, wb_t, start, chunks, joined):
     cols, chan = z.shape[1:]
-    heads = w_b.shape[1]
+    heads = wb_t.shape[0]
     step = NORM_ROWS
     first = start // step
     rows = sum(chunks)
@@ -105,14 +105,14 @@
         grid=(rows // step,),
         in_specs=[
             pl.BlockSpec((step, cols, chan), lambda i: (first + i, 0, 0)),
-            whole((1, chan)), whole((1, chan)), whole(w_b.shape),
+            whole((1, chan)), whole((1, chan)), whole(wb_t.shape),
         ],
         out_specs=specs,
         out_shape=shapes,
         compiler_params=VMEM_LIMIT,
         cost_estimate=pl.CostEstimate(flops=rows * cols * chan * 300, bytes_accessed=rows * cols * chan * 4, transcendentals=0),
         name="norm",
-    )(z, gamma, beta, w_b)
+    )(z, gamma, beta, wb_t)
 
 
 def bias_kernel(info_ref, *refs):
@@ -138,7 +138,7 @@
             in_specs=[whole(p.shape) for p in parts], out_specs=whole(shape),
         ),
         out_shape=jax.ShapeDtypeStruct(shape, f32),
-        compiler_params=VMEM_LIMIT,
+        compiler_params=SMALL_VMEM,
         name="bias",
     )(info, *parts)
 
@@ -254,7 +254,7 @@
         ),
         out_shape=jax.ShapeDtypeStruct(z.shape, z.dtype),
         input_output_aliases=alias,
-        compiler_params=VMEM_LIMIT,
+        compiler_params=pltpu.CompilerParams(vmem_limit_bytes=ATTEND_VMEM[prev is not None]),
         cost_estimate=pl.CostEstimate(flops=rows * cols * chan * 8000, bytes_accessed=rows * cols * chan * 12, transcendentals=0),
         name="attend",
     )(*args)
@@ -279,13 +279,13 @@
         heads = w_b.shape[1]
         sizes = (3 * cols, 7 * cols // 2, 4 * cols)
         col_idx = lax.axis_index('col')
-        gamma, beta = ln_gamma.reshape(1, chan), ln_beta.reshape(1, chan)
+        gamma, beta, wb_t = ln_gamma.reshape(1, chan), ln_beta.reshape(1, chan), w_b.T
         starts = [sum(CHUNKS[:i]) for i in range(len(CHUNKS))]
-        head = normalize(z, gamma, beta, w_b, 0, CHUNKS[:1], False)
-        *tail, tail_bias, rest = normalize(z, gamma, beta, w_b, CHUNKS[0], CHUNKS[1:], True)
+        head = normalize(z, gamma, beta, wb_t, 0, CHUNKS[:1], False)
+        *tail, tail_bias, rest = normalize(z, gamma, beta, wb_t, CHUNKS[0], CHUNKS[1:], True)
         own = [head[0]] + tail
         halves = jnp.concatenate([head[1], tail_bias], axis=0).reshape(2, row_len // 2, heads, cols)
-        info, w_kv, w_qg = make_plan(heads, sizes, res_mask.reshape(4, cols), gamma, beta, w_q, w_k, w_v, w_b, w_g)
+        info, w_kv, w_qg = make_plan(heads, sizes, res_mask.reshape(4, cols), gamma, beta, w_q, w_k, w_v, wb_t, w_g)
         weights = (w_kv, w_qg, w_o)
 
         parts = []

time: 307 us -> 338 us (1.10)
  waiting for transfers between devices: 81.3 us -> 160 us
  starting transfers between devices: 55.9 us -> 19.1 us
  Pallas kernels: 167 us -> 148 us
  local copies, waits for them, and re-layouts: 1.59 us -> 8.8 us
    ppermute x8 -> x7, waiting for transfers between devices: 78 us -> 145 us  [inner(): far.append(lax.ppermute(a, 'col', x_pairs))]
    ppermute x4, starting transfers between devices: 45.9 us -> 10.4 us  [inner(): parts.append(lax.ppermute(half, ('row', 'col'), bias_pairs(m)))]
    pallas_call x8 -> x7, Pallas kernels: 143 us -> 126 us  [attend(): pl.pallas_call(functools.partial(attend_kernel, heads, sizes), grid_spec=...]
    ppermute x4, waiting for transfers between devices: 3.19 us -> 15.4 us  [inner(): parts.append(lax.ppermute(half, ('row', 'col'), bias_pairs(m)))]
    unnamed x1 -> x56, local copies, waits for them, and re-layouts: 1.39 us -> 8.61 us
    ppermute x8 -> x7, starting transfers between devices: 7.84 us -> 6.92 us  [inner(): far.append(lax.ppermute(a, 'col', x_pairs))]
  transfers between devices with their start and end apart: 22 -> 20, of which waited for: 8 -> 6; matrix products, arithmetic and copies ran while one was open for 0% -> 0% of each run, Pallas kernels for 46% -> 34%
where the time goes in v1:
time: 338 us; the launch traced here: 337 us
  waiting for transfers between devices  160 us (47%)
  Pallas kernels  148 us (44%)
  starting transfers between devices  19.1 us (6%)
  local copies, waits for them, and re-layouts  8.8 us (3%)
    ppermute x7, waiting for transfers between devices, inner(): far.append(lax.ppermute(a, 'col', x_pairs))  145 us
    pallas_call x7, Pallas kernels, attend(): pl.pallas_call(functools.partial(attend_kernel, heads, sizes), grid_spec=...  126 us
    pallas_call x2, Pallas kernels, normalize(): pl.pallas_call(functools.partial(norm_kernel, places), grid=(rows // step...  20.1 us
    ppermute x4, waiting for transfers between devices, inner(): parts.append(lax.ppermute(half, ('row', 'col'), bias_pairs(m)))  15.4 us
    ppermute x4, starting transfers between devices, inner(): parts.append(lax.ppermute(half, ('row', 'col'), bias_pairs(m)))  10.4 us
    unnamed x56, local copies, waits for them, and re-layouts  8.61 us
    ppermute x7, starting transfers between devices, inner(): far.append(lax.ppermute(a, 'col', x_pairs))  6.92 us
  transfers between devices with their start and end apart: 20, of which 6 were waited for; matrix products, arithmetic and copies ran while one was open for 0% of the time, Pallas kernels for 34%

profile of v1, /device:TPU:0, one launch (start us, length us, event | category | flops | bytes accessed | tf_op | source)
XLA Modules:
  0.0 337.4 jit_solution(10239939505829556870)
XLA Ops:
  0.0 17.8 %norm.2 = (bf16[48,128,128]{2,1,0:T(8,128)(2,1)}, bf16[48,128,128]{2,1,0:T(8,128)(2,1)}, bf16[48,128,128]{2,1,0:T(8,128)(2,1)}, bf16[32,128,128]{2,1,0:T(8,128)(...) custom-call(bf16[256,128,128]{2,1,0:T(8,128)(2,1)} %refs_4_.13, ...), custom_call_target="tpu_custom_call" | custom-call | flops 1179648000 | bytes 15728640 | tf_op jit(solution)/shard_map/norm/pallas_call | solution.py:103
  17.8 0.9 collective-permute-start
  18.7 2.4 norm.3
  21.1 1.1 pad_maximum_fusion
  22.4 0.7 collective-permute-start.3
  23.1 6.5 %collective-permute-start.5 = (bf16[128,4,128]{2,1,0:T(4,128)(2,1)S(1)}, bf16[128,4,128]{2,1,0:T(4,128)(2,1)S(1)}, u32[]{:S(2)}, u32[]{:S(2)}) collective-permute-start(bf16[128,4,128]{2,1,0:T(4,128)(2,1)S(1)} %get-tuple-element.32), channel_id=1, source_target_pairs={{0,4},{1,5},{2,0},{3,1},{4,6},{5,7},{6,2},{7,3}} | collective-permute-start | bytes 393224 | tf_op jit(solution)/shard_map/ppermute | solution.py:294
  29.6 3.2 collective-permute-start.6
  32.8 3.2 collective-permute-start.15
  36.0 2.3 collective-permute-done.5.refs_2_
  38.3 13.1 %collective-permute-done.6.refs_3_ = bf16[128,4,128]{2,1,0:T(4,128)(2,1)S(1)} collective-permute-done((bf16[128,4,128]{2,1,0:T(4,128)(2,1)S(1)}, bf16[128,4,128]{2,1,0:T(4,128)(2,1)S(1)}, u32[]{:S(2)}, u32[]{:S(2)}) %collective-permute-start.6) | collective-permute-done | bytes 131104 | tf_op jit(solution)/shard_map/ppermute | solution.py:294
  52.2 1.7 collective-permute-start.13
  53.9 1.5 collective-permute-start.7
  55.4 53.1 %collective-permute-done.9.refs_2_ = bf16[32,128,128]{2,1,0:T(8,128)(2,1)S(1)} collective-permute-done((bf16[32,128,128]{2,1,0:T(8,128)(2,1)}, bf16[32,128,128]{2,1,0:T(8,128)(2,1)S(1)}, u32[]{:S(2)}, u32[]{:S(2)}) %collective-permute-start.9) | collective-permute-done | bytes 1048608 | tf_op jit(solution)/shard_map/ppermute | solution.py:298
  108.5 56.2 %collective-permute-done.7.refs_2_ = bf16[32,128,128]{2,1,0:T(8,128)(2,1)S(1)} collective-permute-done((bf16[32,128,128]{2,1,0:T(8,128)(2,1)}, bf16[32,128,128]{2,1,0:T(8,128)(2,1)S(1)}, u32[]{:S(2)}, u32[]{:S(2)}) %collective-permute-start.7) | collective-permute-done | bytes 1048608 | tf_op jit(solution)/shard_map/ppermute | solution.py:298
  164.7 33.8 %collective-permute-done.11.refs_2_ = bf16[48,128,128]{2,1,0:T(8,128)(2,1)} collective-permute-done((bf16[48,128,128]{2,1,0:T(8,128)(2,1)}, bf16[48,128,128]{2,1,0:T(8,128)(2,1)}, u32[]{:S(2)}, u32[]{:S(2)}) %collective-permute-start.11) | collective-permute-done | bytes 1572896 | tf_op jit(solution)/shard_map/ppermute | solution.py:298
  198.5 0.8 copy-done.17
  199.3 0.8 copy-done.18
  200.0 0.8 copy-done.19
  200.8 0.8 copy-done.20
  201.5 0.7 copy-done.21
  203.5 0.7 copy-done.24
  204.2 0.9 plan.1
  206.3 1.4 bias.1.refs_5_
  207.7 1.0 copy-done
  208.8 10.2 %attend.7.refs_9_ = bf16[256,128,128]{2,1,0:T(8,128)(2,1)} custom-call(s32[4]{0:T(128)} %copy-done.15, bf16[16,128,128]{2,1,0:T(8,128)(2,1)} %get-tuple-element.30.refs_0_, bf16[16,128,128]{2,1,0:T(8,128)(2,1)} %copy-done.26, bf16[16,128,128]{2,1,0:T(8,128)(2,1)} %copy-done.25, bf16[16,128,128]{2,1,0:T(8,128)(2,1)} %copy-done.27, ...), custom_call_target="tpu_custom_call" | custom-call | flops 2097152000 | bytes 3145728 | tf_op jit(solution)/shard_map/attend/pallas_call | solution.py:241
  219.0 1.5 collective-permute-done.1.refs_2_
  221.7 22.7 %attend.8.refs_9_ = bf16[256,128,128]{2,1,0:T(8,128)(2,1)} custom-call(s32[4]{0:T(128)S(1)} %copy-done.16, bf16[48,128,128]{2,1,0:T(8,128)(2,1)S(1)} %copy-done.9, bf16[240,128,128]{2,1,0:T(8,128)(2,1)} %collective-permute-done.refs_1_, bf16[48,128,128]{2,1,0:T(8,128)(2,1)S(1)} %collective-permute-done.15.refs_2_, ...), custom_call_target="tpu_custom_call", output_to_operand_aliasing={{}: (10, {})} | custom-call | flops 6291456000 | bytes 9437184 | tf_op jit(solution)/shard_map/attend/pallas_call | solution.py:241
  244.4 22.6 %attend.9.refs_9_ = bf16[256,128,128]{2,1,0:T(8,128)(2,1)} custom-call(s32[4]{0:T(128)S(1)} %copy-done.16, bf16[48,128,128]{2,1,0:T(8,128)(2,1)S(1)} %copy-done.8, bf16[240,128,128]{2,1,0:T(8,128)(2,1)} %collective-permute-done.refs_1_, bf16[48,128,128]{2,1,0:T(8,128)(2,1)S(1)} %collective-permute-done.13.refs_2_, ...), custom_call_target="tpu_custom_call", output_to_operand_aliasing={{}: (10, {})} | custom-call | flops 6291456000 | bytes 9437184 | tf_op jit(solution)/shard_map/attend/pallas_call | solution.py:241
  267.0 22.7 %attend.10.refs_9_ = bf16[256,128,128]{2,1,0:T(8,128)(2,1)} custom-call(s32[4]{0:T(128)S(1)} %copy-done.16, bf16[48,128,128]{2,1,0:T(8,128)(2,1)S(1)} %copy-done.7, bf16[240,128,128]{2,1,0:T(8,128)(2,1)} %collective-permute-done.refs_1_, bf16[48,128,128]{2,1,0:T(8,128)(2,1)} %collective-permute-done.11.refs_2_, ...), custom_call_target="tpu_custom_call", output_to_operand_aliasing={{}: (10, {})} | custom-call | flops 6291456000 | bytes 9437184 | tf_op jit(solution)/shard_map/attend/pallas_call | solution.py:241
  289.7 16.0 %attend.11.refs_9_ = bf16[256,128,128]{2,1,0:T(8,128)(2,1)} custom-call(s32[4]{0:T(128)S(1)} %copy-done.16, bf16[32,128,128]{2,1,0:T(8,128)(2,1)S(1)} %copy-done.12, bf16[240,128,128]{2,1,0:T(8,128)(2,1)} %collective-permute-done.refs_1_, bf16[32,128,128]{2,1,0:T(8,128)(2,1)S(1)} %collective-permute-done.9.refs_2_, ...), custom_call_target="tpu_custom_call", output_to_operand_aliasing={{}: (10, {})} | custom-call | flops 4194304000 | bytes 6291456 | tf_op jit(solution)/shard_map/attend/pallas_call | solution.py:241
  305.7 15.7 %attend.12.refs_9_ = bf16[256,128,128]{2,1,0:T(8,128)(2,1)} custom-call(s32[4]{0:T(128)S(1)} %copy-done.16, bf16[32,128,128]{2,1,0:T(8,128)(2,1)S(1)} %copy-done.11, bf16[240,128,128]{2,1,0:T(8,128)(2,1)} %collective-permute-done.refs_1_, bf16[32,128,128]{2,1,0:T(8,128)(2,1)S(1)} %copy-done.14, ...), custom_call_target="tpu_custom_call", output_to_operand_aliasing={{}: (10, {})} | custom-call | flops 4194304000 | bytes 6291456 | tf_op jit(solution)/shard_map/attend/pallas_call | solution.py:241
  321.4 15.9 %attend.13 = bf16[256,128,128]{2,1,0:T(8,128)(2,1)} custom-call(s32[4]{0:T(128)S(1)} %copy-done.16, bf16[32,128,128]{2,1,0:T(8,128)(2,1)S(1)} %copy-done.10, bf16[240,128,128]{2,1,0:T(8,128)(2,1)} %collective-permute-done.refs_1_, bf16[32,128,128]{2,1,0:T(8,128)(2,1)} %collective-permute-done.1.refs_2_, ...), custom_call_target="tpu_custom_call", output_to_operand_aliasing={{}: (10, {})} | custom-call | flops 4194304000 | bytes 6291456 | tf_op jit(solution)/shard_map/attend/pallas_call | solution.py:241
  (77 shorter events, 4.9 us)
Async XLA Ops:
  17.8 203.2 %collective-permute-start = (bf16[240,128,128]{2,1,0:T(8,128)(2,1)}, bf16[240,128,128]{2,1,0:T(8,128)(2,1)}, u32[]{:S(2)}, u32[]{:S(2)}) collective-permute-start(bf16[240,128,128]{2,1,0:T(8,128)(2,1)} %get-tuple-element.20), channel_id=1, source_target_pairs={{0,1},{1,0},{2,3},{3,2},{4,5},{5,4},{6,7},{7,6}} | collective-permute-start | bytes 23592968 | tf_op jit(solution)/shard_map/ppermute | solution.py:300
  22.4 7.2 %collective-permute-start.3 = (bf16[128,4,128]{2,1,0:T(4,128)(2,1)S(1)}, bf16[128,4,128]{2,1,0:T(4,128)(2,1)S(1)}, u32[]{:S(2)}, u32[]{:S(2)}) collective-permute-start(bf16[128,4,128]{2,1,0:T(4,128)(2,1)S(1)} %get-tuple-element.34), channel_id=1, source_target_pairs={{0,0},{1,1},{2,4},{3,5},{4,2},{5,3},{6,6},{7,7}} | collective-permute-start | bytes 393224 | tf_op jit(solution)/shard_map/ppermute | solution.py:294
  23.1 9.8 %collective-permute-start.4 = (bf16[128,4,128]{2,1,0:T(4,128)(2,1)S(1)}, bf16[128,4,128]{2,1,0:T(4,128)(2,1)S(1)}, u32[]{:S(2)}, u32[]{:S(2)}) collective-permute-start(bf16[128,4,128]{2,1,0:T(4,128)(2,1)S(1)} %get-tuple-element.33), channel_id=1, source_target_pairs={{0,1},{1,0},{2,5},{3,4},{4,3},{5,2},{6,7},{7,6}} | collective-permute-start | bytes 393224 | tf_op jit(solution)/shard_map/ppermute | solution.py:294
  23.1 15.2 %collective-permute-start.5 = (bf16[128,4,128]{2,1,0:T(4,128)(2,1)S(1)}, bf16[128,4,128]{2,1,0:T(4,128)(2,1)S(1)}, u32[]{:S(2)}, u32[]{:S(2)}) collective-permute-start(bf16[128,4,128]{2,1,0:T(4,128)(2,1)S(1)} %get-tuple-element.32), channel_id=1, source_target_pairs={{0,4},{1,5},{2,0},{3,1},{4,6},{5,7},{6,2},{7,3}} | collective-permute-start | bytes 393224 | tf_op jit(solution)/shard_map/ppermute | solution.py:294
  29.6 22.3 %collective-permute-start.18 = (bf16[16,128,128]{2,1,0:T(8,128)(2,1)}, bf16[16,128,128]{2,1,0:T(8,128)(2,1)S(1)}, u32[]{:S(2)}, u32[]{:S(2)}) collective-permute-start(bf16[16,128,128]{2,1,0:T(8,128)(2,1)} %get-tuple-element.30.refs_0_), channel_id=1, source_target_pairs={{0,2},{1,3},{2,0},{3,1},{4,6},{5,7},{6,4},{7,5}} | collective-permute-start | bytes 1572872 | tf_op jit(solution)/shard_map/ppermute | solution.py:298
  29.6 21.8 %collective-permute-start.6 = (bf16[128,4,128]{2,1,0:T(4,128)(2,1)S(1)}, bf16[128,4,128]{2,1,0:T(4,128)(2,1)S(1)}, u32[]{:S(2)}, u32[]{:S(2)}) collective-permute-start(bf16[128,4,128]{2,1,0:T(4,128)(2,1)S(1)} %get-tuple-element.31), channel_id=1, source_target_pairs={{0,5},{1,4},{2,1},{3,0},{4,7},{5,6},{6,3},{7,2}} | collective-permute-start | bytes 393224 | tf_op jit(solution)/shard_map/ppermute | solution.py:294
  32.8 75.7 %collective-permute-start.15 = (bf16[48,128,128]{2,1,0:T(8,128)(2,1)}, bf16[48,128,128]{2,1,0:T(8,128)(2,1)S(1)}, u32[]{:S(2)}, u32[]{:S(2)}) collective-permute-start(bf16[48,128,128]{2,1,0:T(8,128)(2,1)} %get-tuple-element.29.refs_0_), channel_id=1, source_target_pairs={{0,2},{1,3},{2,0},{3,1},{4,6},{5,7},{6,4},{7,5}} | collective-permute-start | bytes 4718600 | tf_op jit(solution)/shard_map/ppermute | solution.py:298
  38.3 13.9 %collective-permute-start.17 = (bf16[16,128,128]{2,1,0:T(8,128)(2,1)}, bf16[16,128,128]{2,1,0:T(8,128)(2,1)S(1)}, u32[]{:S(2)}, u32[]{:S(2)}) collective-permute-start(bf16[16,128,128]{2,1,0:T(8,128)(2,1)} %get-tuple-element.30.refs_0_), channel_id=1, source_target_pairs={{0,1},{1,0},{2,3},{3,2},{4,5},{5,4},{6,7},{7,6}} | collective-permute-start | bytes 1572872 | tf_op jit(solution)/shard_map/ppermute | solution.py:300
  51.4 57.1 %collective-permute-start.9 = (bf16[32,128,128]{2,1,0:T(8,128)(2,1)}, bf16[32,128,128]{2,1,0:T(8,128)(2,1)S(1)}, u32[]{:S(2)}, u32[]{:S(2)}) collective-permute-start(bf16[32,128,128]{2,1,0:T(8,128)(2,1)} %get-tuple-element.26.refs_0_), channel_id=1, source_target_pairs={{0,2},{1,3},{2,0},{3,1},{4,6},{5,7},{6,4},{7,5}} | collective-permute-start | bytes 3145736 | tf_op jit(solution)/shard_map/ppermute | solution.py:298
  51.9 2.0 collective-permute-start.19
  52.2 112.5 %collective-permute-start.13 = (bf16[48,128,128]{2,1,0:T(8,128)(2,1)}, bf16[48,128,128]{2,1,0:T(8,128)(2,1)S(1)}, u32[]{:S(2)}, u32[]{:S(2)}) collective-permute-start(bf16[48,128,128]{2,1,0:T(8,128)(2,1)} %get-tuple-element.28.refs_0_), channel_id=1, source_target_pairs={{0,2},{1,3},{2,0},{3,1},{4,6},{5,7},{6,4},{7,5}} | collective-permute-start | bytes 4718600 | tf_op jit(solution)/shard_map/ppermute | solution.py:298
  53.9 154.8 %copy-start.27 = (bf16[16,128,128]{2,1,0:T(8,128)(2,1)}, bf16[16,128,128]{2,1,0:T(8,128)(2,1)S(1)}, u32[]{:S(2)}) copy-start(bf16[16,128,128]{2,1,0:T(8,128)(2,1)S(1)} %collective-permute-done.19.refs_3_) | copy-start | bytes 1572868
  53.9 110.8 %collective-permute-start.7 = (bf16[32,128,128]{2,1,0:T(8,128)(2,1)}, bf16[32,128,128]{2,1,0:T(8,128)(2,1)S(1)}, u32[]{:S(2)}, u32[]{:S(2)}) collective-permute-start(bf16[32,128,128]{2,1,0:T(8,128)(2,1)} %get-tuple-element.25.refs_0_), channel_id=1, source_target_pairs={{0,2},{1,3},{2,0},{3,1},{4,6},{5,7},{6,4},{7,5}} | collective-permute-start | bytes 3145736 | tf_op jit(solution)/shard_map/ppermute | solution.py:298
  108.5 90.0 %collective-permute-start.11 = (bf16[48,128,128]{2,1,0:T(8,128)(2,1)}, bf16[48,128,128]{2,1,0:T(8,128)(2,1)}, u32[]{:S(2)}, u32[]{:S(2)}) collective-permute-start(bf16[48,128,128]{2,1,0:T(8,128)(2,1)} %get-tuple-element.27.refs_0_), channel_id=1, source_target_pairs={{0,2},{1,3},{2,0},{3,1},{4,6},{5,7},{6,4},{7,5}} | collective-permute-start | bytes 4718600 | tf_op jit(solution)/shard_map/ppermute | solution.py:298
  108.5 112.0 %collective-permute-start.16 = (bf16[48,128,128]{2,1,0:T(8,128)(2,1)S(1)}, bf16[48,128,128]{2,1,0:T(8,128)(2,1)}, u32[]{:S(2)}, u32[]{:S(2)}) collective-permute-start(bf16[48,128,128]{2,1,0:T(8,128)(2,1)S(1)} %collective-permute-done.15.refs_2_), channel_id=1, source_target_pairs={{0,1},{1,0},{2,3},{3,2},{4,5},{5,4},{6,7},{7,6}} | collective-permute-start | bytes 4718600 | tf_op jit(solution)/shard_map/ppermute | solution.py:303
  164.7 44.0 %copy-start.13 = (bf16[32,128,128]{2,1,0:T(8,128)(2,1)}, bf16[32,128,128]{2,1,0:T(8,128)(2,1)S(1)}, u32[]{:S(2)}) copy-start(bf16[32,128,128]{2,1,0:T(8,128)(2,1)S(1)} %collective-permute-done.7.refs_2_) | copy-start | bytes 3145732
  164.7 55.8 %collective-permute-start.1 = (bf16[32,128,128]{2,1,0:T(8,128)(2,1)}, bf16[32,128,128]{2,1,0:T(8,128)(2,1)}, u32[]{:S(2)}, u32[]{:S(2)}) collective-permute-start(bf16[32,128,128]{2,1,0:T(8,128)(2,1)} %get-tuple-element.19.refs_0_), channel_id=1, source_target_pairs={{0,2},{1,3},{2,0},{3,1},{4,6},{5,7},{6,4},{7,5}} | collective-permute-start | bytes 3145736 | tf_op jit(solution)/shard_map/ppermute | solution.py:298
  164.7 79.7 %collective-permute-start.14 = (bf16[48,128,128]{2,1,0:T(8,128)(2,1)S(1)}, bf16[48,128,128]{2,1,0:T(8,128)(2,1)}, u32[]{:S(2)}, u32[]{:S(2)}) collective-permute-start(bf16[48,128,128]{2,1,0:T(8,128)(2,1)S(1)} %collective-permute-done.13.refs_2_), channel_id=1, source_target_pairs={{0,1},{1,0},{2,3},{3,2},{4,5},{5,4},{6,7},{7,6}} | collective-permute-start | bytes 4718600 | tf_op jit(solution)/shard_map/ppermute | solution.py:303
  198.5 68.5 %collective-permute-start.12 = (bf16[48,128,128]{2,1,0:T(8,128)(2,1)}, bf16[48,128,128]{2,1,0:T(8,128)(2,1)}, u32[]{:S(2)}, u32[]{:S(2)}) collective-permute-start(bf16[48,128,128]{2,1,0:T(8,128)(2,1)} %collective-permute-done.11.refs_2_), channel_id=1, source_target_pairs={{0,1},{1,0},{2,3},{3,2},{4,5},{5,4},{6,7},{7,6}} | collective-permute-start | bytes 4718600 | tf_op jit(solution)/shard_map/ppermute | solution.py:303
  208.7 12.3 %copy-start.1 = (f32[512,512]{1,0:T(8,128)S(1)}, f32[512,512]{1,0:T(8,128)}, u32[]{:S(2)}) copy-start(f32[512,512]{1,0:T(8,128)} %copy-done) | copy-start | bytes 3145732
  208.7 12.3 %copy-start.3 = (bf16[128,256]{1,0:T(8,128)(2,1)S(1)}, bf16[128,256]{1,0:T(8,128)(2,1)}, u32[]{:S(2)}) copy-start(bf16[128,256]{1,0:T(8,128)(2,1)} %copy-done.2) | copy-start | bytes 196612
  208.7 12.3 %copy-start.5 = (bf16[128,256]{1,0:T(8,128)(2,1)S(1)}, bf16[128,256]{1,0:T(8,128)(2,1)}, u32[]{:S(2)}) copy-start(bf16[128,256]{1,0:T(8,128)(2,1)} %copy-done.4) | copy-start | bytes 196612
  208.7 12.3 %copy-start.6 = (bf16[128,128]{1,0:T(8,128)(2,1)S(1)}, bf16[128,128]{1,0:T(8,128)(2,1)}, u32[]{:S(2)}) copy-start(bf16[128,128]{1,0:T(8,128)(2,1)} %refs_8_.13) | copy-start | bytes 98308
  219.0 25.4 %copy-start.8 = (bf16[48,128,128]{2,1,0:T(8,128)(2,1)S(1)}, bf16[48,128,128]{2,1,0:T(8,128)(2,1)}, u32[]{:S(2)}) copy-start(bf16[48,128,128]{2,1,0:T(8,128)(2,1)} %get-tuple-element.28.refs_0_) | copy-start | bytes 4718596
  220.5 69.2 %collective-permute-start.10 = (bf16[32,128,128]{2,1,0:T(8,128)(2,1)S(1)}, bf16[32,128,128]{2,1,0:T(8,128)(2,1)S(1)}, u32[]{:S(2)}, u32[]{:S(2)}) collective-permute-start(bf16[32,128,128]{2,1,0:T(8,128)(2,1)S(1)} %collective-permute-done.9.refs_2_), channel_id=1, source_target_pairs={{0,1},{1,0},{2,3},{3,2},{4,5},{5,4},{6,7},{7,6}} | collective-permute-start | bytes 3145736 | tf_op jit(solution)/shard_map/ppermute | solution.py:303
  220.5 85.2 %collective-permute-start.8 = (bf16[32,128,128]{2,1,0:T(8,128)(2,1)}, bf16[32,128,128]{2,1,0:T(8,128)(2,1)S(1)}, u32[]{:S(2)}, u32[]{:S(2)}) collective-permute-start(bf16[32,128,128]{2,1,0:T(8,128)(2,1)} %copy-done.13), channel_id=1, source_target_pairs={{0,1},{1,0},{2,3},{3,2},{4,5},{5,4},{6,7},{7,6}} | collective-permute-start | bytes 3145736 | tf_op jit(solution)/shard_map/ppermute | solution.py:303
  221.0 100.4 %collective-permute-start.2 = (bf16[32,128,128]{2,1,0:T(8,128)(2,1)}, bf16[32,128,128]{2,1,0:T(8,128)(2,1)S(1)}, u32[]{:S(2)}, u32[]{:S(2)}) collective-permute-start(bf16[32,128,128]{2,1,0:T(8,128)(2,1)} %collective-permute-done.1.refs_2_), channel_id=1, source_target_pairs={{0,1},{1,0},{2,3},{3,2},{4,5},{5,4},{6,7},{7,6}} | collective-permute-start | bytes 3145736 | tf_op jit(solution)/shard_map/ppermute | solution.py:303
  244.4 22.6 %copy-start.7 = (bf16[48,128,128]{2,1,0:T(8,128)(2,1)S(1)}, bf16[48,128,128]{2,1,0:T(8,128)(2,1)}, u32[]{:S(2)}) copy-start(bf16[48,128,128]{2,1,0:T(8,128)(2,1)} %get-tuple-element.27.refs_0_) | copy-start | bytes 4718596
  267.0 22.8 %copy-start.12 = (bf16[32,128,128]{2,1,0:T(8,128)(2,1)S(1)}, bf16[32,128,128]{2,1,0:T(8,128)(2,1)}, u32[]{:S(2)}) copy-start(bf16[32,128,128]{2,1,0:T(8,128)(2,1)} %get-tuple-element.26.refs_0_) | copy-start | bytes 3145732
  289.7 16.0 %copy-start.11 = (bf16[32,128,128]{2,1,0:T(8,128)(2,1)S(1)}, bf16[32,128,128]{2,1,0:T(8,128)(2,1)}, u32[]{:S(2)}) copy-start(bf16[32,128,128]{2,1,0:T(8,128)(2,1)} %get-tuple-element.25.refs_0_) | copy-start | bytes 3145732
  289.7 16.0 %copy-start.14 = (bf16[32,128,128]{2,1,0:T(8,128)(2,1)S(1)}, bf16[32,128,128]{2,1,0:T(8,128)(2,1)}, u32[]{:S(2)}) copy-start(bf16[32,128,128]{2,1,0:T(8,128)(2,1)} %copy-done.13) | copy-start | bytes 3145732
  305.7 15.8 %copy-start.10 = (bf16[32,128,128]{2,1,0:T(8,128)(2,1)S(1)}, bf16[32,128,128]{2,1,0:T(8,128)(2,1)}, u32[]{:S(2)}) copy-start(bf16[32,128,128]{2,1,0:T(8,128)(2,1)} %get-tuple-element.19.refs_0_) | copy-start | bytes 3145732
  (16 other events, 27.0 us)

commit v2 on v1

--- a/solution.py
+++ b/solution.py
@@ -9,12 +9,11 @@
 
 
 LN_EPS = 1e-5
-CHUNKS = (16, 48, 48, 48, 32, 32, 32)
+CHUNKS = (16, 32, 48, 48, 48, 32, 32)
 NORM_ROWS = 16
 ATTEND_ROWS = 16
 GROUP = 16
-ATTEND_VMEM = (57 * 1024 * 1024, 40 * 1024 * 1024)
-SMALL_VMEM = pltpu.CompilerParams(vmem_limit_bytes=24 * 1024 * 1024)
+ATTEND_VMEM = (67043328, 40 * 1024 * 1024)
 SCORE_BOUND = 1e8
 VALUE_BOUND = 1e20
 SUM_RANGE = (1e-10, 1e15)
@@ -57,7 +56,7 @@
         in_specs=[whole(x.shape) for x in args],
         out_specs=[pl.BlockSpec(memory_space=pltpu.SMEM), whole((chan, 2 * chan)), whole((chan, 2 * chan))],
         out_shape=[jax.ShapeDtypeStruct((4,), jnp.int32)] + [jax.ShapeDtypeStruct((chan, 2 * chan), bf16)] * 2,
-        compiler_params=SMALL_VMEM,
+        compiler_params=VMEM_LIMIT,
         name="plan",
     )(*args)
 
@@ -138,7 +137,7 @@
             in_specs=[whole(p.shape) for p in parts], out_specs=whole(shape),
         ),
         out_shape=jax.ShapeDtypeStruct(shape, f32),
-        compiler_params=SMALL_VMEM,
+        compiler_params=VMEM_LIMIT,
         name="bias",
     )(info, *parts)
 
@@ -281,10 +280,11 @@
         col_idx = lax.axis_index('col')
         gamma, beta, wb_t = ln_gamma.reshape(1, chan), ln_beta.reshape(1, chan), w_b.T
         starts = [sum(CHUNKS[:i]) for i in range(len(CHUNKS))]
-        head = normalize(z, gamma, beta, wb_t, 0, CHUNKS[:1], False)
-        *tail, tail_bias, rest = normalize(z, gamma, beta, wb_t, CHUNKS[0], CHUNKS[1:], True)
-        own = [head[0]] + tail
-        halves = jnp.concatenate([head[1], tail_bias], axis=0).reshape(2, row_len // 2, heads, cols)
+        first, first_bias = normalize(z, gamma, beta, wb_t, 0, CHUNKS[:1], False)
+        second, second_bias = normalize(z, gamma, beta, wb_t, starts[1], CHUNKS[1:2], False)
+        *others, other_bias, rest = normalize(z, gamma, beta, wb_t, starts[2], CHUNKS[2:], True)
+        own = [first, second] + others
+        halves = jnp.concatenate([first_bias, second_bias, other_bias], axis=0).reshape(2, row_len // 2, heads, cols)
         info, w_kv, w_qg = make_plan(heads, sizes, res_mask.reshape(4, cols), gamma, beta, w_q, w_k, w_v, wb_t, w_g)
         weights = (w_kv, w_qg, w_o)
 
@@ -296,12 +296,12 @@
         far, near = [], []
         for a in own:
             far.append(lax.ppermute(a, 'col', x_pairs))
-        for a in (own[0], rest):
+        for a in (first, second, rest):
             near.append(lax.ppermute(a, 'col', core_pairs))
         out = None
         for i, (start, rows) in enumerate(zip(starts, CHUNKS)):
             diag = lax.ppermute(far[i], 'col', core_pairs)
-            out = attend(heads, sizes, info, (own[i], near[min(i, 1)], far[i], diag), (0, start - CHUNKS[0] if i else 0, 0, 0), z, bias, weights, out, start, rows)
+            out = attend(heads, sizes, info, (own[i], near[min(i, 2)], far[i], diag), (0, max(start - starts[2], 0) if i > 1 else 0, 0, 0), z, bias, weights, out, start, rows)
         return out
 
     return jax.shard_map(inner, mesh=mesh, in_specs=(tile_spec, P('dp'), P(), P(), P(), P(), P(), P(), P(), P()), out_specs=tile_spec, check_vma=False)

time: 338 us -> 345 us (1.021)
  Pallas kernels: 148 us -> 154 us
    ppermute x7, waiting for transfers between devices: 145 us -> 139 us  [inner(): far.append(lax.ppermute(a, 'col', x_pairs))]
    unnamed x56 -> x46, local copies, waits for them, and re-layouts: 8.61 us -> 11.8 us
    pallas_call x2 -> x3, Pallas kernels: 20.1 us -> 22.6 us  [normalize(): pl.pallas_call(functools.partial(norm_kernel, places), grid=(rows // step...]
  transfers between devices with their start and end apart: 20 -> 21, of which waited for: 6 -> 7; matrix products, arithmetic and copies ran while one was open for 0% -> 0% of each run, Pallas kernels for 34% -> 35%
where the time goes in v2:
time: 345 us; the launch traced here: 344 us
  waiting for transfers between devices  157 us (46%)
  Pallas kernels  154 us (45%)
  starting transfers between devices  18.9 us (5%)
  local copies, waits for them, and re-layouts  12 us (3%)
    ppermute x7, waiting for transfers between devices, inner(): far.append(lax.ppermute(a, 'col', x_pairs))  139 us
    pallas_call x7, Pallas kernels, attend(): pl.pallas_call(functools.partial(attend_kernel, heads, sizes), grid_spec=...  126 us
    pallas_call x3, Pallas kernels, normalize(): pl.pallas_call(functools.partial(norm_kernel, places), grid=(rows // step...  22.6 us
    ppermute x4, waiting for transfers between devices, inner(): parts.append(lax.ppermute(half, ('row', 'col'), bias_pairs(m)))  14.8 us
    unnamed x46, local copies, waits for them, and re-layouts  11.8 us
    ppermute x4, starting transfers between devices, inner(): parts.append(lax.ppermute(half, ('row', 'col'), bias_pairs(m)))  10.4 us
  transfers between devices with their start and end apart: 21, of which 7 were waited for; matrix products, arithmetic and copies ran while one was open for 0% of the time, Pallas kernels for 35%

profile of v2, /device:TPU:0, one launch (start us, length us, event | category | flops | bytes accessed | tf_op | source)
XLA Modules:
  0.0 343.7 jit_solution(1118185692657759153)
XLA Ops:
  0.0 16.7 %norm.3 = (bf16[48,128,128]{2,1,0:T(8,128)(2,1)}, bf16[48,128,128]{2,1,0:T(8,128)(2,1)}, bf16[48,128,128]{2,1,0:T(8,128)(2,1)}, bf16[32,128,128]{2,1,0:T(8,128)(...) custom-call(bf16[256,128,128]{2,1,0:T(8,128)(2,1)} %refs_4_.13, ...), custom_call_target="tpu_custom_call" | custom-call | flops 1022361600 | bytes 13631488 | tf_op jit(solution)/shard_map/norm/pallas_call | solution.py:102
  16.7 0.9 collective-permute-start
  17.5 2.4 norm.4
  19.9 3.5 %norm.5 = (bf16[32,128,128]{2,1,0:T(8,128)(2,1)}, bf16[32,4,128]{2,1,0:T(4,128)(2,1)}) custom-call(bf16[256,128,128]{2,1,0:T(8,128)(2,1)} %refs_4_.13, f32[1,128]{1,0:T(1,128)} %bitcast.20, f32[1,128]{1,0:T(1,128)} %bitcast.24, bf16[4,128]{1,0:T(4,128)(2,1)} %bitcast.16), custom_call_target="tpu_custom_call" | custom-call | flops 157286400 | bytes 2097152 | tf_op jit(solution)/shard_map/norm/pallas_call | solution.py:102
  23.5 1.1 pad_maximum_fusion
  25.5 6.5 %collective-permute-start.5 = (bf16[128,4,128]{2,1,0:T(4,128)(2,1)S(1)}, bf16[128,4,128]{2,1,0:T(4,128)(2,1)S(1)}, u32[]{:S(2)}, u32[]{:S(2)}) collective-permute-start(bf16[128,4,128]{2,1,0:T(4,128)(2,1)S(1)} %get-tuple-element.34), channel_id=1, source_target_pairs={{0,4},{1,5},{2,0},{3,1},{4,6},{5,7},{6,2},{7,3}} | collective-permute-start | bytes 393224 | tf_op jit(solution)/shard_map/ppermute | solution.py:294
  32.0 3.2 collective-permute-start.6
  35.2 3.2 collective-permute-start.16
  38.4 2.3 collective-permute-done.5.refs_2_
  41.3 12.5 %collective-permute-done.6.refs_3_ = bf16[128,4,128]{2,1,0:T(4,128)(2,1)} collective-permute-done((bf16[128,4,128]{2,1,0:T(4,128)(2,1)S(1)}, bf16[128,4,128]{2,1,0:T(4,128)(2,1)}, u32[]{:S(2)}, u32[]{:S(2)}) %collective-permute-start.6) | collective-permute-done | bytes 131104 | tf_op jit(solution)/shard_map/ppermute | solution.py:294
  54.8 3.1 collective-permute-done.20.refs_3_
  57.9 19.4 %collective-permute-done.16.refs_2_ = bf16[32,128,128]{2,1,0:T(8,128)(2,1)} collective-permute-done((bf16[32,128,128]{2,1,0:T(8,128)(2,1)}, bf16[32,128,128]{2,1,0:T(8,128)(2,1)}, u32[]{:S(2)}, u32[]{:S(2)}) %collective-permute-start.16) | collective-permute-done | bytes 1048608 | tf_op jit(solution)/shard_map/ppermute | solution.py:298
  77.3 1.0 copy-done.13
  78.3 2.0 collective-permute-start.9
  80.3 53.1 %collective-permute-done.7.refs_2_ = bf16[32,128,128]{2,1,0:T(8,128)(2,1)} collective-permute-done((bf16[32,128,128]{2,1,0:T(8,128)(2,1)}, bf16[32,128,128]{2,1,0:T(8,128)(2,1)}, u32[]{:S(2)}, u32[]{:S(2)}) %collective-permute-start.7) | collective-permute-done | bytes 1048608 | tf_op jit(solution)/shard_map/ppermute | solution.py:298
  134.0 33.2 %collective-permute-done.11.refs_2_ = bf16[48,128,128]{2,1,0:T(8,128)(2,1)} collective-permute-done((bf16[48,128,128]{2,1,0:T(8,128)(2,1)}, bf16[48,128,128]{2,1,0:T(8,128)(2,1)}, u32[]{:S(2)}, u32[]{:S(2)}) %collective-permute-start.11) | collective-permute-done | bytes 1572896 | tf_op jit(solution)/shard_map/ppermute | solution.py:298
  167.2 33.7 %collective-permute-done.9.refs_2_ = bf16[48,128,128]{2,1,0:T(8,128)(2,1)} collective-permute-done((bf16[48,128,128]{2,1,0:T(8,128)(2,1)}, bf16[48,128,128]{2,1,0:T(8,128)(2,1)}, u32[]{:S(2)}, u32[]{:S(2)}) %collective-permute-start.9) | collective-permute-done | bytes 1572896 | tf_op jit(solution)/shard_map/ppermute | solution.py:298
  200.9 1.7 plan.1
  202.5 3.6 %bias.1.refs_5_ = f32[512,512]{1,0:T(8,128)} custom-call(s32[4]{0:T(128)} %get-tuple-element.19.info_ref, bf16[128,4,128]{2,1,0:T(4,128)(2,1)} %copy-done.20, bf16[128,4,128]{2,1,0:T(4,128)(2,1)} %copy-done.21, bf16[128,4,128]{2,1,0:T(4,128)(2,1)} %copy-done.22, bf16[128,4,128]{2,1,0:T(4,128)(2,1)} %collective-permute-done.6.refs_3_), custom_call_target="tpu_custom_call" | custom-call | tf_op jit(solution)/shard_map/bias/pallas_call | solution.py:133
  206.7 10.1 %attend.7.refs_9_ = bf16[256,128,128]{2,1,0:T(8,128)(2,1)} custom-call(s32[4]{0:T(128)} %get-tuple-element.19.info_ref, bf16[16,128,128]{2,1,0:T(8,128)(2,1)} %get-tuple-element.32.refs_0_, bf16[16,128,128]{2,1,0:T(8,128)(2,1)} %copy-done.18, bf16[16,128,128]{2,1,0:T(8,128)(2,1)} %copy-done.17, bf16[16,128,128]{2,1,0:T(8,128)(2,1)} %copy-done.19, ...), custom_call_target="tpu_custom_call" | custom-call | flops 2097152000 | bytes 3145728 | tf_op jit(solution)/shard_map/attend/pallas_call | solution.py:240
  216.7 3.4 copy-done
  220.1 1.2 copy-done.1
  221.3 0.8 copy-done.3
  222.2 0.8 copy-done.4
  223.8 1.2 copy-done.12
  225.0 1.2 copy-done.14
  226.9 16.0 %attend.8.refs_9_ = bf16[256,128,128]{2,1,0:T(8,128)(2,1)} custom-call(s32[4]{0:T(128)S(1)} %copy-done.15, bf16[32,128,128]{2,1,0:T(8,128)(2,1)S(1)} %copy-done.12, bf16[32,128,128]{2,1,0:T(8,128)(2,1)S(1)} %copy-done.14, bf16[32,128,128]{2,1,0:T(8,128)(2,1)} %collective-permute-done.16.refs_2_, ...), custom_call_target="tpu_custom_call", output_to_operand_aliasing={{}: (10, {})} | custom-call | flops 4194304000 | bytes 6291456 | tf_op jit(solution)/shard_map/attend/pallas_call | solution.py:240
  243.4 22.7 %attend.9.refs_9_ = bf16[256,128,128]{2,1,0:T(8,128)(2,1)} custom-call(s32[4]{0:T(128)S(1)} %copy-done.16, bf16[48,128,128]{2,1,0:T(8,128)(2,1)S(1)} %copy-done.9, bf16[208,128,128]{2,1,0:T(8,128)(2,1)} %collective-permute-done.refs_1_, bf16[48,128,128]{2,1,0:T(8,128)(2,1)} %collective-permute-done.13.refs_2_, ...), custom_call_target="tpu_custom_call", output_to_operand_aliasing={{}: (10, {})} | custom-call | flops 6291456000 | bytes 9437184 | tf_op jit(solution)/shard_map/attend/pallas_call | solution.py:240
  266.2 22.7 %attend.10.refs_9_ = bf16[256,128,128]{2,1,0:T(8,128)(2,1)} custom-call(s32[4]{0:T(128)S(1)} %copy-done.16, bf16[48,128,128]{2,1,0:T(8,128)(2,1)S(1)} %copy-done.8, bf16[208,128,128]{2,1,0:T(8,128)(2,1)} %collective-permute-done.refs_1_, bf16[48,128,128]{2,1,0:T(8,128)(2,1)} %collective-permute-done.11.refs_2_, ...), custom_call_target="tpu_custom_call", output_to_operand_aliasing={{}: (10, {})} | custom-call | flops 6291456000 | bytes 9437184 | tf_op jit(solution)/shard_map/attend/pallas_call | solution.py:240
  288.9 22.9 %attend.11.refs_9_ = bf16[256,128,128]{2,1,0:T(8,128)(2,1)} custom-call(s32[4]{0:T(128)S(1)} %copy-done.16, bf16[48,128,128]{2,1,0:T(8,128)(2,1)S(1)} %copy-done.7, bf16[208,128,128]{2,1,0:T(8,128)(2,1)} %collective-permute-done.refs_1_, bf16[48,128,128]{2,1,0:T(8,128)(2,1)} %collective-permute-done.9.refs_2_, ...), custom_call_target="tpu_custom_call", output_to_operand_aliasing={{}: (10, {})} | custom-call | flops 6291456000 | bytes 9437184 | tf_op jit(solution)/shard_map/attend/pallas_call | solution.py:240
  311.9 15.9 %attend.12.refs_9_ = bf16[256,128,128]{2,1,0:T(8,128)(2,1)} custom-call(s32[4]{0:T(128)S(1)} %copy-done.16, bf16[32,128,128]{2,1,0:T(8,128)(2,1)S(1)} %copy-done.11, bf16[208,128,128]{2,1,0:T(8,128)(2,1)} %collective-permute-done.refs_1_, bf16[32,128,128]{2,1,0:T(8,128)(2,1)} %collective-permute-done.7.refs_2_, ...), custom_call_target="tpu_custom_call", output_to_operand_aliasing={{}: (10, {})} | custom-call | flops 4194304000 | bytes 6291456 | tf_op jit(solution)/shard_map/attend/pallas_call | solution.py:240
  327.8 15.9 %attend.13 = bf16[256,128,128]{2,1,0:T(8,128)(2,1)} custom-call(s32[4]{0:T(128)S(1)} %copy-done.16, bf16[32,128,128]{2,1,0:T(8,128)(2,1)S(1)} %copy-done.10, bf16[208,128,128]{2,1,0:T(8,128)(2,1)} %collective-permute-done.refs_1_, bf16[32,128,128]{2,1,0:T(8,128)(2,1)} %collective-permute-done.1.refs_2_, ...), custom_call_target="tpu_custom_call", output_to_operand_aliasing={{}: (10, {})} | custom-call | flops 4194304000 | bytes 6291456 | tf_op jit(solution)/shard_map/attend/pallas_call | solution.py:240
  (70 shorter events, 5.5 us)
Async XLA Ops:
  16.7 226.8 %collective-permute-start = (bf16[208,128,128]{2,1,0:T(8,128)(2,1)}, bf16[208,128,128]{2,1,0:T(8,128)(2,1)}, u32[]{:S(2)}, u32[]{:S(2)}) collective-permute-start(bf16[208,128,128]{2,1,0:T(8,128)(2,1)} %get-tuple-element.21), channel_id=1, source_target_pairs={{0,1},{1,0},{2,3},{3,2},{4,5},{5,4},{6,7},{7,6}} | collective-permute-start | bytes 20447240 | tf_op jit(solution)/shard_map/ppermute | solution.py:300
  24.8 7.2 %collective-permute-start.3 = (bf16[128,4,128]{2,1,0:T(4,128)(2,1)S(1)}, bf16[128,4,128]{2,1,0:T(4,128)(2,1)S(1)}, u32[]{:S(2)}, u32[]{:S(2)}) collective-permute-start(bf16[128,4,128]{2,1,0:T(4,128)(2,1)S(1)} %get-tuple-element.36), channel_id=1, source_target_pairs={{0,0},{1,1},{2,4},{3,5},{4,2},{5,3},{6,6},{7,7}} | collective-permute-start | bytes 393224 | tf_op jit(solution)/shard_map/ppermute | solution.py:294
  25.4 9.8 %collective-permute-start.4 = (bf16[128,4,128]{2,1,0:T(4,128)(2,1)S(1)}, bf16[128,4,128]{2,1,0:T(4,128)(2,1)S(1)}, u32[]{:S(2)}, u32[]{:S(2)}) collective-permute-start(bf16[128,4,128]{2,1,0:T(4,128)(2,1)S(1)} %get-tuple-element.35), channel_id=1, source_target_pairs={{0,1},{1,0},{2,5},{3,4},{4,3},{5,2},{6,7},{7,6}} | collective-permute-start | bytes 393224 | tf_op jit(solution)/shard_map/ppermute | solution.py:294
  25.5 15.2 %collective-permute-start.5 = (bf16[128,4,128]{2,1,0:T(4,128)(2,1)S(1)}, bf16[128,4,128]{2,1,0:T(4,128)(2,1)S(1)}, u32[]{:S(2)}, u32[]{:S(2)}) collective-permute-start(bf16[128,4,128]{2,1,0:T(4,128)(2,1)S(1)} %get-tuple-element.34), channel_id=1, source_target_pairs={{0,4},{1,5},{2,0},{3,1},{4,6},{5,7},{6,2},{7,3}} | collective-permute-start | bytes 393224 | tf_op jit(solution)/shard_map/ppermute | solution.py:294
  32.0 22.7 %collective-permute-start.19 = (bf16[16,128,128]{2,1,0:T(8,128)(2,1)}, bf16[16,128,128]{2,1,0:T(8,128)(2,1)S(1)}, u32[]{:S(2)}, u32[]{:S(2)}) collective-permute-start(bf16[16,128,128]{2,1,0:T(8,128)(2,1)} %get-tuple-element.32.refs_0_), channel_id=1, source_target_pairs={{0,2},{1,3},{2,0},{3,1},{4,6},{5,7},{6,4},{7,5}} | collective-permute-start | bytes 1572872 | tf_op jit(solution)/shard_map/ppermute | solution.py:298
  32.0 21.9 %collective-permute-start.6 = (bf16[128,4,128]{2,1,0:T(4,128)(2,1)S(1)}, bf16[128,4,128]{2,1,0:T(4,128)(2,1)}, u32[]{:S(2)}, u32[]{:S(2)}) collective-permute-start(bf16[128,4,128]{2,1,0:T(4,128)(2,1)S(1)} %get-tuple-element.33), channel_id=1, source_target_pairs={{0,5},{1,4},{2,1},{3,0},{4,7},{5,6},{6,3},{7,2}} | collective-permute-start | bytes 393224 | tf_op jit(solution)/shard_map/ppermute | solution.py:294
  35.2 42.0 %collective-permute-start.16 = (bf16[32,128,128]{2,1,0:T(8,128)(2,1)}, bf16[32,128,128]{2,1,0:T(8,128)(2,1)}, u32[]{:S(2)}, u32[]{:S(2)}) collective-permute-start(bf16[32,128,128]{2,1,0:T(8,128)(2,1)} %get-tuple-element.31.refs_0_), channel_id=1, source_target_pairs={{0,2},{1,3},{2,0},{3,1},{4,6},{5,7},{6,4},{7,5}} | collective-permute-start | bytes 3145736 | tf_op jit(solution)/shard_map/ppermute | solution.py:298
  40.7 14.0 %collective-permute-start.18 = (bf16[16,128,128]{2,1,0:T(8,128)(2,1)}, bf16[16,128,128]{2,1,0:T(8,128)(2,1)S(1)}, u32[]{:S(2)}, u32[]{:S(2)}) collective-permute-start(bf16[16,128,128]{2,1,0:T(8,128)(2,1)} %get-tuple-element.32.refs_0_), channel_id=1, source_target_pairs={{0,1},{1,0},{2,3},{3,2},{4,5},{5,4},{6,7},{7,6}} | collective-permute-start | bytes 1572872 | tf_op jit(solution)/shard_map/ppermute | solution.py:300
  53.9 23.4 %collective-permute-start.15 = (bf16[32,128,128]{2,1,0:T(8,128)(2,1)}, bf16[32,128,128]{2,1,0:T(8,128)(2,1)S(1)}, u32[]{:S(2)}, u32[]{:S(2)}) collective-permute-start(bf16[32,128,128]{2,1,0:T(8,128)(2,1)} %get-tuple-element.31.refs_0_), channel_id=1, source_target_pairs={{0,1},{1,0},{2,3},{3,2},{4,5},{5,4},{6,7},{7,6}} | collective-permute-start | bytes 3145736 | tf_op jit(solution)/shard_map/ppermute | solution.py:300
  54.6 22.7 %copy-start.17 = (bf16[16,128,128]{2,1,0:T(8,128)(2,1)}, bf16[16,128,128]{2,1,0:T(8,128)(2,1)S(1)}, u32[]{:S(2)}) copy-start(bf16[16,128,128]{2,1,0:T(8,128)(2,1)S(1)} %collective-permute-done.19.refs_2_) | copy-start | bytes 1572868
  54.6 3.2 collective-permute-start.20
  54.7 23.6 %copy-start.18 = (bf16[16,128,128]{2,1,0:T(8,128)(2,1)}, bf16[16,128,128]{2,1,0:T(8,128)(2,1)S(1)}, u32[]{:S(2)}) copy-start(bf16[16,128,128]{2,1,0:T(8,128)(2,1)S(1)} %collective-permute-done.18.refs_1_) | copy-start | bytes 1572868
  54.7 78.8 %collective-permute-start.13 = (bf16[48,128,128]{2,1,0:T(8,128)(2,1)}, bf16[48,128,128]{2,1,0:T(8,128)(2,1)}, u32[]{:S(2)}, u32[]{:S(2)}) collective-permute-start(bf16[48,128,128]{2,1,0:T(8,128)(2,1)} %get-tuple-element.30.refs_0_), channel_id=1, source_target_pairs={{0,2},{1,3},{2,0},{3,1},{4,6},{5,7},{6,4},{7,5}} | collective-permute-start | bytes 4718600 | tf_op jit(solution)/shard_map/ppermute | solution.py:298
  57.9 22.4 %copy-start.19 = (bf16[16,128,128]{2,1,0:T(8,128)(2,1)}, bf16[16,128,128]{2,1,0:T(8,128)(2,1)S(1)}, u32[]{:S(2)}) copy-start(bf16[16,128,128]{2,1,0:T(8,128)(2,1)S(1)} %collective-permute-done.20.refs_3_) | copy-start | bytes 1572868
  57.9 75.6 %collective-permute-start.7 = (bf16[32,128,128]{2,1,0:T(8,128)(2,1)}, bf16[32,128,128]{2,1,0:T(8,128)(2,1)}, u32[]{:S(2)}, u32[]{:S(2)}) collective-permute-start(bf16[32,128,128]{2,1,0:T(8,128)(2,1)} %get-tuple-element.27.refs_0_), channel_id=1, source_target_pairs={{0,2},{1,3},{2,0},{3,1},{4,6},{5,7},{6,4},{7,5}} | collective-permute-start | bytes 3145736 | tf_op jit(solution)/shard_map/ppermute | solution.py:298
  77.3 89.9 %collective-permute-start.11 = (bf16[48,128,128]{2,1,0:T(8,128)(2,1)}, bf16[48,128,128]{2,1,0:T(8,128)(2,1)}, u32[]{:S(2)}, u32[]{:S(2)}) collective-permute-start(bf16[48,128,128]{2,1,0:T(8,128)(2,1)} %get-tuple-element.29.refs_0_), channel_id=1, source_target_pairs={{0,2},{1,3},{2,0},{3,1},{4,6},{5,7},{6,4},{7,5}} | collective-permute-start | bytes 4718600 | tf_op jit(solution)/shard_map/ppermute | solution.py:298
  78.3 122.6 %collective-permute-start.9 = (bf16[48,128,128]{2,1,0:T(8,128)(2,1)}, bf16[48,128,128]{2,1,0:T(8,128)(2,1)}, u32[]{:S(2)}, u32[]{:S(2)}) collective-permute-start(bf16[48,128,128]{2,1,0:T(8,128)(2,1)} %get-tuple-element.28.refs_0_), channel_id=1, source_target_pairs={{0,2},{1,3},{2,0},{3,1},{4,6},{5,7},{6,4},{7,5}} | collective-permute-start | bytes 4718600 | tf_op jit(solution)/shard_map/ppermute | solution.py:298
  133.4 72.7 %collective-permute-start.17 = (bf16[32,128,128]{2,1,0:T(8,128)(2,1)}, bf16[32,128,128]{2,1,0:T(8,128)(2,1)}, u32[]{:S(2)}, u32[]{:S(2)}) collective-permute-start(bf16[32,128,128]{2,1,0:T(8,128)(2,1)} %collective-permute-done.16.refs_2_), channel_id=1, source_target_pairs={{0,1},{1,0},{2,3},{3,2},{4,5},{5,4},{6,7},{7,6}} | collective-permute-start | bytes 3145736 | tf_op jit(solution)/shard_map/ppermute | solution.py:303
  133.5 109.5 %collective-permute-start.14 = (bf16[48,128,128]{2,1,0:T(8,128)(2,1)}, bf16[48,128,128]{2,1,0:T(8,128)(2,1)}, u32[]{:S(2)}, u32[]{:S(2)}) collective-permute-start(bf16[48,128,128]{2,1,0:T(8,128)(2,1)} %collective-permute-done.13.refs_2_), channel_id=1, source_target_pairs={{0,1},{1,0},{2,3},{3,2},{4,5},{5,4},{6,7},{7,6}} | collective-permute-start | bytes 4718600 | tf_op jit(solution)/shard_map/ppermute | solution.py:303
  167.2 75.7 %collective-permute-start.1 = (bf16[32,128,128]{2,1,0:T(8,128)(2,1)}, bf16[32,128,128]{2,1,0:T(8,128)(2,1)}, u32[]{:S(2)}, u32[]{:S(2)}) collective-permute-start(bf16[32,128,128]{2,1,0:T(8,128)(2,1)} %get-tuple-element.20.refs_0_), channel_id=1, source_target_pairs={{0,2},{1,3},{2,0},{3,1},{4,6},{5,7},{6,4},{7,5}} | collective-permute-start | bytes 3145736 | tf_op jit(solution)/shard_map/ppermute | solution.py:298
  200.9 65.3 %collective-permute-start.12 = (bf16[48,128,128]{2,1,0:T(8,128)(2,1)}, bf16[48,128,128]{2,1,0:T(8,128)(2,1)}, u32[]{:S(2)}, u32[]{:S(2)}) collective-permute-start(bf16[48,128,128]{2,1,0:T(8,128)(2,1)} %collective-permute-done.11.refs_2_), channel_id=1, source_target_pairs={{0,1},{1,0},{2,3},{3,2},{4,5},{5,4},{6,7},{7,6}} | collective-permute-start | bytes 4718600 | tf_op jit(solution)/shard_map/ppermute | solution.py:303
  206.2 82.7 %collective-permute-start.10 = (bf16[48,128,128]{2,1,0:T(8,128)(2,1)}, bf16[48,128,128]{2,1,0:T(8,128)(2,1)}, u32[]{:S(2)}, u32[]{:S(2)}) collective-permute-start(bf16[48,128,128]{2,1,0:T(8,128)(2,1)} %collective-permute-done.9.refs_2_), channel_id=1, source_target_pairs={{0,1},{1,0},{2,3},{3,2},{4,5},{5,4},{6,7},{7,6}} | collective-permute-start | bytes 4718600 | tf_op jit(solution)/shard_map/ppermute | solution.py:303
  226.8 16.6 %copy-start.2 = (f32[512,512]{1,0:T(8,128)S(1)}, f32[512,512]{1,0:T(8,128)}, u32[]{:S(2)}) copy-start(f32[512,512]{1,0:T(8,128)} %bias.1.refs_5_) | copy-start | bytes 3145732
  226.8 16.6 %copy-start.6 = (bf16[128,128]{1,0:T(8,128)(2,1)S(1)}, bf16[128,128]{1,0:T(8,128)(2,1)}, u32[]{:S(2)}) copy-start(bf16[128,128]{1,0:T(8,128)(2,1)} %refs_8_.13) | copy-start | bytes 98308
  226.8 16.6 %copy-start.9 = (bf16[48,128,128]{2,1,0:T(8,128)(2,1)S(1)}, bf16[48,128,128]{2,1,0:T(8,128)(2,1)}, u32[]{:S(2)}) copy-start(bf16[48,128,128]{2,1,0:T(8,128)(2,1)} %get-tuple-element.30.refs_0_) | copy-start | bytes 4718596
  226.8 16.6 %copy-start.16 = (s32[4]{0:T(128)S(1)}, s32[4]{0:T(128)}, u32[]{:S(2)}) copy-start(s32[4]{0:T(128)} %get-tuple-element.19.info_ref) | copy-start | bytes 52
  242.9 23.3 %copy-start.8 = (bf16[48,128,128]{2,1,0:T(8,128)(2,1)S(1)}, bf16[48,128,128]{2,1,0:T(8,128)(2,1)}, u32[]{:S(2)}) copy-start(bf16[48,128,128]{2,1,0:T(8,128)(2,1)} %get-tuple-element.29.refs_0_) | copy-start | bytes 4718596
  242.9 69.0 %collective-permute-start.8 = (bf16[32,128,128]{2,1,0:T(8,128)(2,1)}, bf16[32,128,128]{2,1,0:T(8,128)(2,1)S(1)}, u32[]{:S(2)}, u32[]{:S(2)}) collective-permute-start(bf16[32,128,128]{2,1,0:T(8,128)(2,1)} %collective-permute-done.7.refs_2_), channel_id=1, source_target_pairs={{0,1},{1,0},{2,3},{3,2},{4,5},{5,4},{6,7},{7,6}} | collective-permute-start | bytes 3145736 | tf_op jit(solution)/shard_map/ppermute | solution.py:303
  242.9 84.9 %collective-permute-start.2 = (bf16[32,128,128]{2,1,0:T(8,128)(2,1)}, bf16[32,128,128]{2,1,0:T(8,128)(2,1)S(1)}, u32[]{:S(2)}, u32[]{:S(2)}) collective-permute-start(bf16[32,128,128]{2,1,0:T(8,128)(2,1)} %collective-permute-done.1.refs_2_), channel_id=1, source_target_pairs={{0,1},{1,0},{2,3},{3,2},{4,5},{5,4},{6,7},{7,6}} | collective-permute-start | bytes 3145736 | tf_op jit(solution)/shard_map/ppermute | solution.py:303
  266.2 22.8 %copy-start.7 = (bf16[48,128,128]{2,1,0:T(8,128)(2,1)S(1)}, bf16[48,128,128]{2,1,0:T(8,128)(2,1)}, u32[]{:S(2)}) copy-start(bf16[48,128,128]{2,1,0:T(8,128)(2,1)} %get-tuple-element.28.refs_0_) | copy-start | bytes 4718596
  288.9 23.0 %copy-start.11 = (bf16[32,128,128]{2,1,0:T(8,128)(2,1)S(1)}, bf16[32,128,128]{2,1,0:T(8,128)(2,1)}, u32[]{:S(2)}) copy-start(bf16[32,128,128]{2,1,0:T(8,128)(2,1)} %get-tuple-element.27.refs_0_) | copy-start | bytes 3145732
  311.9 15.9 %copy-start.10 = (bf16[32,128,128]{2,1,0:T(8,128)(2,1)S(1)}, bf16[32,128,128]{2,1,0:T(8,128)(2,1)}, u32[]{:S(2)}) copy-start(bf16[32,128,128]{2,1,0:T(8,128)(2,1)} %get-tuple-element.20.refs_0_) | copy-start | bytes 3145732
  (12 other events, 25.9 us)

commit v3 on v2

--- a/solution.py
+++ b/solution.py
@@ -13,7 +13,7 @@
 NORM_ROWS = 16
 ATTEND_ROWS = 16
 GROUP = 16
-ATTEND_VMEM = (67043328, 40 * 1024 * 1024)
+ATTEND_VMEM = 67043328
 SCORE_BOUND = 1e8
 VALUE_BOUND = 1e20
 SUM_RANGE = (1e-10, 1e15)
@@ -31,7 +31,7 @@
 def plan_kernel(heads, sizes, mask_ref, gamma_ref, beta_ref, wq_ref, wk_ref, wv_ref, wb_ref, wg_ref, info_ref, wkv_ref, wqg_ref):
     chan = gamma_ref.shape[1]
     dim = chan // heads
-    row_idx, col_idx = lax.axis_index('row'), lax.axis_index('col')
+    col_idx = lax.axis_index('col')
     wkv_ref[:, :chan], wkv_ref[:, chan:] = wk_ref[...], wv_ref[...]
     wqg_ref[:, :chan], wqg_ref[:, chan:] = wq_ref[...], wg_ref[...]
     reach = jnp.broadcast_to(jnp.abs(gamma_ref[...]) * chan ** 0.5 + jnp.abs(beta_ref[...]), (8, chan)) * 1.05
@@ -44,9 +44,8 @@
     length = jnp.sum(mask_ref[...].astype(f32)).astype(jnp.int32)
     used = jnp.where(length <= sizes[0], sizes[0], sizes[1])
     info_ref[0] = col_idx
-    info_ref[1] = 2 * row_idx + (col_idx & 1)
-    info_ref[2] = length
-    info_ref[3] = jnp.where((s_bound < SCORE_BOUND) & (v_bound < VALUE_BOUND), used, sizes[2])
+    info_ref[1] = length
+    info_ref[2] = jnp.where((s_bound < SCORE_BOUND) & (v_bound < VALUE_BOUND), used, sizes[2])
 
 
 def make_plan(heads, sizes, *args):
@@ -55,7 +54,7 @@
         functools.partial(plan_kernel, heads, sizes),
         in_specs=[whole(x.shape) for x in args],
         out_specs=[pl.BlockSpec(memory_space=pltpu.SMEM), whole((chan, 2 * chan)), whole((chan, 2 * chan))],
-        out_shape=[jax.ShapeDtypeStruct((4,), jnp.int32)] + [jax.ShapeDtypeStruct((chan, 2 * chan), bf16)] * 2,
+        out_shape=[jax.ShapeDtypeStruct((3,), jnp.int32)] + [jax.ShapeDtypeStruct((chan, 2 * chan), bf16)] * 2,
         compiler_params=VMEM_LIMIT,
         name="plan",
     )(*args)
@@ -117,9 +116,9 @@
 def bias_kernel(info_ref, *refs):
     parts, out_ref = refs[:-1], refs[-1]
     queries, heads, cols = parts[0].shape
-    base, length = info_ref[1], info_ref[2]
+    col, length = info_ref[0], info_ref[1]
     for m, part in enumerate(parts):
-        first = pl.multiple_of((base ^ m) * cols, cols)
+        first = pl.multiple_of((col ^ m) * cols, cols)
         key = first + lax.broadcasted_iota(jnp.int32, (cols, queries), 0)
         key_bias = jnp.where(key < length, 0.0, -1e9).astype(f32)
         b = part[...].astype(f32)
@@ -148,7 +147,7 @@
     out_ref, k_s, vt_s, q_s, g_s, p_s, l_s, o_s = refs[-8:]
     step, cols, chan = z_ref.shape
     dim = chan // heads
-    col, used = info_ref[0], info_ref[3]
+    col, used = info_ref[0], info_ref[2]
 
     @pl.when(pl.program_id(0) == 0)
     def _():
@@ -253,7 +252,7 @@
         ),
         out_shape=jax.ShapeDtypeStruct(z.shape, z.dtype),
         input_output_aliases=alias,
-        compiler_params=pltpu.CompilerParams(vmem_limit_bytes=ATTEND_VMEM[prev is not None]),
+        compiler_params=pltpu.CompilerParams(vmem_limit_bytes=ATTEND_VMEM),
         cost_estimate=pl.CostEstimate(flops=rows * cols * chan * 8000, bytes_accessed=rows * cols * chan * 12, transcendentals=0),
         name="attend",
     )(*args)
@@ -261,20 +260,12 @@
 
 def solution(mesh):
     tile_spec = P(('dp', 'row'), 'col', None)
-    num_rows, num_cols = mesh.shape['row'], mesh.shape['col']
+    num_cols = mesh.shape['col']
     x_pairs = [(c, c ^ 2) for c in range(num_cols)]
     core_pairs = [(c, c ^ 1) for c in range(num_cols)]
 
-    def bias_pairs(m):
-        pairs = []
-        for r in range(num_rows):
-            for c in range(num_cols):
-                e = c ^ m
-                pairs.append((r * num_cols + c, (e >> 1) * num_cols + 2 * r + (e & 1)))
-        return pairs
-
     def inner(z, res_mask, ln_gamma, ln_beta, w_q, w_k, w_v, w_b, w_g, w_o):
-        row_len, cols, chan = z.shape
+        _, cols, chan = z.shape
         heads = w_b.shape[1]
         sizes = (3 * cols, 7 * cols // 2, 4 * cols)
         col_idx = lax.axis_index('col')
@@ -284,14 +275,17 @@
         second, second_bias = normalize(z, gamma, beta, wb_t, starts[1], CHUNKS[1:2], False)
         *others, other_bias, rest = normalize(z, gamma, beta, wb_t, starts[2], CHUNKS[2:], True)
         own = [first, second] + others
-        halves = jnp.concatenate([first_bias, second_bias, other_bias], axis=0).reshape(2, row_len // 2, heads, cols)
+        bias_tile = jnp.concatenate([first_bias, second_bias, other_bias], axis=0)
+        other_tile = lax.ppermute(bias_tile, 'row', [(0, 1), (1, 0)])
         info, w_kv, w_qg = make_plan(heads, sizes, res_mask.reshape(4, cols), gamma, beta, w_q, w_k, w_v, wb_t, w_g)
         weights = (w_kv, w_qg, w_o)
 
+        halves = [bias_tile[:cols], bias_tile[cols:], other_tile[:cols], other_tile[cols:]]
         parts = []
-        for m in range(4):
-            half = lax.dynamic_index_in_dim(halves, (col_idx ^ m) & 1, 0, keepdims=False)
-            parts.append(lax.ppermute(half, ('row', 'col'), bias_pairs(m)))
+        for m in range(num_cols):
+            place = (col_idx ^ m) ^ (2 * lax.axis_index('row'))
+            send = jnp.where(place & 2, jnp.where(place & 1, halves[3], halves[2]), jnp.where(place & 1, halves[1], halves[0]))
+            parts.append(lax.ppermute(send, 'col', [(c, c ^ m) for c in range(num_cols)]) if m else send)
         bias = lay_bias(info, parts)
         far, near = [], []
         for a in own:

time: 345 us -> 346 us (level)
  Pallas kernels: 154 us -> 161 us
  local copies, waits for them, and re-layouts: 12 us -> 5.01 us
    ppermute x4, waiting for transfers between devices: 14.8 us -> 22.7 us  [the longest x3 15.7 us: inner(): lax.ppermute(send, 'col', [(c, c ^ m) for c in range(num_cols)])]
    unnamed x46 -> x16, local copies, waits for them, and re-layouts: 11.8 us -> 3.98 us
    pallas_call x7, Pallas kernels: 126 us -> 133 us  [attend(): pl.pallas_call(functools.partial(attend_kernel, heads, sizes), grid_spec=...]
    ppermute x4, starting transfers between devices: 10.4 us -> 5.53 us  [the longest x3 2.99 us: inner(): lax.ppermute(send, 'col', [(c, c ^ m) for c in range(num_cols)])]
  transfers between devices with their start and end apart: 21 -> 21, of which waited for: 7 -> 8; matrix products, arithmetic and copies ran while one was open for 0% -> 2% of each run, Pallas kernels for 35% -> 37%
where the time goes in v3:
time: 346 us; the launch traced here: 345 us
  Pallas kernels  161 us (47%)
  waiting for transfers between devices  159 us (46%)
  starting transfers between devices  17.1 us (5%)
  local copies, waits for them, and re-layouts  5.01 us (1%)
    ppermute x7, waiting for transfers between devices, inner(): far.append(lax.ppermute(a, 'col', x_pairs))  136 us
    pallas_call x7, Pallas kernels, attend(): pl.pallas_call(functools.partial(attend_kernel, heads, sizes), grid_spec=...  133 us
    pallas_call x3, Pallas kernels, normalize(): pl.pallas_call(functools.partial(norm_kernel, places), grid=(rows // step...  22.7 us
    ppermute x3, waiting for transfers between devices, inner(): lax.ppermute(send, 'col', [(c, c ^ m) for c in range(num_cols)])  15.7 us
    ppermute x7, starting transfers between devices, inner(): far.append(lax.ppermute(a, 'col', x_pairs))  7.98 us
    ppermute x1, waiting for transfers between devices, inner(): other_tile = lax.ppermute(bias_tile, 'row', [(0, 1), (1, 0)])  6.97 us
  transfers between devices with their start and end apart: 21, of which 8 were waited for; matrix products, arithmetic and copies ran while one was open for 2% of the time, Pallas kernels for 37%

profile of v3, /device:TPU:0, one launch (start us, length us, event | category | flops | bytes accessed | tf_op | source)
XLA Modules:
  0.0 345.4 jit_solution(8191262967391274007)
XLA Ops:
  0.0 16.7 %norm.3 = (bf16[48,128,128]{2,1,0:T(8,128)(2,1)}, bf16[48,128,128]{2,1,0:T(8,128)(2,1)}, bf16[48,128,128]{2,1,0:T(8,128)(2,1)}, bf16[32,128,128]{2,1,0:T(8,128)(...) custom-call(bf16[256,128,128]{2,1,0:T(8,128)(2,1)} %refs_4_.13, ...), custom_call_target="tpu_custom_call" | custom-call | flops 1022361600 | bytes 13631488 | tf_op jit(solution)/shard_map/norm/pallas_call | solution.py:101
  16.7 0.9 collective-permute-start
  17.6 2.4 norm.4
  20.1 3.5 %norm.5 = (bf16[32,128,128]{2,1,0:T(8,128)(2,1)}, bf16[32,4,128]{2,1,0:T(4,128)(2,1)}) custom-call(bf16[256,128,128]{2,1,0:T(8,128)(2,1)} %refs_4_.13, f32[1,128]{1,0:T(1,128)} %bitcast.10, f32[1,128]{1,0:T(1,128)} %bitcast.14, bf16[4,128]{1,0:T(4,128)(2,1)} %bitcast.6), custom_call_target="tpu_custom_call" | custom-call | flops 157286400 | bytes 2097152 | tf_op jit(solution)/shard_map/norm/pallas_call | solution.py:101
  24.3 0.8 constant_dynamic-update-slice_fusion.1
  25.1 1.0 constant_dynamic-update-slice_fusion
  26.1 2.5 collective-permute-start.3
  28.7 7.0 %collective-permute-done.3 = bf16[256,4,128]{2,1,0:T(4,128)(2,1)S(1)} collective-permute-done((bf16[256,4,128]{2,1,0:T(4,128)(2,1)S(1)}, bf16[256,4,128]{2,1,0:T(4,128)(2,1)S(1)}, u32[]{:S(2)}, u32[]{:S(2)}) %collective-permute-start.3) | collective-permute-done | bytes 262176 | tf_op jit(solution)/shard_map/ppermute | solution.py:279
  36.3 1.1 select_select_fusion
  37.5 1.7 collective-permute-start.5
  39.6 1.2 collective-permute-start.6
  41.4 2.6 collective-permute-done.5.refs_2_
  44.0 13.2 %collective-permute-done.6.refs_3_ = bf16[128,4,128]{2,1,0:T(4,128)(2,1)S(1)} collective-permute-done((bf16[128,4,128]{2,1,0:T(4,128)(2,1)S(1)}, bf16[128,4,128]{2,1,0:T(4,128)(2,1)S(1)}, u32[]{:S(2)}, u32[]{:S(2)}) %collective-permute-start.6) | collective-permute-done | bytes 131104 | tf_op jit(solution)/shard_map/ppermute | solution.py:288
  57.8 0.8 copy-done.1
  59.2 1.7 collective-permute-start.13
  61.8 1.7 collective-permute-start.7
  63.5 17.0 %collective-permute-done.16.refs_2_ = bf16[32,128,128]{2,1,0:T(8,128)(2,1)} collective-permute-done((bf16[32,128,128]{2,1,0:T(8,128)(2,1)}, bf16[32,128,128]{2,1,0:T(8,128)(2,1)}, u32[]{:S(2)}, u32[]{:S(2)}) %collective-permute-start.16) | collective-permute-done | bytes 1048608 | tf_op jit(solution)/shard_map/ppermute | solution.py:292
  80.5 1.7 collective-permute-start.11
  82.6 54.1 %collective-permute-done.7.refs_2_ = bf16[32,128,128]{2,1,0:T(8,128)(2,1)} collective-permute-done((bf16[32,128,128]{2,1,0:T(8,128)(2,1)}, bf16[32,128,128]{2,1,0:T(8,128)(2,1)}, u32[]{:S(2)}, u32[]{:S(2)}) %collective-permute-start.7) | collective-permute-done | bytes 1048608 | tf_op jit(solution)/shard_map/ppermute | solution.py:292
  137.2 33.2 %collective-permute-done.11.refs_2_ = bf16[48,128,128]{2,1,0:T(8,128)(2,1)} collective-permute-done((bf16[48,128,128]{2,1,0:T(8,128)(2,1)}, bf16[48,128,128]{2,1,0:T(8,128)(2,1)}, u32[]{:S(2)}, u32[]{:S(2)}) %collective-permute-start.11) | collective-permute-done | bytes 1572896 | tf_op jit(solution)/shard_map/ppermute | solution.py:292
  170.4 1.7 collective-permute-start.1
  172.1 32.0 %collective-permute-done.9.refs_2_ = bf16[48,128,128]{2,1,0:T(8,128)(2,1)} collective-permute-done((bf16[48,128,128]{2,1,0:T(8,128)(2,1)}, bf16[48,128,128]{2,1,0:T(8,128)(2,1)}, u32[]{:S(2)}, u32[]{:S(2)}) %collective-permute-start.9) | collective-permute-done | bytes 1572896 | tf_op jit(solution)/shard_map/ppermute | solution.py:292
  204.1 1.7 plan.1
  205.8 1.9 select_select_fusion.3.refs_0_
  207.7 3.6 %bias.1.refs_5_ = f32[512,512]{1,0:T(8,128)} custom-call(s32[3]{0:T(128)} %get-tuple-element.19.info_ref, bf16[128,4,128]{2,1,0:T(4,128)(2,1)} %select_select_fusion.3.refs_0_, bf16[128,4,128]{2,1,0:T(4,128)(2,1)} %copy-done.5, bf16[128,4,128]{2,1,0:T(4,128)(2,1)} %collective-permute-done.5.refs_2_, bf16[128,4,128]{2,1,0:T(4,128)(2,1)} %copy-done.6), custom_call_target="tpu_custom_call" | custom-call | tf_op jit(solution)/shard_map/bias/pallas_call | solution.py:132
  211.7 10.1 %attend.7.refs_9_ = bf16[256,128,128]{2,1,0:T(8,128)(2,1)} custom-call(s32[3]{0:T(128)} %get-tuple-element.19.info_ref, bf16[16,128,128]{2,1,0:T(8,128)(2,1)} %get-tuple-element.32.refs_0_, bf16[16,128,128]{2,1,0:T(8,128)(2,1)} %copy-done.2, bf16[16,128,128]{2,1,0:T(8,128)(2,1)} %copy-done.1, bf16[16,128,128]{2,1,0:T(8,128)(2,1)} %copy-done.3, ...), custom_call_target="tpu_custom_call" | custom-call | flops 2097152000 | bytes 3145728 | tf_op jit(solution)/shard_map/attend/pallas_call | solution.py:239
  221.8 17.3 %attend.8.refs_9_ = bf16[256,128,128]{2,1,0:T(8,128)(2,1)} custom-call(s32[3]{0:T(128)} %get-tuple-element.19.info_ref, bf16[32,128,128]{2,1,0:T(8,128)(2,1)} %get-tuple-element.31.refs_0_, bf16[32,128,128]{2,1,0:T(8,128)(2,1)} %collective-permute-done.15.refs_1_, ...), custom_call_target="tpu_custom_call", output_to_operand_aliasing={{}: (10, {})} | custom-call | flops 4194304000 | bytes 6291456 | tf_op jit(solution)/shard_map/attend/pallas_call | solution.py:239
  239.7 23.7 %attend.9.refs_9_ = bf16[256,128,128]{2,1,0:T(8,128)(2,1)} custom-call(s32[3]{0:T(128)} %get-tuple-element.19.info_ref, bf16[48,128,128]{2,1,0:T(8,128)(2,1)} %get-tuple-element.30.refs_0_, bf16[208,128,128]{2,1,0:T(8,128)(2,1)} %collective-permute-done.refs_1_, ...), custom_call_target="tpu_custom_call", output_to_operand_aliasing={{}: (10, {})} | custom-call | flops 6291456000 | bytes 9437184 | tf_op jit(solution)/shard_map/attend/pallas_call | solution.py:239
  263.4 23.7 %attend.10.refs_9_ = bf16[256,128,128]{2,1,0:T(8,128)(2,1)} custom-call(s32[3]{0:T(128)} %get-tuple-element.19.info_ref, bf16[48,128,128]{2,1,0:T(8,128)(2,1)} %get-tuple-element.29.refs_0_, bf16[208,128,128]{2,1,0:T(8,128)(2,1)} %collective-permute-done.refs_1_, ...), custom_call_target="tpu_custom_call", output_to_operand_aliasing={{}: (10, {})} | custom-call | flops 6291456000 | bytes 9437184 | tf_op jit(solution)/shard_map/attend/pallas_call | solution.py:239
  287.1 24.0 %attend.11.refs_9_ = bf16[256,128,128]{2,1,0:T(8,128)(2,1)} custom-call(s32[3]{0:T(128)} %get-tuple-element.19.info_ref, bf16[48,128,128]{2,1,0:T(8,128)(2,1)} %get-tuple-element.28.refs_0_, bf16[208,128,128]{2,1,0:T(8,128)(2,1)} %collective-permute-done.refs_1_, ...), custom_call_target="tpu_custom_call", output_to_operand_aliasing={{}: (10, {})} | custom-call | flops 6291456000 | bytes 9437184 | tf_op jit(solution)/shard_map/attend/pallas_call | solution.py:239
  311.1 17.2 %attend.12.refs_9_ = bf16[256,128,128]{2,1,0:T(8,128)(2,1)} custom-call(s32[3]{0:T(128)} %get-tuple-element.19.info_ref, bf16[32,128,128]{2,1,0:T(8,128)(2,1)} %get-tuple-element.27.refs_0_, bf16[208,128,128]{2,1,0:T(8,128)(2,1)} %collective-permute-done.refs_1_, ...), custom_call_target="tpu_custom_call", output_to_operand_aliasing={{}: (10, {})} | custom-call | flops 4194304000 | bytes 6291456 | tf_op jit(solution)/shard_map/attend/pallas_call | solution.py:239
  328.3 17.2 %attend.13 = bf16[256,128,128]{2,1,0:T(8,128)(2,1)} custom-call(s32[3]{0:T(128)} %get-tuple-element.19.info_ref, bf16[32,128,128]{2,1,0:T(8,128)(2,1)} %get-tuple-element.20.refs_0_, bf16[208,128,128]{2,1,0:T(8,128)(2,1)} %collective-permute-done.refs_1_, bf16[32,128,128]{2,1,0:T(8,128)(2,1)} %collective-permute-done.1.refs_2_, ...), custom_call_target="tpu_custom_call", output_to_operand_aliasing={{}: (10, {})} | custom-call | flops 4194304000 | bytes 6291456 | tf_op jit(solution)/shard_map/attend/pallas_call | solution.py:239
  (41 shorter events, 6.4 us)
Async XLA Ops:
  16.7 222.9 %collective-permute-start = (bf16[208,128,128]{2,1,0:T(8,128)(2,1)}, bf16[208,128,128]{2,1,0:T(8,128)(2,1)}, u32[]{:S(2)}, u32[]{:S(2)}) collective-permute-start(bf16[208,128,128]{2,1,0:T(8,128)(2,1)} %get-tuple-element.21), channel_id=1, source_target_pairs={{0,1},{1,0},{2,3},{3,2},{4,5},{5,4},{6,7},{7,6}} | collective-permute-start | bytes 20447240 | tf_op jit(solution)/shard_map/ppermute | solution.py:294
  26.1 37.4 %copy-start.4 = (bf16[256,4,128]{2,1,0:T(4,128)(2,1)}, bf16[256,4,128]{2,1,0:T(4,128)(2,1)S(1)}, u32[]{:S(2)}) copy-start(bf16[256,4,128]{2,1,0:T(4,128)(2,1)S(1)} %constant_dynamic-update-slice_fusion) | copy-start | bytes 786436
  26.1 9.5 %collective-permute-start.3 = (bf16[256,4,128]{2,1,0:T(4,128)(2,1)S(1)}, bf16[256,4,128]{2,1,0:T(4,128)(2,1)S(1)}, u32[]{:S(2)}, u32[]{:S(2)}) collective-permute-start(bf16[256,4,128]{2,1,0:T(4,128)(2,1)S(1)} %constant_dynamic-update-slice_fusion), channel_id=1, source_target_pairs={{0,4},{4,0},{1,5},{5,1},{2,6},{6,2},{3,7},{7,3}} | collective-permute-start | bytes 786440 | tf_op jit(solution)/shard_map/ppermute | solution.py:279
  35.6 0.7 copy-start
  37.5 3.3 collective-permute-start.4
  37.5 6.5 %collective-permute-start.5 = (bf16[128,4,128]{2,1,0:T(4,128)(2,1)S(1)}, bf16[128,4,128]{2,1,0:T(4,128)(2,1)}, u32[]{:S(2)}, u32[]{:S(2)}) collective-permute-start(bf16[128,4,128]{2,1,0:T(4,128)(2,1)S(1)} %get-tuple-element.35), channel_id=1, source_target_pairs={{0,2},{1,3},{2,0},{3,1},{4,6},{5,7},{6,4},{7,5}} | collective-permute-start | bytes 393224 | tf_op jit(solution)/shard_map/ppermute | solution.py:288
  39.2 18.6 %collective-permute-start.19 = (bf16[16,128,128]{2,1,0:T(8,128)(2,1)}, bf16[16,128,128]{2,1,0:T(8,128)(2,1)S(1)}, u32[]{:S(2)}, u32[]{:S(2)}) collective-permute-start(bf16[16,128,128]{2,1,0:T(8,128)(2,1)} %get-tuple-element.32.refs_0_), channel_id=1, source_target_pairs={{0,2},{1,3},{2,0},{3,1},{4,6},{5,7},{6,4},{7,5}} | collective-permute-start | bytes 1572872 | tf_op jit(solution)/shard_map/ppermute | solution.py:292
  39.6 17.6 %collective-permute-start.6 = (bf16[128,4,128]{2,1,0:T(4,128)(2,1)S(1)}, bf16[128,4,128]{2,1,0:T(4,128)(2,1)S(1)}, u32[]{:S(2)}, u32[]{:S(2)}) collective-permute-start(bf16[128,4,128]{2,1,0:T(4,128)(2,1)S(1)} %get-tuple-element.33), channel_id=1, source_target_pairs={{0,3},{1,2},{2,1},{3,0},{4,7},{5,6},{6,5},{7,4}} | collective-permute-start | bytes 393224 | tf_op jit(solution)/shard_map/ppermute | solution.py:288
  40.8 0.7 copy-start.5
  40.8 39.7 %collective-permute-start.16 = (bf16[32,128,128]{2,1,0:T(8,128)(2,1)}, bf16[32,128,128]{2,1,0:T(8,128)(2,1)}, u32[]{:S(2)}, u32[]{:S(2)}) collective-permute-start(bf16[32,128,128]{2,1,0:T(8,128)(2,1)} %get-tuple-element.31.refs_0_), channel_id=1, source_target_pairs={{0,2},{1,3},{2,0},{3,1},{4,6},{5,7},{6,4},{7,5}} | collective-permute-start | bytes 3145736 | tf_op jit(solution)/shard_map/ppermute | solution.py:292
  44.0 15.2 %collective-permute-start.18 = (bf16[16,128,128]{2,1,0:T(8,128)(2,1)}, bf16[16,128,128]{2,1,0:T(8,128)(2,1)S(1)}, u32[]{:S(2)}, u32[]{:S(2)}) collective-permute-start(bf16[16,128,128]{2,1,0:T(8,128)(2,1)} %get-tuple-element.32.refs_0_), channel_id=1, source_target_pairs={{0,1},{1,0},{2,3},{3,2},{4,5},{5,4},{6,7},{7,6}} | collective-permute-start | bytes 1572872 | tf_op jit(solution)/shard_map/ppermute | solution.py:294
  57.2 0.7 copy-start.6
  57.2 25.1 %collective-permute-start.15 = (bf16[32,128,128]{2,1,0:T(8,128)(2,1)}, bf16[32,128,128]{2,1,0:T(8,128)(2,1)}, u32[]{:S(2)}, u32[]{:S(2)}) collective-permute-start(bf16[32,128,128]{2,1,0:T(8,128)(2,1)} %get-tuple-element.31.refs_0_), channel_id=1, source_target_pairs={{0,1},{1,0},{2,3},{3,2},{4,5},{5,4},{6,7},{7,6}} | collective-permute-start | bytes 3145736 | tf_op jit(solution)/shard_map/ppermute | solution.py:294
  57.8 0.8 copy-start.1
  58.6 2.4 collective-permute-start.20
  59.2 1.8 copy-start.2
  59.2 77.5 %collective-permute-start.13 = (bf16[48,128,128]{2,1,0:T(8,128)(2,1)}, bf16[48,128,128]{2,1,0:T(8,128)(2,1)}, u32[]{:S(2)}, u32[]{:S(2)}) collective-permute-start(bf16[48,128,128]{2,1,0:T(8,128)(2,1)} %get-tuple-element.30.refs_0_), channel_id=1, source_target_pairs={{0,2},{1,3},{2,0},{3,1},{4,6},{5,7},{6,4},{7,5}} | collective-permute-start | bytes 4718600 | tf_op jit(solution)/shard_map/ppermute | solution.py:292
  61.0 0.8 copy-start.3
  61.8 74.9 %collective-permute-start.7 = (bf16[32,128,128]{2,1,0:T(8,128)(2,1)}, bf16[32,128,128]{2,1,0:T(8,128)(2,1)}, u32[]{:S(2)}, u32[]{:S(2)}) collective-permute-start(bf16[32,128,128]{2,1,0:T(8,128)(2,1)} %get-tuple-element.27.refs_0_), channel_id=1, source_target_pairs={{0,2},{1,3},{2,0},{3,1},{4,6},{5,7},{6,4},{7,5}} | collective-permute-start | bytes 3145736 | tf_op jit(solution)/shard_map/ppermute | solution.py:292
  80.5 89.9 %collective-permute-start.11 = (bf16[48,128,128]{2,1,0:T(8,128)(2,1)}, bf16[48,128,128]{2,1,0:T(8,128)(2,1)}, u32[]{:S(2)}, u32[]{:S(2)}) collective-permute-start(bf16[48,128,128]{2,1,0:T(8,128)(2,1)} %get-tuple-element.29.refs_0_), channel_id=1, source_target_pairs={{0,2},{1,3},{2,0},{3,1},{4,6},{5,7},{6,4},{7,5}} | collective-permute-start | bytes 4718600 | tf_op jit(solution)/shard_map/ppermute | solution.py:292
  82.2 121.9 %collective-permute-start.9 = (bf16[48,128,128]{2,1,0:T(8,128)(2,1)}, bf16[48,128,128]{2,1,0:T(8,128)(2,1)}, u32[]{:S(2)}, u32[]{:S(2)}) collective-permute-start(bf16[48,128,128]{2,1,0:T(8,128)(2,1)} %get-tuple-element.28.refs_0_), channel_id=1, source_target_pairs={{0,2},{1,3},{2,0},{3,1},{4,6},{5,7},{6,4},{7,5}} | collective-permute-start | bytes 4718600 | tf_op jit(solution)/shard_map/ppermute | solution.py:292
  136.7 74.5 %collective-permute-start.17 = (bf16[32,128,128]{2,1,0:T(8,128)(2,1)}, bf16[32,128,128]{2,1,0:T(8,128)(2,1)}, u32[]{:S(2)}, u32[]{:S(2)}) collective-permute-start(bf16[32,128,128]{2,1,0:T(8,128)(2,1)} %collective-permute-done.16.refs_2_), channel_id=1, source_target_pairs={{0,1},{1,0},{2,3},{3,2},{4,5},{5,4},{6,7},{7,6}} | collective-permute-start | bytes 3145736 | tf_op jit(solution)/shard_map/ppermute | solution.py:297
  136.7 102.4 %collective-permute-start.14 = (bf16[48,128,128]{2,1,0:T(8,128)(2,1)}, bf16[48,128,128]{2,1,0:T(8,128)(2,1)}, u32[]{:S(2)}, u32[]{:S(2)}) collective-permute-start(bf16[48,128,128]{2,1,0:T(8,128)(2,1)} %collective-permute-done.13.refs_2_), channel_id=1, source_target_pairs={{0,1},{1,0},{2,3},{3,2},{4,5},{5,4},{6,7},{7,6}} | collective-permute-start | bytes 4718600 | tf_op jit(solution)/shard_map/ppermute | solution.py:297
  170.4 68.7 %collective-permute-start.1 = (bf16[32,128,128]{2,1,0:T(8,128)(2,1)}, bf16[32,128,128]{2,1,0:T(8,128)(2,1)}, u32[]{:S(2)}, u32[]{:S(2)}) collective-permute-start(bf16[32,128,128]{2,1,0:T(8,128)(2,1)} %get-tuple-element.20.refs_0_), channel_id=1, source_target_pairs={{0,2},{1,3},{2,0},{3,1},{4,6},{5,7},{6,4},{7,5}} | collective-permute-start | bytes 3145736 | tf_op jit(solution)/shard_map/ppermute | solution.py:292
  204.1 59.3 %collective-permute-start.12 = (bf16[48,128,128]{2,1,0:T(8,128)(2,1)}, bf16[48,128,128]{2,1,0:T(8,128)(2,1)}, u32[]{:S(2)}, u32[]{:S(2)}) collective-permute-start(bf16[48,128,128]{2,1,0:T(8,128)(2,1)} %collective-permute-done.11.refs_2_), channel_id=1, source_target_pairs={{0,1},{1,0},{2,3},{3,2},{4,5},{5,4},{6,7},{7,6}} | collective-permute-start | bytes 4718600 | tf_op jit(solution)/shard_map/ppermute | solution.py:297
  211.2 75.9 %collective-permute-start.10 = (bf16[48,128,128]{2,1,0:T(8,128)(2,1)}, bf16[48,128,128]{2,1,0:T(8,128)(2,1)}, u32[]{:S(2)}, u32[]{:S(2)}) collective-permute-start(bf16[48,128,128]{2,1,0:T(8,128)(2,1)} %collective-permute-done.9.refs_2_), channel_id=1, source_target_pairs={{0,1},{1,0},{2,3},{3,2},{4,5},{5,4},{6,7},{7,6}} | collective-permute-start | bytes 4718600 | tf_op jit(solution)/shard_map/ppermute | solution.py:297
  239.1 72.0 %collective-permute-start.8 = (bf16[32,128,128]{2,1,0:T(8,128)(2,1)}, bf16[32,128,128]{2,1,0:T(8,128)(2,1)}, u32[]{:S(2)}, u32[]{:S(2)}) collective-permute-start(bf16[32,128,128]{2,1,0:T(8,128)(2,1)} %collective-permute-done.7.refs_2_), channel_id=1, source_target_pairs={{0,1},{1,0},{2,3},{3,2},{4,5},{5,4},{6,7},{7,6}} | collective-permute-start | bytes 3145736 | tf_op jit(solution)/shard_map/ppermute | solution.py:297
  239.2 89.1 %collective-permute-start.2 = (bf16[32,128,128]{2,1,0:T(8,128)(2,1)}, bf16[32,128,128]{2,1,0:T(8,128)(2,1)}, u32[]{:S(2)}, u32[]{:S(2)}) collective-permute-start(bf16[32,128,128]{2,1,0:T(8,128)(2,1)} %collective-permute-done.1.refs_2_), channel_id=1, source_target_pairs={{0,1},{1,0},{2,3},{3,2},{4,5},{5,4},{6,7},{7,6}} | collective-permute-start | bytes 3145736 | tf_op jit(solution)/shard_map/ppermute | solution.py:297

commit v4 on v3

--- a/solution.py
+++ b/solution.py
@@ -13,7 +13,6 @@
 NORM_ROWS = 16
 ATTEND_ROWS = 16
 GROUP = 16
-ATTEND_VMEM = 67043328
 SCORE_BOUND = 1e8
 VALUE_BOUND = 1e20
 SUM_RANGE = (1e-10, 1e15)
@@ -21,7 +20,7 @@
 NT = (((1,), (1,)), ((), ()))
 f32, bf16 = jnp.float32, jnp.bfloat16
 dot = functools.partial(lax.dot_general, preferred_element_type=f32)
-VMEM_LIMIT = pltpu.CompilerParams(vmem_limit_bytes=67043328)
+VMEM_LIMIT = pltpu.CompilerParams(vmem_limit_bytes=57 * 1024 * 1024)
 
 
 def whole(shape):
@@ -60,7 +59,8 @@
     )(*args)
 
 
-def norm_kernel(places, z_ref, gamma_ref, beta_ref, wb_ref, *out_refs):
+def norm_kernel(places, aliased, z_ref, gamma_ref, beta_ref, wb_ref, *out_refs):
+    out_refs = out_refs[1:] if aliased else out_refs
     rows, cols, chan = z_ref.shape
     b_ref = out_refs[len(places)]
     z = z_ref[...].reshape(rows * cols, chan)
@@ -81,8 +81,8 @@
         b_ref[r] = b[:, r * cols:(r + 1) * cols].astype(bf16)
 
 
-def normalize(z, gamma, beta, wb_t, start, chunks, joined):
-    cols, chan = z.shape[1:]
+def normalize(z, gamma, beta, wb_t, prev, start, chunks, joined):
+    total, cols, chan = z.shape
     heads = wb_t.shape[0]
     step = NORM_ROWS
     first = start // step
@@ -93,24 +93,29 @@
         steps = max(c // step, 1)
         places.append((lo, steps, offset))
         specs.append(pl.BlockSpec((min(step, c), cols, chan), lambda i, lo=lo, steps=steps: (jnp.clip(i - lo, 0, steps - 1), 0, 0)))
-    specs.append(pl.BlockSpec((step, heads, cols), lambda i: (i, 0, 0)))
-    shapes = [jax.ShapeDtypeStruct((c, cols, chan), bf16) for c in chunks] + [jax.ShapeDtypeStruct((rows, heads, cols), bf16)]
+    specs.append(pl.BlockSpec((step, heads, cols), lambda i: (first + i, 0, 0)))
+    shapes = [jax.ShapeDtypeStruct((c, cols, chan), bf16) for c in chunks] + [jax.ShapeDtypeStruct((total, heads, cols), bf16)]
     if joined:
         specs.append(pl.BlockSpec((step, cols, chan), lambda i: (i, 0, 0)))
         shapes.append(jax.ShapeDtypeStruct((rows, cols, chan), bf16))
+    args = [z, gamma, beta, wb_t]
+    in_specs = [pl.BlockSpec((step, cols, chan), lambda i: (first + i, 0, 0))] + [whole(x.shape) for x in args[1:]]
+    alias = {}
+    if prev is not None:
+        alias = {len(args): len(chunks)}
+        args.append(prev)
+        in_specs.append(pl.BlockSpec(memory_space=pl.ANY))
     return pl.pallas_call(
-        functools.partial(norm_kernel, places),
+        functools.partial(norm_kernel, places, prev is not None),
         grid=(rows // step,),
-        in_specs=[
-            pl.BlockSpec((step, cols, chan), lambda i: (first + i, 0, 0)),
-            whole((1, chan)), whole((1, chan)), whole(wb_t.shape),
-        ],
+        in_specs=in_specs,
         out_specs=specs,
         out_shape=shapes,
+        input_output_aliases=alias,
         compiler_params=VMEM_LIMIT,
         cost_estimate=pl.CostEstimate(flops=rows * cols * chan * 300, bytes_accessed=rows * cols * chan * 4, transcendentals=0),
         name="norm",
-    )(z, gamma, beta, wb_t)
+    )(*args)
 
 
 def bias_kernel(info_ref, *refs):
@@ -252,7 +257,7 @@
         ),
         out_shape=jax.ShapeDtypeStruct(z.shape, z.dtype),
         input_output_aliases=alias,
-        compiler_params=pltpu.CompilerParams(vmem_limit_bytes=ATTEND_VMEM),
+        compiler_params=VMEM_LIMIT,
         cost_estimate=pl.CostEstimate(flops=rows * cols * chan * 8000, bytes_accessed=rows * cols * chan * 12, transcendentals=0),
         name="attend",
     )(*args)
@@ -271,11 +276,10 @@
         col_idx = lax.axis_index('col')
         gamma, beta, wb_t = ln_gamma.reshape(1, chan), ln_beta.reshape(1, chan), w_b.T
         starts = [sum(CHUNKS[:i]) for i in range(len(CHUNKS))]
-        first, first_bias = normalize(z, gamma, beta, wb_t, 0, CHUNKS[:1], False)
-        second, second_bias = normalize(z, gamma, beta, wb_t, starts[1], CHUNKS[1:2], False)
-        *others, other_bias, rest = normalize(z, gamma, beta, wb_t, starts[2], CHUNKS[2:], True)
+        first, bias_tile = normalize(z, gamma, beta, wb_t, None, 0, CHUNKS[:1], False)
+        second, bias_tile = normalize(z, gamma, beta, wb_t, bias_tile, starts[1], CHUNKS[1:2], False)
+        *others, bias_tile, rest = normalize(z, gamma, beta, wb_t, bias_tile, starts[2], CHUNKS[2:], True)
         own = [first, second] + others
-        bias_tile = jnp.concatenate([first_bias, second_bias, other_bias], axis=0)
         other_tile = lax.ppermute(bias_tile, 'row', [(0, 1), (1, 0)])
         info, w_kv, w_qg = make_plan(heads, sizes, res_mask.reshape(4, cols), gamma, beta, w_q, w_k, w_v, wb_t, w_g)
         weights = (w_kv, w_qg, w_o)

time: 346 us -> 336 us (0.971)
  waiting for transfers between devices: 159 us -> 151 us
    ppermute x3, waiting for transfers between devices: 15.7 us -> 5.68 us  [inner(): lax.ppermute(send, 'col', [(c, c ^ m) for c in range(num_cols)])]
  transfers between devices with their start and end apart: 21 -> 21, of which waited for: 8 -> 9; matrix products, arithmetic and copies ran while one was open for 2% -> 1% of each run, Pallas kernels for 37% -> 36%
where the time goes in v4:
time: 336 us; the launch traced here: 335 us
  Pallas kernels  162 us (48%)
  waiting for transfers between devices  151 us (45%)
  starting transfers between devices  17.6 us (5%)
    ppermute x7, waiting for transfers between devices, inner(): far.append(lax.ppermute(a, 'col', x_pairs))  138 us
    pallas_call x7, Pallas kernels, attend(): pl.pallas_call(functools.partial(attend_kernel, heads, sizes), grid_spec=...  133 us
    pallas_call x3, Pallas kernels, normalize(): pl.pallas_call(functools.partial(norm_kernel, places, prev is not None),...  22.8 us
    ppermute x7, starting transfers between devices, inner(): far.append(lax.ppermute(a, 'col', x_pairs))  9.47 us
  transfers between devices with their start and end apart: 21, of which 9 were waited for; matrix products, arithmetic and copies ran while one was open for 1% of the time, Pallas kernels for 36%

profile of v4, /device:TPU:0, one launch (start us, length us, event | category | flops | bytes accessed | tf_op | source)
XLA Modules:
  0.0 334.9 jit_solution(15332227763850672835)
XLA Ops:
  0.0 2.4 norm.3
  2.4 3.6 %norm.4 = (bf16[32,128,128]{2,1,0:T(8,128)(2,1)}, bf16[256,4,128]{2,1,0:T(4,128)(2,1)}) custom-call(bf16[256,128,128]{2,1,0:T(8,128)(2,1)} %refs_4_.13, f32[1,128]{1,0:T(1,128)} %bitcast.9, f32[1,128]{1,0:T(1,128)} %bitcast.13, bf16[4,128]{1,0:T(4,128)(2,1)} %bitcast.5, ...), custom_call_target="tpu_custom_call", output_to_operand_aliasing={{1}: (4, {})} | custom-call | flops 157286400 | bytes 2097152 | tf_op jit(solution)/shard_map/norm/pallas_call | solution.py:108
  6.0 16.8 %norm.5 = (bf16[48,128,128]{2,1,0:T(8,128)(2,1)}, bf16[48,128,128]{2,1,0:T(8,128)(2,1)}, bf16[48,128,128]{2,1,0:T(8,128)(2,1)}, bf16[32,128,128]{2,1,0:T(8,128)(...) custom-call(bf16[256,128,128]{2,1,0:T(8,128)(2,1)} %refs_4_.13, ...), custom_call_target="tpu_custom_call", output_to_operand_aliasing={{5}: (4, {})} | custom-call | flops 1022361600 | bytes 13631488 | tf_op jit(solution)/shard_map/norm/pallas_call | solution.py:108
  22.8 0.8 collective-permute-start
  23.6 2.5 collective-permute-start.3
  26.2 1.5 collective-permute-start.19
  27.6 5.7 %collective-permute-done.3 = bf16[256,4,128]{2,1,0:T(4,128)(2,1)S(1)} collective-permute-done((bf16[256,4,128]{2,1,0:T(4,128)(2,1)}, bf16[256,4,128]{2,1,0:T(4,128)(2,1)S(1)}, u32[]{:S(2)}, u32[]{:S(2)}) %collective-permute-start.3) | collective-permute-done | bytes 262176 | tf_op jit(solution)/shard_map/ppermute | solution.py:283
  33.3 1.8 select_select_fusion
  35.1 1.7 collective-permute-start.5
  36.9 1.1 select_select_fusion.2
  38.4 5.4 %collective-permute-done.5.refs_2_ = bf16[128,4,128]{2,1,0:T(4,128)(2,1)S(1)} collective-permute-done((bf16[128,4,128]{2,1,0:T(4,128)(2,1)S(1)}, bf16[128,4,128]{2,1,0:T(4,128)(2,1)S(1)}, u32[]{:S(2)}, u32[]{:S(2)}) %collective-permute-start.5) | collective-permute-done | bytes 131104 | tf_op jit(solution)/shard_map/ppermute | solution.py:292
  43.8 1.5 collective-permute-start.16
  46.9 1.0 collective-permute-done.18.refs_1_
  47.9 1.5 collective-permute-start.13
  50.2 1.5 collective-permute-start.7
  51.7 18.2 %collective-permute-done.16.refs_2_ = bf16[32,128,128]{2,1,0:T(8,128)(2,1)} collective-permute-done((bf16[32,128,128]{2,1,0:T(8,128)(2,1)S(1)}, bf16[32,128,128]{2,1,0:T(8,128)(2,1)}, u32[]{:S(2)}, u32[]{:S(2)}) %collective-permute-start.16) | collective-permute-done | bytes 1048608 | tf_op jit(solution)/shard_map/ppermute | solution.py:296
  69.9 1.5 collective-permute-start.11
  71.9 54.1 %collective-permute-done.7.refs_2_ = bf16[32,128,128]{2,1,0:T(8,128)(2,1)} collective-permute-done((bf16[32,128,128]{2,1,0:T(8,128)(2,1)}, bf16[32,128,128]{2,1,0:T(8,128)(2,1)}, u32[]{:S(2)}, u32[]{:S(2)}) %collective-permute-start.7) | collective-permute-done | bytes 1048608 | tf_op jit(solution)/shard_map/ppermute | solution.py:296
  126.6 33.0 %collective-permute-done.11.refs_2_ = bf16[48,128,128]{2,1,0:T(8,128)(2,1)S(1)} collective-permute-done((bf16[48,128,128]{2,1,0:T(8,128)(2,1)}, bf16[48,128,128]{2,1,0:T(8,128)(2,1)S(1)}, u32[]{:S(2)}, u32[]{:S(2)}) %collective-permute-start.11) | collective-permute-done | bytes 1572896 | tf_op jit(solution)/shard_map/ppermute | solution.py:296
  159.7 1.5 collective-permute-start.1
  161.2 32.2 %collective-permute-done.9.refs_2_ = bf16[48,128,128]{2,1,0:T(8,128)(2,1)S(1)} collective-permute-done((bf16[48,128,128]{2,1,0:T(8,128)(2,1)}, bf16[48,128,128]{2,1,0:T(8,128)(2,1)S(1)}, u32[]{:S(2)}, u32[]{:S(2)}) %collective-permute-start.9) | collective-permute-done | bytes 1572896 | tf_op jit(solution)/shard_map/ppermute | solution.py:296
  193.4 2.0 plan.1
  195.4 3.6 %bias.1.refs_5_ = f32[512,512]{1,0:T(8,128)} custom-call(s32[3]{0:T(128)} %get-tuple-element.19.info_ref, bf16[128,4,128]{2,1,0:T(4,128)(2,1)} %get-tuple-element.35.refs_0_, bf16[128,4,128]{2,1,0:T(4,128)(2,1)} %copy-done.13, bf16[128,4,128]{2,1,0:T(4,128)(2,1)} %copy-done.11, bf16[128,4,128]{2,1,0:T(4,128)(2,1)} %copy-done.12), custom_call_target="tpu_custom_call" | custom-call | tf_op jit(solution)/shard_map/bias/pallas_call | solution.py:137
  199.2 10.1 %attend.7.refs_9_ = bf16[256,128,128]{2,1,0:T(8,128)(2,1)} custom-call(s32[3]{0:T(128)} %get-tuple-element.19.info_ref, bf16[16,128,128]{2,1,0:T(8,128)(2,1)} %get-tuple-element.32.refs_0_, bf16[16,128,128]{2,1,0:T(8,128)(2,1)} %copy-done.9, bf16[16,128,128]{2,1,0:T(8,128)(2,1)} %copy-done.8, bf16[16,128,128]{2,1,0:T(8,128)(2,1)} %copy-done.10, ...), custom_call_target="tpu_custom_call" | custom-call | flops 2097152000 | bytes 3145728 | tf_op jit(solution)/shard_map/attend/pallas_call | solution.py:244
  209.2 17.3 %attend.8.refs_9_ = bf16[256,128,128]{2,1,0:T(8,128)(2,1)} custom-call(s32[3]{0:T(128)} %get-tuple-element.19.info_ref, bf16[32,128,128]{2,1,0:T(8,128)(2,1)} %get-tuple-element.31.refs_0_, bf16[32,128,128]{2,1,0:T(8,128)(2,1)} %copy-done.5, bf16[32,128,128]{2,1,0:T(8,128)(2,1)} %collective-permute-done.16.refs_2_, ...), custom_call_target="tpu_custom_call", output_to_operand_aliasing={{}: (10, {})} | custom-call | flops 4194304000 | bytes 6291456 | tf_op jit(solution)/shard_map/attend/pallas_call | solution.py:244
  227.1 0.9 copy-done.3
  228.0 23.7 %attend.9.refs_9_ = bf16[256,128,128]{2,1,0:T(8,128)(2,1)} custom-call(s32[3]{0:T(128)} %get-tuple-element.19.info_ref, bf16[48,128,128]{2,1,0:T(8,128)(2,1)} %get-tuple-element.30.refs_0_, bf16[208,128,128]{2,1,0:T(8,128)(2,1)} %collective-permute-done.refs_1_, bf16[48,128,128]{2,1,0:T(8,128)(2,1)} %copy-done, ...), custom_call_target="tpu_custom_call", output_to_operand_aliasing={{}: (10, {})} | custom-call | flops 6291456000 | bytes 9437184 | tf_op jit(solution)/shard_map/attend/pallas_call | solution.py:244
  251.8 23.7 %attend.10.refs_9_ = bf16[256,128,128]{2,1,0:T(8,128)(2,1)} custom-call(s32[3]{0:T(128)} %get-tuple-element.19.info_ref, bf16[48,128,128]{2,1,0:T(8,128)(2,1)} %get-tuple-element.29.refs_0_, bf16[208,128,128]{2,1,0:T(8,128)(2,1)} %collective-permute-done.refs_1_, bf16[48,128,128]{2,1,0:T(8,128)(2,1)} %copy-done.2, ...), custom_call_target="tpu_custom_call", output_to_operand_aliasing={{}: (10, {})} | custom-call | flops 6291456000 | bytes 9437184 | tf_op jit(solution)/shard_map/attend/pallas_call | solution.py:244
  275.5 24.1 %attend.11.refs_9_ = bf16[256,128,128]{2,1,0:T(8,128)(2,1)} custom-call(s32[3]{0:T(128)} %get-tuple-element.19.info_ref, bf16[48,128,128]{2,1,0:T(8,128)(2,1)} %get-tuple-element.28.refs_0_, bf16[208,128,128]{2,1,0:T(8,128)(2,1)} %collective-permute-done.refs_1_, bf16[48,128,128]{2,1,0:T(8,128)(2,1)} %copy-done.1, ...), custom_call_target="tpu_custom_call", output_to_operand_aliasing={{}: (10, {})} | custom-call | flops 6291456000 | bytes 9437184 | tf_op jit(solution)/shard_map/attend/pallas_call | solution.py:244
  299.6 17.2 %attend.12.refs_9_ = bf16[256,128,128]{2,1,0:T(8,128)(2,1)} custom-call(s32[3]{0:T(128)} %get-tuple-element.19.info_ref, bf16[32,128,128]{2,1,0:T(8,128)(2,1)} %get-tuple-element.27.refs_0_, bf16[208,128,128]{2,1,0:T(8,128)(2,1)} %collective-permute-done.refs_1_, ...), custom_call_target="tpu_custom_call", output_to_operand_aliasing={{}: (10, {})} | custom-call | flops 4194304000 | bytes 6291456 | tf_op jit(solution)/shard_map/attend/pallas_call | solution.py:244
  316.8 1.0 copy-done.6
  317.8 17.1 %attend.13 = bf16[256,128,128]{2,1,0:T(8,128)(2,1)} custom-call(s32[3]{0:T(128)} %get-tuple-element.19.info_ref, bf16[32,128,128]{2,1,0:T(8,128)(2,1)} %get-tuple-element.22.refs_0_, bf16[208,128,128]{2,1,0:T(8,128)(2,1)} %collective-permute-done.refs_1_, bf16[32,128,128]{2,1,0:T(8,128)(2,1)} %collective-permute-done.1.refs_2_, ...), custom_call_target="tpu_custom_call", output_to_operand_aliasing={{}: (10, {})} | custom-call | flops 4194304000 | bytes 6291456 | tf_op jit(solution)/shard_map/attend/pallas_call | solution.py:244
  (52 shorter events, 4.7 us)
Async XLA Ops:
  2.4 23.8 %copy-start.7 = (bf16[16,128,128]{2,1,0:T(8,128)(2,1)S(1)}, bf16[16,128,128]{2,1,0:T(8,128)(2,1)}, u32[]{:S(2)}) copy-start(bf16[16,128,128]{2,1,0:T(8,128)(2,1)} %get-tuple-element.32.refs_0_) | copy-start | bytes 1572868
  6.0 37.8 %copy-start.4 = (bf16[32,128,128]{2,1,0:T(8,128)(2,1)S(1)}, bf16[32,128,128]{2,1,0:T(8,128)(2,1)}, u32[]{:S(2)}) copy-start(bf16[32,128,128]{2,1,0:T(8,128)(2,1)} %get-tuple-element.31.refs_0_) | copy-start | bytes 3145732
  22.8 204.3 %collective-permute-start = (bf16[208,128,128]{2,1,0:T(8,128)(2,1)}, bf16[208,128,128]{2,1,0:T(8,128)(2,1)}, u32[]{:S(2)}, u32[]{:S(2)}) collective-permute-start(bf16[208,128,128]{2,1,0:T(8,128)(2,1)} %get-tuple-element.23), channel_id=1, source_target_pairs={{0,1},{1,0},{2,3},{3,2},{4,5},{5,4},{6,7},{7,6}} | collective-permute-start | bytes 20447240 | tf_op jit(solution)/shard_map/ppermute | solution.py:298
  23.6 9.7 %collective-permute-start.3 = (bf16[256,4,128]{2,1,0:T(4,128)(2,1)}, bf16[256,4,128]{2,1,0:T(4,128)(2,1)S(1)}, u32[]{:S(2)}, u32[]{:S(2)}) collective-permute-start(bf16[256,4,128]{2,1,0:T(4,128)(2,1)} %get-tuple-element.24), channel_id=1, source_target_pairs={{0,4},{4,0},{1,5},{5,1},{2,6},{6,2},{3,7},{7,3}} | collective-permute-start | bytes 786440 | tf_op jit(solution)/shard_map/ppermute | solution.py:283
  26.2 20.3 %collective-permute-start.19 = (bf16[16,128,128]{2,1,0:T(8,128)(2,1)S(1)}, bf16[16,128,128]{2,1,0:T(8,128)(2,1)S(1)}, u32[]{:S(2)}, u32[]{:S(2)}) collective-permute-start(bf16[16,128,128]{2,1,0:T(8,128)(2,1)S(1)} %copy-done.7), channel_id=1, source_target_pairs={{0,2},{1,3},{2,0},{3,1},{4,6},{5,7},{6,4},{7,5}} | collective-permute-start | bytes 1572872 | tf_op jit(solution)/shard_map/ppermute | solution.py:296
  35.1 8.6 %collective-permute-start.5 = (bf16[128,4,128]{2,1,0:T(4,128)(2,1)S(1)}, bf16[128,4,128]{2,1,0:T(4,128)(2,1)S(1)}, u32[]{:S(2)}, u32[]{:S(2)}) collective-permute-start(bf16[128,4,128]{2,1,0:T(4,128)(2,1)S(1)} %get-tuple-element.34), channel_id=1, source_target_pairs={{0,2},{1,3},{2,0},{3,1},{4,6},{5,7},{6,4},{7,5}} | collective-permute-start | bytes 393224 | tf_op jit(solution)/shard_map/ppermute | solution.py:292
  36.9 8.7 %collective-permute-start.6 = (bf16[128,4,128]{2,1,0:T(4,128)(2,1)S(1)}, bf16[128,4,128]{2,1,0:T(4,128)(2,1)S(1)}, u32[]{:S(2)}, u32[]{:S(2)}) collective-permute-start(bf16[128,4,128]{2,1,0:T(4,128)(2,1)S(1)} %get-tuple-element.33), channel_id=1, source_target_pairs={{0,3},{1,2},{2,1},{3,0},{4,7},{5,6},{6,5},{7,4}} | collective-permute-start | bytes 393224 | tf_op jit(solution)/shard_map/ppermute | solution.py:292
  38.0 8.4 %collective-permute-start.4 = (bf16[128,4,128]{2,1,0:T(4,128)(2,1)S(1)}, bf16[128,4,128]{2,1,0:T(4,128)(2,1)S(1)}, u32[]{:S(2)}, u32[]{:S(2)}) collective-permute-start(bf16[128,4,128]{2,1,0:T(4,128)(2,1)S(1)} %select_select_fusion.2), channel_id=1, source_target_pairs={{0,1},{1,0},{2,3},{3,2},{4,5},{5,4},{6,7},{7,6}} | collective-permute-start | bytes 393224 | tf_op jit(solution)/shard_map/ppermute | solution.py:292
  43.8 151.6 %copy-start.11 = (bf16[128,4,128]{2,1,0:T(4,128)(2,1)}, bf16[128,4,128]{2,1,0:T(4,128)(2,1)S(1)}, u32[]{:S(2)}) copy-start(bf16[128,4,128]{2,1,0:T(4,128)(2,1)S(1)} %collective-permute-done.5.refs_2_) | copy-start | bytes 393220
  43.8 26.1 %collective-permute-start.16 = (bf16[32,128,128]{2,1,0:T(8,128)(2,1)S(1)}, bf16[32,128,128]{2,1,0:T(8,128)(2,1)}, u32[]{:S(2)}, u32[]{:S(2)}) collective-permute-start(bf16[32,128,128]{2,1,0:T(8,128)(2,1)S(1)} %copy-done.4), channel_id=1, source_target_pairs={{0,2},{1,3},{2,0},{3,1},{4,6},{5,7},{6,4},{7,5}} | collective-permute-start | bytes 3145736 | tf_op jit(solution)/shard_map/ppermute | solution.py:296
  45.6 149.8 %copy-start.12 = (bf16[128,4,128]{2,1,0:T(4,128)(2,1)}, bf16[128,4,128]{2,1,0:T(4,128)(2,1)S(1)}, u32[]{:S(2)}) copy-start(bf16[128,4,128]{2,1,0:T(4,128)(2,1)S(1)} %collective-permute-done.6.refs_3_) | copy-start | bytes 393220
  45.6 2.4 collective-permute-start.18
  46.4 149.0 %copy-start.13 = (bf16[128,4,128]{2,1,0:T(4,128)(2,1)}, bf16[128,4,128]{2,1,0:T(4,128)(2,1)S(1)}, u32[]{:S(2)}) copy-start(bf16[128,4,128]{2,1,0:T(4,128)(2,1)S(1)} %collective-permute-done.4.refs_1_) | copy-start | bytes 393220
  46.4 25.0 %collective-permute-start.15 = (bf16[32,128,128]{2,1,0:T(8,128)(2,1)S(1)}, bf16[32,128,128]{2,1,0:T(8,128)(2,1)S(1)}, u32[]{:S(2)}, u32[]{:S(2)}) collective-permute-start(bf16[32,128,128]{2,1,0:T(8,128)(2,1)S(1)} %copy-done.4), channel_id=1, source_target_pairs={{0,1},{1,0},{2,3},{3,2},{4,5},{5,4},{6,7},{7,6}} | collective-permute-start | bytes 3145736 | tf_op jit(solution)/shard_map/ppermute | solution.py:298
  46.4 79.6 %copy-start.8 = (bf16[16,128,128]{2,1,0:T(8,128)(2,1)}, bf16[16,128,128]{2,1,0:T(8,128)(2,1)S(1)}, u32[]{:S(2)}) copy-start(bf16[16,128,128]{2,1,0:T(8,128)(2,1)S(1)} %collective-permute-done.19.refs_2_) | copy-start | bytes 1572868
  46.4 3.7 %collective-permute-start.20 = (bf16[16,128,128]{2,1,0:T(8,128)(2,1)S(1)}, bf16[16,128,128]{2,1,0:T(8,128)(2,1)S(1)}, u32[]{:S(2)}, u32[]{:S(2)}) collective-permute-start(bf16[16,128,128]{2,1,0:T(8,128)(2,1)S(1)} %collective-permute-done.19.refs_2_), channel_id=1, source_target_pairs={{0,1},{1,0},{2,3},{3,2},{4,5},{5,4},{6,7},{7,6}} | collective-permute-start | bytes 1572872 | tf_op jit(solution)/shard_map/ppermute | solution.py:301
  47.9 78.2 %copy-start.9 = (bf16[16,128,128]{2,1,0:T(8,128)(2,1)}, bf16[16,128,128]{2,1,0:T(8,128)(2,1)S(1)}, u32[]{:S(2)}) copy-start(bf16[16,128,128]{2,1,0:T(8,128)(2,1)S(1)} %collective-permute-done.18.refs_1_) | copy-start | bytes 1572868
  47.9 78.2 %collective-permute-start.13 = (bf16[48,128,128]{2,1,0:T(8,128)(2,1)}, bf16[48,128,128]{2,1,0:T(8,128)(2,1)S(1)}, u32[]{:S(2)}, u32[]{:S(2)}) collective-permute-start(bf16[48,128,128]{2,1,0:T(8,128)(2,1)} %get-tuple-element.30.refs_0_), channel_id=1, source_target_pairs={{0,2},{1,3},{2,0},{3,1},{4,6},{5,7},{6,4},{7,5}} | collective-permute-start | bytes 4718600 | tf_op jit(solution)/shard_map/ppermute | solution.py:296
  50.2 19.7 %copy-start.10 = (bf16[16,128,128]{2,1,0:T(8,128)(2,1)}, bf16[16,128,128]{2,1,0:T(8,128)(2,1)S(1)}, u32[]{:S(2)}) copy-start(bf16[16,128,128]{2,1,0:T(8,128)(2,1)S(1)} %collective-permute-done.20.refs_3_) | copy-start | bytes 1572868
  50.2 75.9 %collective-permute-start.7 = (bf16[32,128,128]{2,1,0:T(8,128)(2,1)}, bf16[32,128,128]{2,1,0:T(8,128)(2,1)}, u32[]{:S(2)}, u32[]{:S(2)}) collective-permute-start(bf16[32,128,128]{2,1,0:T(8,128)(2,1)} %get-tuple-element.27.refs_0_), channel_id=1, source_target_pairs={{0,2},{1,3},{2,0},{3,1},{4,6},{5,7},{6,4},{7,5}} | collective-permute-start | bytes 3145736 | tf_op jit(solution)/shard_map/ppermute | solution.py:296
  69.9 89.8 %collective-permute-start.11 = (bf16[48,128,128]{2,1,0:T(8,128)(2,1)}, bf16[48,128,128]{2,1,0:T(8,128)(2,1)S(1)}, u32[]{:S(2)}, u32[]{:S(2)}) collective-permute-start(bf16[48,128,128]{2,1,0:T(8,128)(2,1)} %get-tuple-element.29.refs_0_), channel_id=1, source_target_pairs={{0,2},{1,3},{2,0},{3,1},{4,6},{5,7},{6,4},{7,5}} | collective-permute-start | bytes 4718600 | tf_op jit(solution)/shard_map/ppermute | solution.py:296
  71.4 122.0 %copy-start.5 = (bf16[32,128,128]{2,1,0:T(8,128)(2,1)}, bf16[32,128,128]{2,1,0:T(8,128)(2,1)S(1)}, u32[]{:S(2)}) copy-start(bf16[32,128,128]{2,1,0:T(8,128)(2,1)S(1)} %collective-permute-done.15.refs_1_) | copy-start | bytes 3145732
  71.4 122.0 %collective-permute-start.9 = (bf16[48,128,128]{2,1,0:T(8,128)(2,1)}, bf16[48,128,128]{2,1,0:T(8,128)(2,1)S(1)}, u32[]{:S(2)}, u32[]{:S(2)}) collective-permute-start(bf16[48,128,128]{2,1,0:T(8,128)(2,1)} %get-tuple-element.28.refs_0_), channel_id=1, source_target_pairs={{0,2},{1,3},{2,0},{3,1},{4,6},{5,7},{6,4},{7,5}} | collective-permute-start | bytes 4718600 | tf_op jit(solution)/shard_map/ppermute | solution.py:296
  126.1 72.9 %collective-permute-start.17 = (bf16[32,128,128]{2,1,0:T(8,128)(2,1)}, bf16[32,128,128]{2,1,0:T(8,128)(2,1)}, u32[]{:S(2)}, u32[]{:S(2)}) collective-permute-start(bf16[32,128,128]{2,1,0:T(8,128)(2,1)} %collective-permute-done.16.refs_2_), channel_id=1, source_target_pairs={{0,1},{1,0},{2,3},{3,2},{4,5},{5,4},{6,7},{7,6}} | collective-permute-start | bytes 3145736 | tf_op jit(solution)/shard_map/ppermute | solution.py:301
  126.1 83.1 %copy-start = (bf16[48,128,128]{2,1,0:T(8,128)(2,1)}, bf16[48,128,128]{2,1,0:T(8,128)(2,1)S(1)}, u32[]{:S(2)}) copy-start(bf16[48,128,128]{2,1,0:T(8,128)(2,1)S(1)} %collective-permute-done.13.refs_2_) | copy-start | bytes 4718596
  126.1 100.8 %collective-permute-start.14 = (bf16[48,128,128]{2,1,0:T(8,128)(2,1)S(1)}, bf16[48,128,128]{2,1,0:T(8,128)(2,1)S(1)}, u32[]{:S(2)}, u32[]{:S(2)}) collective-permute-start(bf16[48,128,128]{2,1,0:T(8,128)(2,1)S(1)} %collective-permute-done.13.refs_2_), channel_id=1, source_target_pairs={{0,1},{1,0},{2,3},{3,2},{4,5},{5,4},{6,7},{7,6}} | collective-permute-start | bytes 4718600 | tf_op jit(solution)/shard_map/ppermute | solution.py:301
  159.7 49.6 %copy-start.2 = (bf16[48,128,128]{2,1,0:T(8,128)(2,1)}, bf16[48,128,128]{2,1,0:T(8,128)(2,1)S(1)}, u32[]{:S(2)}) copy-start(bf16[48,128,128]{2,1,0:T(8,128)(2,1)S(1)} %collective-permute-done.11.refs_2_) | copy-start | bytes 4718596
  159.7 66.9 %collective-permute-start.1 = (bf16[32,128,128]{2,1,0:T(8,128)(2,1)}, bf16[32,128,128]{2,1,0:T(8,128)(2,1)}, u32[]{:S(2)}, u32[]{:S(2)}) collective-permute-start(bf16[32,128,128]{2,1,0:T(8,128)(2,1)} %get-tuple-element.22.refs_0_), channel_id=1, source_target_pairs={{0,2},{1,3},{2,0},{3,1},{4,6},{5,7},{6,4},{7,5}} | collective-permute-start | bytes 3145736 | tf_op jit(solution)/shard_map/ppermute | solution.py:296
  193.4 58.4 %collective-permute-start.12 = (bf16[48,128,128]{2,1,0:T(8,128)(2,1)S(1)}, bf16[48,128,128]{2,1,0:T(8,128)(2,1)}, u32[]{:S(2)}, u32[]{:S(2)}) collective-permute-start(bf16[48,128,128]{2,1,0:T(8,128)(2,1)S(1)} %collective-permute-done.11.refs_2_), channel_id=1, source_target_pairs={{0,1},{1,0},{2,3},{3,2},{4,5},{5,4},{6,7},{7,6}} | collective-permute-start | bytes 4718600 | tf_op jit(solution)/shard_map/ppermute | solution.py:301
  199.0 76.5 %collective-permute-start.10 = (bf16[48,128,128]{2,1,0:T(8,128)(2,1)S(1)}, bf16[48,128,128]{2,1,0:T(8,128)(2,1)}, u32[]{:S(2)}, u32[]{:S(2)}) collective-permute-start(bf16[48,128,128]{2,1,0:T(8,128)(2,1)S(1)} %collective-permute-done.9.refs_2_), channel_id=1, source_target_pairs={{0,1},{1,0},{2,3},{3,2},{4,5},{5,4},{6,7},{7,6}} | collective-permute-start | bytes 4718600 | tf_op jit(solution)/shard_map/ppermute | solution.py:301
  226.6 73.0 %collective-permute-start.8 = (bf16[32,128,128]{2,1,0:T(8,128)(2,1)}, bf16[32,128,128]{2,1,0:T(8,128)(2,1)}, u32[]{:S(2)}, u32[]{:S(2)}) collective-permute-start(bf16[32,128,128]{2,1,0:T(8,128)(2,1)} %collective-permute-done.7.refs_2_), channel_id=1, source_target_pairs={{0,1},{1,0},{2,3},{3,2},{4,5},{5,4},{6,7},{7,6}} | collective-permute-start | bytes 3145736 | tf_op jit(solution)/shard_map/ppermute | solution.py:301
  226.9 89.9 %collective-permute-start.2 = (bf16[32,128,128]{2,1,0:T(8,128)(2,1)}, bf16[32,128,128]{2,1,0:T(8,128)(2,1)S(1)}, u32[]{:S(2)}, u32[]{:S(2)}) collective-permute-start(bf16[32,128,128]{2,1,0:T(8,128)(2,1)} %collective-permute-done.1.refs_2_), channel_id=1, source_target_pairs={{0,1},{1,0},{2,3},{3,2},{4,5},{5,4},{6,7},{7,6}} | collective-permute-start | bytes 3145736 | tf_op jit(solution)/shard_map/ppermute | solution.py:301
  (3 other events, 18.0 us)

commit v5 on v4

--- a/solution.py
+++ b/solution.py
@@ -13,6 +13,7 @@
 NORM_ROWS = 16
 ATTEND_ROWS = 16
 GROUP = 16
+ATTEND_VMEM = (67043328, 40 * 1024 * 1024)
 SCORE_BOUND = 1e8
 VALUE_BOUND = 1e20
 SUM_RANGE = (1e-10, 1e15)
@@ -20,7 +21,7 @@
 NT = (((1,), (1,)), ((), ()))
 f32, bf16 = jnp.float32, jnp.bfloat16
 dot = functools.partial(lax.dot_general, preferred_element_type=f32)
-VMEM_LIMIT = pltpu.CompilerParams(vmem_limit_bytes=57 * 1024 * 1024)
+VMEM_LIMIT = pltpu.CompilerParams(vmem_limit_bytes=67043328)
 
 
 def whole(shape):
@@ -257,7 +258,7 @@
         ),
         out_shape=jax.ShapeDtypeStruct(z.shape, z.dtype),
         input_output_aliases=alias,
-        compiler_params=VMEM_LIMIT,
+        compiler_params=pltpu.CompilerParams(vmem_limit_bytes=ATTEND_VMEM[prev is not None]),
         cost_estimate=pl.CostEstimate(flops=rows * cols * chan * 8000, bytes_accessed=rows * cols * chan * 12, transcendentals=0),
         name="attend",
     )(*args)

time: 336 us -> 338 us (level)
  local copies, waits for them, and re-layouts: 2.02 us -> 11.2 us
  Pallas kernels: 162 us -> 154 us
    unnamed x28 -> x44, local copies, waits for them, and re-layouts: 2.02 us -> 11.2 us
    pallas_call x7, Pallas kernels: 133 us -> 126 us  [attend(): pl.pallas_call(functools.partial(attend_kernel, heads, sizes), grid_spec=...]
  transfers between devices with their start and end apart: 21 -> 21, of which waited for: 9 -> 9; matrix products, arithmetic and copies ran while one was open for 1% -> 1% of each run, Pallas kernels for 36% -> 34%
where the time goes in v5:
time: 338 us; the launch traced here: 337 us
  Pallas kernels  154 us (46%)
  waiting for transfers between devices  150 us (44%)
  starting transfers between devices  17.8 us (5%)
  local copies, waits for them, and re-layouts  11.2 us (3%)
    ppermute x7, waiting for transfers between devices, inner(): far.append(lax.ppermute(a, 'col', x_pairs))  137 us
    pallas_call x7, Pallas kernels, attend(): pl.pallas_call(functools.partial(attend_kernel, heads, sizes), grid_spec=...  126 us
    pallas_call x3, Pallas kernels, normalize(): pl.pallas_call(functools.partial(norm_kernel, places, prev is not None),...  22.6 us
    unnamed x44, local copies, waits for them, and re-layouts  11.2 us
    ppermute x7, starting transfers between devices, inner(): far.append(lax.ppermute(a, 'col', x_pairs))  9.47 us
  transfers between devices with their start and end apart: 21, of which 9 were waited for; matrix products, arithmetic and copies ran while one was open for 1% of the time, Pallas kernels for 34%

profile of v5, /device:TPU:0, one launch (start us, length us, event | category | flops | bytes accessed | tf_op | source)
XLA Modules:
  0.0 336.7 jit_solution(1251857413711753038)
XLA Ops:
  0.0 2.4 norm.3
  2.4 3.5 %norm.4 = (bf16[32,128,128]{2,1,0:T(8,128)(2,1)}, bf16[256,4,128]{2,1,0:T(4,128)(2,1)}) custom-call(bf16[256,128,128]{2,1,0:T(8,128)(2,1)} %refs_4_.13, f32[1,128]{1,0:T(1,128)} %bitcast.9, f32[1,128]{1,0:T(1,128)} %bitcast.13, bf16[4,128]{1,0:T(4,128)(2,1)} %bitcast.5, ...), custom_call_target="tpu_custom_call", output_to_operand_aliasing={{1}: (4, {})} | custom-call | flops 157286400 | bytes 2097152 | tf_op jit(solution)/shard_map/norm/pallas_call | solution.py:109
  5.9 16.7 %norm.5 = (bf16[48,128,128]{2,1,0:T(8,128)(2,1)}, bf16[48,128,128]{2,1,0:T(8,128)(2,1)}, bf16[48,128,128]{2,1,0:T(8,128)(2,1)}, bf16[32,128,128]{2,1,0:T(8,128)(...) custom-call(bf16[256,128,128]{2,1,0:T(8,128)(2,1)} %refs_4_.13, ...), custom_call_target="tpu_custom_call", output_to_operand_aliasing={{5}: (4, {})} | custom-call | flops 1022361600 | bytes 13631488 | tf_op jit(solution)/shard_map/norm/pallas_call | solution.py:109
  23.5 2.5 collective-permute-start.3
  26.0 1.5 collective-permute-start.19
  27.5 5.7 %collective-permute-done.3 = bf16[256,4,128]{2,1,0:T(4,128)(2,1)S(1)} collective-permute-done((bf16[256,4,128]{2,1,0:T(4,128)(2,1)}, bf16[256,4,128]{2,1,0:T(4,128)(2,1)S(1)}, u32[]{:S(2)}, u32[]{:S(2)}) %collective-permute-start.3) | collective-permute-done | bytes 262176 | tf_op jit(solution)/shard_map/ppermute | solution.py:284
  33.2 1.8 select_select_fusion
  35.0 1.7 collective-permute-start.5
  38.3 5.6 %collective-permute-done.5.refs_2_ = bf16[128,4,128]{2,1,0:T(4,128)(2,1)S(1)} collective-permute-done((bf16[128,4,128]{2,1,0:T(4,128)(2,1)S(1)}, bf16[128,4,128]{2,1,0:T(4,128)(2,1)S(1)}, u32[]{:S(2)}, u32[]{:S(2)}) %collective-permute-start.5) | collective-permute-done | bytes 131104 | tf_op jit(solution)/shard_map/ppermute | solution.py:293
  43.8 1.5 collective-permute-start.16
  46.9 1.2 collective-permute-done.18.refs_1_
  48.1 1.5 collective-permute-start.13
  50.3 1.5 collective-permute-start.7
  51.8 18.3 %collective-permute-done.16.refs_2_ = bf16[32,128,128]{2,1,0:T(8,128)(2,1)} collective-permute-done((bf16[32,128,128]{2,1,0:T(8,128)(2,1)}, bf16[32,128,128]{2,1,0:T(8,128)(2,1)}, u32[]{:S(2)}, u32[]{:S(2)}) %collective-permute-start.16) | collective-permute-done | bytes 1048608 | tf_op jit(solution)/shard_map/ppermute | solution.py:297
  70.2 1.5 collective-permute-start.11
  73.2 53.1 %collective-permute-done.7.refs_2_ = bf16[32,128,128]{2,1,0:T(8,128)(2,1)} collective-permute-done((bf16[32,128,128]{2,1,0:T(8,128)(2,1)}, bf16[32,128,128]{2,1,0:T(8,128)(2,1)}, u32[]{:S(2)}, u32[]{:S(2)}) %collective-permute-start.7) | collective-permute-done | bytes 1048608 | tf_op jit(solution)/shard_map/ppermute | solution.py:297
  126.9 33.2 %collective-permute-done.11.refs_2_ = bf16[48,128,128]{2,1,0:T(8,128)(2,1)} collective-permute-done((bf16[48,128,128]{2,1,0:T(8,128)(2,1)}, bf16[48,128,128]{2,1,0:T(8,128)(2,1)}, u32[]{:S(2)}, u32[]{:S(2)}) %collective-permute-start.11) | collective-permute-done | bytes 1572896 | tf_op jit(solution)/shard_map/ppermute | solution.py:297
  160.1 1.5 collective-permute-start.1
  161.5 32.2 %collective-permute-done.9.refs_2_ = bf16[48,128,128]{2,1,0:T(8,128)(2,1)} collective-permute-done((bf16[48,128,128]{2,1,0:T(8,128)(2,1)}, bf16[48,128,128]{2,1,0:T(8,128)(2,1)}, u32[]{:S(2)}, u32[]{:S(2)}) %collective-permute-start.9) | collective-permute-done | bytes 1572896 | tf_op jit(solution)/shard_map/ppermute | solution.py:297
  193.8 1.7 plan.1
  195.4 3.6 %bias.1.refs_5_ = f32[512,512]{1,0:T(8,128)} custom-call(s32[3]{0:T(128)} %get-tuple-element.19.info_ref, bf16[128,4,128]{2,1,0:T(4,128)(2,1)} %get-tuple-element.35.refs_0_, bf16[128,4,128]{2,1,0:T(4,128)(2,1)} %collective-permute-done.4.refs_1_, bf16[128,4,128]{2,1,0:T(4,128)(2,1)} %copy-done.20, bf16[128,4,128]{2,1,0:T(4,128)(2,1)} %copy-done.21), custom_call_target="tpu_custom_call" | custom-call | tf_op jit(solution)/shard_map/bias/pallas_call | solution.py:138
  199.6 10.1 %attend.7.refs_9_ = bf16[256,128,128]{2,1,0:T(8,128)(2,1)} custom-call(s32[3]{0:T(128)} %get-tuple-element.19.info_ref, bf16[16,128,128]{2,1,0:T(8,128)(2,1)} %get-tuple-element.32.refs_0_, bf16[16,128,128]{2,1,0:T(8,128)(2,1)} %copy-done.18, bf16[16,128,128]{2,1,0:T(8,128)(2,1)} %copy-done.17, bf16[16,128,128]{2,1,0:T(8,128)(2,1)} %copy-done.19, ...), custom_call_target="tpu_custom_call" | custom-call | flops 2097152000 | bytes 3145728 | tf_op jit(solution)/shard_map/attend/pallas_call | solution.py:245
  209.6 3.4 %copy-done = bf16[256,128,128]{2,1,0:T(8,128)(2,1)S(1)} copy-done((bf16[256,128,128]{2,1,0:T(8,128)(2,1)S(1)}, bf16[256,128,128]{2,1,0:T(8,128)(2,1)}, u32[]{:S(2)}) %copy-start) | copy-done | bytes 8388632
  213.0 1.2 copy-done.1
  216.7 1.2 copy-done.12
  217.9 1.2 copy-done.14
  219.8 16.0 %attend.8.refs_9_ = bf16[256,128,128]{2,1,0:T(8,128)(2,1)} custom-call(s32[3]{0:T(128)S(1)} %copy-done.15, bf16[32,128,128]{2,1,0:T(8,128)(2,1)S(1)} %copy-done.12, bf16[32,128,128]{2,1,0:T(8,128)(2,1)S(1)} %copy-done.14, bf16[32,128,128]{2,1,0:T(8,128)(2,1)} %collective-permute-done.16.refs_2_, ...), custom_call_target="tpu_custom_call", output_to_operand_aliasing={{}: (10, {})} | custom-call | flops 4194304000 | bytes 6291456 | tf_op jit(solution)/shard_map/attend/pallas_call | solution.py:245
  236.4 22.7 %attend.9.refs_9_ = bf16[256,128,128]{2,1,0:T(8,128)(2,1)} custom-call(s32[3]{0:T(128)S(1)} %copy-done.16, bf16[48,128,128]{2,1,0:T(8,128)(2,1)S(1)} %copy-done.9, bf16[208,128,128]{2,1,0:T(8,128)(2,1)} %collective-permute-done.refs_1_, bf16[48,128,128]{2,1,0:T(8,128)(2,1)} %collective-permute-done.13.refs_2_, ...), custom_call_target="tpu_custom_call", output_to_operand_aliasing={{}: (10, {})} | custom-call | flops 6291456000 | bytes 9437184 | tf_op jit(solution)/shard_map/attend/pallas_call | solution.py:245
  259.1 22.7 %attend.10.refs_9_ = bf16[256,128,128]{2,1,0:T(8,128)(2,1)} custom-call(s32[3]{0:T(128)S(1)} %copy-done.16, bf16[48,128,128]{2,1,0:T(8,128)(2,1)S(1)} %copy-done.8, bf16[208,128,128]{2,1,0:T(8,128)(2,1)} %collective-permute-done.refs_1_, bf16[48,128,128]{2,1,0:T(8,128)(2,1)} %collective-permute-done.11.refs_2_, ...), custom_call_target="tpu_custom_call", output_to_operand_aliasing={{}: (10, {})} | custom-call | flops 6291456000 | bytes 9437184 | tf_op jit(solution)/shard_map/attend/pallas_call | solution.py:245
  281.9 22.9 %attend.11.refs_9_ = bf16[256,128,128]{2,1,0:T(8,128)(2,1)} custom-call(s32[3]{0:T(128)S(1)} %copy-done.16, bf16[48,128,128]{2,1,0:T(8,128)(2,1)S(1)} %copy-done.7, bf16[208,128,128]{2,1,0:T(8,128)(2,1)} %collective-permute-done.refs_1_, bf16[48,128,128]{2,1,0:T(8,128)(2,1)} %collective-permute-done.9.refs_2_, ...), custom_call_target="tpu_custom_call", output_to_operand_aliasing={{}: (10, {})} | custom-call | flops 6291456000 | bytes 9437184 | tf_op jit(solution)/shard_map/attend/pallas_call | solution.py:245
  304.8 15.9 %attend.12.refs_9_ = bf16[256,128,128]{2,1,0:T(8,128)(2,1)} custom-call(s32[3]{0:T(128)S(1)} %copy-done.16, bf16[32,128,128]{2,1,0:T(8,128)(2,1)S(1)} %copy-done.11, bf16[208,128,128]{2,1,0:T(8,128)(2,1)} %collective-permute-done.refs_1_, bf16[32,128,128]{2,1,0:T(8,128)(2,1)} %collective-permute-done.7.refs_2_, ...), custom_call_target="tpu_custom_call", output_to_operand_aliasing={{}: (10, {})} | custom-call | flops 4194304000 | bytes 6291456 | tf_op jit(solution)/shard_map/attend/pallas_call | solution.py:245
  320.8 15.9 %attend.13 = bf16[256,128,128]{2,1,0:T(8,128)(2,1)} custom-call(s32[3]{0:T(128)S(1)} %copy-done.16, bf16[32,128,128]{2,1,0:T(8,128)(2,1)S(1)} %copy-done.10, bf16[208,128,128]{2,1,0:T(8,128)(2,1)} %collective-permute-done.refs_1_, bf16[32,128,128]{2,1,0:T(8,128)(2,1)} %collective-permute-done.1.refs_2_, ...), custom_call_target="tpu_custom_call", output_to_operand_aliasing={{}: (10, {})} | custom-call | flops 4194304000 | bytes 6291456 | tf_op jit(solution)/shard_map/attend/pallas_call | solution.py:245
  (68 shorter events, 10.9 us)
Async XLA Ops:
  22.6 213.7 %collective-permute-start = (bf16[208,128,128]{2,1,0:T(8,128)(2,1)}, bf16[208,128,128]{2,1,0:T(8,128)(2,1)}, u32[]{:S(2)}, u32[]{:S(2)}) collective-permute-start(bf16[208,128,128]{2,1,0:T(8,128)(2,1)} %get-tuple-element.23), channel_id=1, source_target_pairs={{0,1},{1,0},{2,3},{3,2},{4,5},{5,4},{6,7},{7,6}} | collective-permute-start | bytes 20447240 | tf_op jit(solution)/shard_map/ppermute | solution.py:299
  23.5 9.7 %collective-permute-start.3 = (bf16[256,4,128]{2,1,0:T(4,128)(2,1)}, bf16[256,4,128]{2,1,0:T(4,128)(2,1)S(1)}, u32[]{:S(2)}, u32[]{:S(2)}) collective-permute-start(bf16[256,4,128]{2,1,0:T(4,128)(2,1)} %get-tuple-element.24), channel_id=1, source_target_pairs={{0,4},{4,0},{1,5},{5,1},{2,6},{6,2},{3,7},{7,3}} | collective-permute-start | bytes 786440 | tf_op jit(solution)/shard_map/ppermute | solution.py:284
  26.0 20.4 %collective-permute-start.19 = (bf16[16,128,128]{2,1,0:T(8,128)(2,1)}, bf16[16,128,128]{2,1,0:T(8,128)(2,1)S(1)}, u32[]{:S(2)}, u32[]{:S(2)}) collective-permute-start(bf16[16,128,128]{2,1,0:T(8,128)(2,1)} %get-tuple-element.32.refs_0_), channel_id=1, source_target_pairs={{0,2},{1,3},{2,0},{3,1},{4,6},{5,7},{6,4},{7,5}} | collective-permute-start | bytes 1572872 | tf_op jit(solution)/shard_map/ppermute | solution.py:297
  35.0 8.8 %collective-permute-start.5 = (bf16[128,4,128]{2,1,0:T(4,128)(2,1)S(1)}, bf16[128,4,128]{2,1,0:T(4,128)(2,1)S(1)}, u32[]{:S(2)}, u32[]{:S(2)}) collective-permute-start(bf16[128,4,128]{2,1,0:T(4,128)(2,1)S(1)} %get-tuple-element.34), channel_id=1, source_target_pairs={{0,2},{1,3},{2,0},{3,1},{4,6},{5,7},{6,4},{7,5}} | collective-permute-start | bytes 393224 | tf_op jit(solution)/shard_map/ppermute | solution.py:293
  36.7 8.8 %collective-permute-start.6 = (bf16[128,4,128]{2,1,0:T(4,128)(2,1)S(1)}, bf16[128,4,128]{2,1,0:T(4,128)(2,1)S(1)}, u32[]{:S(2)}, u32[]{:S(2)}) collective-permute-start(bf16[128,4,128]{2,1,0:T(4,128)(2,1)S(1)} %get-tuple-element.33), channel_id=1, source_target_pairs={{0,3},{1,2},{2,1},{3,0},{4,7},{5,6},{6,5},{7,4}} | collective-permute-start | bytes 393224 | tf_op jit(solution)/shard_map/ppermute | solution.py:293
  37.8 8.5 %collective-permute-start.4 = (bf16[128,4,128]{2,1,0:T(4,128)(2,1)S(1)}, bf16[128,4,128]{2,1,0:T(4,128)(2,1)}, u32[]{:S(2)}, u32[]{:S(2)}) collective-permute-start(bf16[128,4,128]{2,1,0:T(4,128)(2,1)S(1)} %select_select_fusion.2), channel_id=1, source_target_pairs={{0,1},{1,0},{2,3},{3,2},{4,5},{5,4},{6,7},{7,6}} | collective-permute-start | bytes 393224 | tf_op jit(solution)/shard_map/ppermute | solution.py:293
  43.8 82.5 %copy-start.20 = (bf16[128,4,128]{2,1,0:T(4,128)(2,1)}, bf16[128,4,128]{2,1,0:T(4,128)(2,1)S(1)}, u32[]{:S(2)}) copy-start(bf16[128,4,128]{2,1,0:T(4,128)(2,1)S(1)} %collective-permute-done.5.refs_2_) | copy-start | bytes 393220
  43.8 26.3 %collective-permute-start.16 = (bf16[32,128,128]{2,1,0:T(8,128)(2,1)}, bf16[32,128,128]{2,1,0:T(8,128)(2,1)}, u32[]{:S(2)}, u32[]{:S(2)}) collective-permute-start(bf16[32,128,128]{2,1,0:T(8,128)(2,1)} %get-tuple-element.31.refs_0_), channel_id=1, source_target_pairs={{0,2},{1,3},{2,0},{3,1},{4,6},{5,7},{6,4},{7,5}} | collective-permute-start | bytes 3145736 | tf_op jit(solution)/shard_map/ppermute | solution.py:297
  45.5 80.8 %copy-start.21 = (bf16[128,4,128]{2,1,0:T(4,128)(2,1)}, bf16[128,4,128]{2,1,0:T(4,128)(2,1)S(1)}, u32[]{:S(2)}) copy-start(bf16[128,4,128]{2,1,0:T(4,128)(2,1)S(1)} %collective-permute-done.6.refs_3_) | copy-start | bytes 393220
  45.5 2.6 collective-permute-start.18
  46.3 25.3 %collective-permute-start.15 = (bf16[32,128,128]{2,1,0:T(8,128)(2,1)}, bf16[32,128,128]{2,1,0:T(8,128)(2,1)S(1)}, u32[]{:S(2)}, u32[]{:S(2)}) collective-permute-start(bf16[32,128,128]{2,1,0:T(8,128)(2,1)} %get-tuple-element.31.refs_0_), channel_id=1, source_target_pairs={{0,1},{1,0},{2,3},{3,2},{4,5},{5,4},{6,7},{7,6}} | collective-permute-start | bytes 3145736 | tf_op jit(solution)/shard_map/ppermute | solution.py:299
  46.4 25.3 %copy-start.17 = (bf16[16,128,128]{2,1,0:T(8,128)(2,1)}, bf16[16,128,128]{2,1,0:T(8,128)(2,1)S(1)}, u32[]{:S(2)}) copy-start(bf16[16,128,128]{2,1,0:T(8,128)(2,1)S(1)} %collective-permute-done.19.refs_2_) | copy-start | bytes 1572868
  46.4 4.0 %collective-permute-start.20 = (bf16[16,128,128]{2,1,0:T(8,128)(2,1)S(1)}, bf16[16,128,128]{2,1,0:T(8,128)(2,1)S(1)}, u32[]{:S(2)}, u32[]{:S(2)}) collective-permute-start(bf16[16,128,128]{2,1,0:T(8,128)(2,1)S(1)} %collective-permute-done.19.refs_2_), channel_id=1, source_target_pairs={{0,1},{1,0},{2,3},{3,2},{4,5},{5,4},{6,7},{7,6}} | collective-permute-start | bytes 1572872 | tf_op jit(solution)/shard_map/ppermute | solution.py:302
  48.1 24.6 %copy-start.18 = (bf16[16,128,128]{2,1,0:T(8,128)(2,1)}, bf16[16,128,128]{2,1,0:T(8,128)(2,1)S(1)}, u32[]{:S(2)}) copy-start(bf16[16,128,128]{2,1,0:T(8,128)(2,1)S(1)} %collective-permute-done.18.refs_1_) | copy-start | bytes 1572868
  48.1 78.3 %collective-permute-start.13 = (bf16[48,128,128]{2,1,0:T(8,128)(2,1)}, bf16[48,128,128]{2,1,0:T(8,128)(2,1)}, u32[]{:S(2)}, u32[]{:S(2)}) collective-permute-start(bf16[48,128,128]{2,1,0:T(8,128)(2,1)} %get-tuple-element.30.refs_0_), channel_id=1, source_target_pairs={{0,2},{1,3},{2,0},{3,1},{4,6},{5,7},{6,4},{7,5}} | collective-permute-start | bytes 4718600 | tf_op jit(solution)/shard_map/ppermute | solution.py:297
  50.3 22.9 %copy-start.19 = (bf16[16,128,128]{2,1,0:T(8,128)(2,1)}, bf16[16,128,128]{2,1,0:T(8,128)(2,1)S(1)}, u32[]{:S(2)}) copy-start(bf16[16,128,128]{2,1,0:T(8,128)(2,1)S(1)} %collective-permute-done.20.refs_3_) | copy-start | bytes 1572868
  50.3 76.0 %collective-permute-start.7 = (bf16[32,128,128]{2,1,0:T(8,128)(2,1)}, bf16[32,128,128]{2,1,0:T(8,128)(2,1)}, u32[]{:S(2)}, u32[]{:S(2)}) collective-permute-start(bf16[32,128,128]{2,1,0:T(8,128)(2,1)} %get-tuple-element.27.refs_0_), channel_id=1, source_target_pairs={{0,2},{1,3},{2,0},{3,1},{4,6},{5,7},{6,4},{7,5}} | collective-permute-start | bytes 3145736 | tf_op jit(solution)/shard_map/ppermute | solution.py:297
  70.2 89.9 %collective-permute-start.11 = (bf16[48,128,128]{2,1,0:T(8,128)(2,1)}, bf16[48,128,128]{2,1,0:T(8,128)(2,1)}, u32[]{:S(2)}, u32[]{:S(2)}) collective-permute-start(bf16[48,128,128]{2,1,0:T(8,128)(2,1)} %get-tuple-element.29.refs_0_), channel_id=1, source_target_pairs={{0,2},{1,3},{2,0},{3,1},{4,6},{5,7},{6,4},{7,5}} | collective-permute-start | bytes 4718600 | tf_op jit(solution)/shard_map/ppermute | solution.py:297
  72.7 121.1 %collective-permute-start.9 = (bf16[48,128,128]{2,1,0:T(8,128)(2,1)}, bf16[48,128,128]{2,1,0:T(8,128)(2,1)}, u32[]{:S(2)}, u32[]{:S(2)}) collective-permute-start(bf16[48,128,128]{2,1,0:T(8,128)(2,1)} %get-tuple-element.28.refs_0_), channel_id=1, source_target_pairs={{0,2},{1,3},{2,0},{3,1},{4,6},{5,7},{6,4},{7,5}} | collective-permute-start | bytes 4718600 | tf_op jit(solution)/shard_map/ppermute | solution.py:297
  126.4 72.7 %collective-permute-start.17 = (bf16[32,128,128]{2,1,0:T(8,128)(2,1)}, bf16[32,128,128]{2,1,0:T(8,128)(2,1)}, u32[]{:S(2)}, u32[]{:S(2)}) collective-permute-start(bf16[32,128,128]{2,1,0:T(8,128)(2,1)} %collective-permute-done.16.refs_2_), channel_id=1, source_target_pairs={{0,1},{1,0},{2,3},{3,2},{4,5},{5,4},{6,7},{7,6}} | collective-permute-start | bytes 3145736 | tf_op jit(solution)/shard_map/ppermute | solution.py:302
  126.4 109.5 %collective-permute-start.14 = (bf16[48,128,128]{2,1,0:T(8,128)(2,1)}, bf16[48,128,128]{2,1,0:T(8,128)(2,1)}, u32[]{:S(2)}, u32[]{:S(2)}) collective-permute-start(bf16[48,128,128]{2,1,0:T(8,128)(2,1)} %collective-permute-done.13.refs_2_), channel_id=1, source_target_pairs={{0,1},{1,0},{2,3},{3,2},{4,5},{5,4},{6,7},{7,6}} | collective-permute-start | bytes 4718600 | tf_op jit(solution)/shard_map/ppermute | solution.py:302
  160.1 75.8 %collective-permute-start.1 = (bf16[32,128,128]{2,1,0:T(8,128)(2,1)}, bf16[32,128,128]{2,1,0:T(8,128)(2,1)}, u32[]{:S(2)}, u32[]{:S(2)}) collective-permute-start(bf16[32,128,128]{2,1,0:T(8,128)(2,1)} %get-tuple-element.22.refs_0_), channel_id=1, source_target_pairs={{0,2},{1,3},{2,0},{3,1},{4,6},{5,7},{6,4},{7,5}} | collective-permute-start | bytes 3145736 | tf_op jit(solution)/shard_map/ppermute | solution.py:297
  193.8 65.4 %collective-permute-start.12 = (bf16[48,128,128]{2,1,0:T(8,128)(2,1)}, bf16[48,128,128]{2,1,0:T(8,128)(2,1)}, u32[]{:S(2)}, u32[]{:S(2)}) collective-permute-start(bf16[48,128,128]{2,1,0:T(8,128)(2,1)} %collective-permute-done.11.refs_2_), channel_id=1, source_target_pairs={{0,1},{1,0},{2,3},{3,2},{4,5},{5,4},{6,7},{7,6}} | collective-permute-start | bytes 4718600 | tf_op jit(solution)/shard_map/ppermute | solution.py:302
  199.1 82.8 %collective-permute-start.10 = (bf16[48,128,128]{2,1,0:T(8,128)(2,1)}, bf16[48,128,128]{2,1,0:T(8,128)(2,1)}, u32[]{:S(2)}, u32[]{:S(2)}) collective-permute-start(bf16[48,128,128]{2,1,0:T(8,128)(2,1)} %collective-permute-done.9.refs_2_), channel_id=1, source_target_pairs={{0,1},{1,0},{2,3},{3,2},{4,5},{5,4},{6,7},{7,6}} | collective-permute-start | bytes 4718600 | tf_op jit(solution)/shard_map/ppermute | solution.py:302
  219.8 16.6 %copy-start.6 = (bf16[128,128]{1,0:T(8,128)(2,1)S(1)}, bf16[128,128]{1,0:T(8,128)(2,1)}, u32[]{:S(2)}) copy-start(bf16[128,128]{1,0:T(8,128)(2,1)} %refs_8_.13) | copy-start | bytes 98308
  219.8 16.6 %copy-start.9 = (bf16[48,128,128]{2,1,0:T(8,128)(2,1)S(1)}, bf16[48,128,128]{2,1,0:T(8,128)(2,1)}, u32[]{:S(2)}) copy-start(bf16[48,128,128]{2,1,0:T(8,128)(2,1)} %get-tuple-element.30.refs_0_) | copy-start | bytes 4718596
  219.8 16.6 %copy-start.16 = (s32[3]{0:T(128)S(1)}, s32[3]{0:T(128)}, u32[]{:S(2)}) copy-start(s32[3]{0:T(128)} %get-tuple-element.19.info_ref) | copy-start | bytes 40
  235.8 23.3 %copy-start.8 = (bf16[48,128,128]{2,1,0:T(8,128)(2,1)S(1)}, bf16[48,128,128]{2,1,0:T(8,128)(2,1)}, u32[]{:S(2)}) copy-start(bf16[48,128,128]{2,1,0:T(8,128)(2,1)} %get-tuple-element.29.refs_0_) | copy-start | bytes 4718596
  235.8 69.0 %collective-permute-start.8 = (bf16[32,128,128]{2,1,0:T(8,128)(2,1)}, bf16[32,128,128]{2,1,0:T(8,128)(2,1)S(1)}, u32[]{:S(2)}, u32[]{:S(2)}) collective-permute-start(bf16[32,128,128]{2,1,0:T(8,128)(2,1)} %collective-permute-done.7.refs_2_), channel_id=1, source_target_pairs={{0,1},{1,0},{2,3},{3,2},{4,5},{5,4},{6,7},{7,6}} | collective-permute-start | bytes 3145736 | tf_op jit(solution)/shard_map/ppermute | solution.py:302
  235.9 84.9 %collective-permute-start.2 = (bf16[32,128,128]{2,1,0:T(8,128)(2,1)}, bf16[32,128,128]{2,1,0:T(8,128)(2,1)S(1)}, u32[]{:S(2)}, u32[]{:S(2)}) collective-permute-start(bf16[32,128,128]{2,1,0:T(8,128)(2,1)} %collective-permute-done.1.refs_2_), channel_id=1, source_target_pairs={{0,1},{1,0},{2,3},{3,2},{4,5},{5,4},{6,7},{7,6}} | collective-permute-start | bytes 3145736 | tf_op jit(solution)/shard_map/ppermute | solution.py:302
  259.1 22.8 %copy-start.7 = (bf16[48,128,128]{2,1,0:T(8,128)(2,1)S(1)}, bf16[48,128,128]{2,1,0:T(8,128)(2,1)}, u32[]{:S(2)}) copy-start(bf16[48,128,128]{2,1,0:T(8,128)(2,1)} %get-tuple-element.28.refs_0_) | copy-start | bytes 4718596
  281.9 23.0 %copy-start.11 = (bf16[32,128,128]{2,1,0:T(8,128)(2,1)S(1)}, bf16[32,128,128]{2,1,0:T(8,128)(2,1)}, u32[]{:S(2)}) copy-start(bf16[32,128,128]{2,1,0:T(8,128)(2,1)} %get-tuple-element.27.refs_0_) | copy-start | bytes 3145732
  (11 other events, 43.7 us)

commit v6 on v5

--- a/solution.py
+++ b/solution.py
@@ -13,7 +13,7 @@
 NORM_ROWS = 16
 ATTEND_ROWS = 16
 GROUP = 16
-ATTEND_VMEM = (67043328, 40 * 1024 * 1024)
+ATTEND_VMEM = 40 * 1024 * 1024
 SCORE_BOUND = 1e8
 VALUE_BOUND = 1e20
 SUM_RANGE = (1e-10, 1e15)
@@ -142,7 +142,7 @@
             in_specs=[whole(p.shape) for p in parts], out_specs=whole(shape),
         ),
         out_shape=jax.ShapeDtypeStruct(shape, f32),
-        compiler_params=VMEM_LIMIT,
+        compiler_params=pltpu.CompilerParams(vmem_limit_bytes=ATTEND_VMEM),
         name="bias",
     )(info, *parts)
 
@@ -258,7 +258,7 @@
         ),
         out_shape=jax.ShapeDtypeStruct(z.shape, z.dtype),
         input_output_aliases=alias,
-        compiler_params=pltpu.CompilerParams(vmem_limit_bytes=ATTEND_VMEM[prev is not None]),
+        compiler_params=pltpu.CompilerParams(vmem_limit_bytes=ATTEND_VMEM),
         cost_estimate=pl.CostEstimate(flops=rows * cols * chan * 8000, bytes_accessed=rows * cols * chan * 12, transcendentals=0),
         name="attend",
     )(*args)

time: 338 us -> 338 us (level)
  local copies, waits for them, and re-layouts: 11.2 us -> 20.2 us
  Pallas kernels: 154 us -> 150 us
    unnamed x44 -> x60, local copies, waits for them, and re-layouts: 11.2 us -> 20.2 us
  transfers between devices with their start and end apart: 21 -> 21, of which waited for: 9 -> 8; matrix products, arithmetic and copies ran while one was open for 1% -> 1% of each run, Pallas kernels for 34% -> 33%
where the time goes in v6:
time: 338 us; the launch traced here: 337 us
  Pallas kernels  150 us (44%)
  waiting for transfers between devices  148 us (44%)
  local copies, waits for them, and re-layouts  20.2 us (6%)
  starting transfers between devices  16.3 us (5%)
    ppermute x7, waiting for transfers between devices, inner(): far.append(lax.ppermute(a, 'col', x_pairs))  136 us
    pallas_call x7, Pallas kernels, attend(): pl.pallas_call(functools.partial(attend_kernel, heads, sizes), grid_spec=...  124 us
    pallas_call x3, Pallas kernels, normalize(): pl.pallas_call(functools.partial(norm_kernel, places, prev is not None),...  22.6 us
    unnamed x60, local copies, waits for them, and re-layouts  20.2 us
    ppermute x7, starting transfers between devices, inner(): far.append(lax.ppermute(a, 'col', x_pairs))  8.66 us
  transfers between devices with their start and end apart: 21, of which 8 were waited for; matrix products, arithmetic and copies ran while one was open for 1% of the time, Pallas kernels for 33%

profile of v6, /device:TPU:0, one launch (start us, length us, event | category | flops | bytes accessed | tf_op | source)
XLA Modules:
  0.0 337.3 jit_solution(6464423833445986915)
XLA Ops:
  0.0 2.4 norm.3
  2.4 3.5 %norm.4 = (bf16[32,128,128]{2,1,0:T(8,128)(2,1)}, bf16[256,4,128]{2,1,0:T(4,128)(2,1)}) custom-call(bf16[256,128,128]{2,1,0:T(8,128)(2,1)} %refs_4_.13, f32[1,128]{1,0:T(1,128)} %bitcast.9, f32[1,128]{1,0:T(1,128)} %bitcast.13, bf16[4,128]{1,0:T(4,128)(2,1)} %bitcast.5, ...), custom_call_target="tpu_custom_call", output_to_operand_aliasing={{1}: (4, {})} | custom-call | flops 157286400 | bytes 2097152 | tf_op jit(solution)/shard_map/norm/pallas_call | solution.py:109
  5.9 16.7 %norm.5 = (bf16[48,128,128]{2,1,0:T(8,128)(2,1)}, bf16[48,128,128]{2,1,0:T(8,128)(2,1)}, bf16[48,128,128]{2,1,0:T(8,128)(2,1)}, bf16[32,128,128]{2,1,0:T(8,128)(...) custom-call(bf16[256,128,128]{2,1,0:T(8,128)(2,1)} %refs_4_.13, ...), custom_call_target="tpu_custom_call", output_to_operand_aliasing={{5}: (4, {})} | custom-call | flops 1022361600 | bytes 13631488 | tf_op jit(solution)/shard_map/norm/pallas_call | solution.py:109
  23.4 2.5 collective-permute-start.3
  26.0 1.5 collective-permute-start.19
  27.4 5.7 %collective-permute-done.3 = bf16[256,4,128]{2,1,0:T(4,128)(2,1)S(1)} collective-permute-done((bf16[256,4,128]{2,1,0:T(4,128)(2,1)}, bf16[256,4,128]{2,1,0:T(4,128)(2,1)S(1)}, u32[]{:S(2)}, u32[]{:S(2)}) %collective-permute-start.3) | collective-permute-done | bytes 262176 | tf_op jit(solution)/shard_map/ppermute | solution.py:284
  33.1 1.8 select_select_fusion
  35.0 1.7 collective-permute-start.5
  36.7 1.1 select_select_fusion.2
  38.2 5.6 %collective-permute-done.5.refs_2_ = bf16[128,4,128]{2,1,0:T(4,128)(2,1)S(1)} collective-permute-done((bf16[128,4,128]{2,1,0:T(4,128)(2,1)S(1)}, bf16[128,4,128]{2,1,0:T(4,128)(2,1)S(1)}, u32[]{:S(2)}, u32[]{:S(2)}) %collective-permute-start.5) | collective-permute-done | bytes 131104 | tf_op jit(solution)/shard_map/ppermute | solution.py:293
  44.4 1.5 collective-permute-start.16
  49.5 1.1 collective-permute-start.13
  51.8 1.1 collective-permute-start.7
  52.9 17.9 %collective-permute-done.16.refs_2_ = bf16[32,128,128]{2,1,0:T(8,128)(2,1)} collective-permute-done((bf16[32,128,128]{2,1,0:T(8,128)(2,1)}, bf16[32,128,128]{2,1,0:T(8,128)(2,1)}, u32[]{:S(2)}, u32[]{:S(2)}) %collective-permute-start.16) | collective-permute-done | bytes 1048608 | tf_op jit(solution)/shard_map/ppermute | solution.py:297
  70.8 1.5 collective-permute-start.11
  73.8 53.2 %collective-permute-done.7.refs_2_ = bf16[32,128,128]{2,1,0:T(8,128)(2,1)} collective-permute-done((bf16[32,128,128]{2,1,0:T(8,128)(2,1)}, bf16[32,128,128]{2,1,0:T(8,128)(2,1)}, u32[]{:S(2)}, u32[]{:S(2)}) %collective-permute-start.7) | collective-permute-done | bytes 1048608 | tf_op jit(solution)/shard_map/ppermute | solution.py:297
  127.5 33.2 %collective-permute-done.11.refs_2_ = bf16[48,128,128]{2,1,0:T(8,128)(2,1)} collective-permute-done((bf16[48,128,128]{2,1,0:T(8,128)(2,1)}, bf16[48,128,128]{2,1,0:T(8,128)(2,1)}, u32[]{:S(2)}, u32[]{:S(2)}) %collective-permute-start.11) | collective-permute-done | bytes 1572896 | tf_op jit(solution)/shard_map/ppermute | solution.py:297
  160.7 1.5 collective-permute-start.1
  162.1 32.2 %collective-permute-done.9.refs_2_ = bf16[48,128,128]{2,1,0:T(8,128)(2,1)} collective-permute-done((bf16[48,128,128]{2,1,0:T(8,128)(2,1)}, bf16[48,128,128]{2,1,0:T(8,128)(2,1)}, u32[]{:S(2)}, u32[]{:S(2)}) %collective-permute-start.9) | collective-permute-done | bytes 1572896 | tf_op jit(solution)/shard_map/ppermute | solution.py:297
  194.4 1.7 plan.1
  200.3 1.4 bias.1.refs_5_
  202.2 3.4 %copy-done = bf16[256,128,128]{2,1,0:T(8,128)(2,1)S(1)} copy-done((bf16[256,128,128]{2,1,0:T(8,128)(2,1)S(1)}, bf16[256,128,128]{2,1,0:T(8,128)(2,1)}, u32[]{:S(2)}) %copy-start) | copy-done | bytes 8388632
  208.0 1.0 copy-done.13
  209.0 1.0 copy-done.15
  210.1 1.0 copy-done.17
  212.8 7.9 %attend.7.refs_9_ = bf16[256,128,128]{2,1,0:T(8,128)(2,1)} custom-call(s32[3]{0:T(128)S(1)} %copy-done.28, bf16[16,128,128]{2,1,0:T(8,128)(2,1)S(1)} %copy-done.13, bf16[16,128,128]{2,1,0:T(8,128)(2,1)S(1)} %copy-done.17, bf16[16,128,128]{2,1,0:T(8,128)(2,1)S(1)} %copy-done.15, bf16[16,128,128]{2,1,0:T(8,128)(2,1)S(1)} %copy-done.19, ...), custom_call_target="tpu_custom_call" | custom-call | flops 2097152000 | bytes 3145728 | tf_op jit(solution)/shard_map/attend/pallas_call | solution.py:245
  220.7 16.0 %attend.8.refs_9_ = bf16[256,128,128]{2,1,0:T(8,128)(2,1)} custom-call(s32[3]{0:T(128)S(1)} %copy-done.29, bf16[32,128,128]{2,1,0:T(8,128)(2,1)S(1)} %copy-done.10, bf16[32,128,128]{2,1,0:T(8,128)(2,1)S(1)} %copy-done.12, bf16[32,128,128]{2,1,0:T(8,128)(2,1)} %collective-permute-done.16.refs_2_, ...), custom_call_target="tpu_custom_call", output_to_operand_aliasing={{}: (10, {})} | custom-call | flops 4194304000 | bytes 6291456 | tf_op jit(solution)/shard_map/attend/pallas_call | solution.py:245
  237.2 22.7 %attend.9.refs_9_ = bf16[256,128,128]{2,1,0:T(8,128)(2,1)} custom-call(s32[3]{0:T(128)S(1)} %copy-done.29, bf16[48,128,128]{2,1,0:T(8,128)(2,1)S(1)} %copy-done.7, bf16[208,128,128]{2,1,0:T(8,128)(2,1)} %collective-permute-done.refs_1_, bf16[48,128,128]{2,1,0:T(8,128)(2,1)} %collective-permute-done.13.refs_2_, ...), custom_call_target="tpu_custom_call", output_to_operand_aliasing={{}: (10, {})} | custom-call | flops 6291456000 | bytes 9437184 | tf_op jit(solution)/shard_map/attend/pallas_call | solution.py:245
  260.0 22.7 %attend.10.refs_9_ = bf16[256,128,128]{2,1,0:T(8,128)(2,1)} custom-call(s32[3]{0:T(128)S(1)} %copy-done.29, bf16[48,128,128]{2,1,0:T(8,128)(2,1)S(1)} %copy-done.6, bf16[208,128,128]{2,1,0:T(8,128)(2,1)} %collective-permute-done.refs_1_, bf16[48,128,128]{2,1,0:T(8,128)(2,1)} %collective-permute-done.11.refs_2_, ...), custom_call_target="tpu_custom_call", output_to_operand_aliasing={{}: (10, {})} | custom-call | flops 6291456000 | bytes 9437184 | tf_op jit(solution)/shard_map/attend/pallas_call | solution.py:245
  282.7 22.8 %attend.11.refs_9_ = bf16[256,128,128]{2,1,0:T(8,128)(2,1)} custom-call(s32[3]{0:T(128)S(1)} %copy-done.29, bf16[48,128,128]{2,1,0:T(8,128)(2,1)S(1)} %copy-done.5, bf16[208,128,128]{2,1,0:T(8,128)(2,1)} %collective-permute-done.refs_1_, bf16[48,128,128]{2,1,0:T(8,128)(2,1)} %collective-permute-done.9.refs_2_, ...), custom_call_target="tpu_custom_call", output_to_operand_aliasing={{}: (10, {})} | custom-call | flops 6291456000 | bytes 9437184 | tf_op jit(solution)/shard_map/attend/pallas_call | solution.py:245
  305.5 15.9 %attend.12.refs_9_ = bf16[256,128,128]{2,1,0:T(8,128)(2,1)} custom-call(s32[3]{0:T(128)S(1)} %copy-done.29, bf16[32,128,128]{2,1,0:T(8,128)(2,1)S(1)} %copy-done.9, bf16[208,128,128]{2,1,0:T(8,128)(2,1)} %collective-permute-done.refs_1_, bf16[32,128,128]{2,1,0:T(8,128)(2,1)} %collective-permute-done.7.refs_2_, ...), custom_call_target="tpu_custom_call", output_to_operand_aliasing={{}: (10, {})} | custom-call | flops 4194304000 | bytes 6291456 | tf_op jit(solution)/shard_map/attend/pallas_call | solution.py:245
  321.4 15.9 %attend.13 = bf16[256,128,128]{2,1,0:T(8,128)(2,1)} custom-call(s32[3]{0:T(128)S(1)} %copy-done.29, bf16[32,128,128]{2,1,0:T(8,128)(2,1)S(1)} %copy-done.8, bf16[208,128,128]{2,1,0:T(8,128)(2,1)} %collective-permute-done.refs_1_, bf16[32,128,128]{2,1,0:T(8,128)(2,1)} %collective-permute-done.1.refs_2_, ...), custom_call_target="tpu_custom_call", output_to_operand_aliasing={{}: (10, {})} | custom-call | flops 4194304000 | bytes 6291456 | tf_op jit(solution)/shard_map/attend/pallas_call | solution.py:245
  (84 shorter events, 18.1 us)
Async XLA Ops:
  22.6 214.6 %collective-permute-start = (bf16[208,128,128]{2,1,0:T(8,128)(2,1)}, bf16[208,128,128]{2,1,0:T(8,128)(2,1)}, u32[]{:S(2)}, u32[]{:S(2)}) collective-permute-start(bf16[208,128,128]{2,1,0:T(8,128)(2,1)} %get-tuple-element.23), channel_id=1, source_target_pairs={{0,1},{1,0},{2,3},{3,2},{4,5},{5,4},{6,7},{7,6}} | collective-permute-start | bytes 20447240 | tf_op jit(solution)/shard_map/ppermute | solution.py:299
  23.4 9.7 %collective-permute-start.3 = (bf16[256,4,128]{2,1,0:T(4,128)(2,1)}, bf16[256,4,128]{2,1,0:T(4,128)(2,1)S(1)}, u32[]{:S(2)}, u32[]{:S(2)}) collective-permute-start(bf16[256,4,128]{2,1,0:T(4,128)(2,1)} %get-tuple-element.24), channel_id=1, source_target_pairs={{0,4},{4,0},{1,5},{5,1},{2,6},{6,2},{3,7},{7,3}} | collective-permute-start | bytes 786440 | tf_op jit(solution)/shard_map/ppermute | solution.py:284
  26.0 21.8 %collective-permute-start.19 = (bf16[16,128,128]{2,1,0:T(8,128)(2,1)}, bf16[16,128,128]{2,1,0:T(8,128)(2,1)S(1)}, u32[]{:S(2)}, u32[]{:S(2)}) collective-permute-start(bf16[16,128,128]{2,1,0:T(8,128)(2,1)} %get-tuple-element.32.refs_0_), channel_id=1, source_target_pairs={{0,2},{1,3},{2,0},{3,1},{4,6},{5,7},{6,4},{7,5}} | collective-permute-start | bytes 1572872 | tf_op jit(solution)/shard_map/ppermute | solution.py:297
  35.0 8.8 %collective-permute-start.5 = (bf16[128,4,128]{2,1,0:T(4,128)(2,1)S(1)}, bf16[128,4,128]{2,1,0:T(4,128)(2,1)S(1)}, u32[]{:S(2)}, u32[]{:S(2)}) collective-permute-start(bf16[128,4,128]{2,1,0:T(4,128)(2,1)S(1)} %get-tuple-element.34), channel_id=1, source_target_pairs={{0,2},{1,3},{2,0},{3,1},{4,6},{5,7},{6,4},{7,5}} | collective-permute-start | bytes 393224 | tf_op jit(solution)/shard_map/ppermute | solution.py:293
  36.7 9.2 %collective-permute-start.6 = (bf16[128,4,128]{2,1,0:T(4,128)(2,1)S(1)}, bf16[128,4,128]{2,1,0:T(4,128)(2,1)S(1)}, u32[]{:S(2)}, u32[]{:S(2)}) collective-permute-start(bf16[128,4,128]{2,1,0:T(4,128)(2,1)S(1)} %get-tuple-element.33), channel_id=1, source_target_pairs={{0,3},{1,2},{2,1},{3,0},{4,7},{5,6},{6,5},{7,4}} | collective-permute-start | bytes 393224 | tf_op jit(solution)/shard_map/ppermute | solution.py:293
  37.8 8.8 %collective-permute-start.4 = (bf16[128,4,128]{2,1,0:T(4,128)(2,1)S(1)}, bf16[128,4,128]{2,1,0:T(4,128)(2,1)S(1)}, u32[]{:S(2)}, u32[]{:S(2)}) collective-permute-start(bf16[128,4,128]{2,1,0:T(4,128)(2,1)S(1)} %select_select_fusion.2), channel_id=1, source_target_pairs={{0,1},{1,0},{2,3},{3,2},{4,5},{5,4},{6,7},{7,6}} | collective-permute-start | bytes 393224 | tf_op jit(solution)/shard_map/ppermute | solution.py:293
  44.4 26.3 %collective-permute-start.16 = (bf16[32,128,128]{2,1,0:T(8,128)(2,1)}, bf16[32,128,128]{2,1,0:T(8,128)(2,1)}, u32[]{:S(2)}, u32[]{:S(2)}) collective-permute-start(bf16[32,128,128]{2,1,0:T(8,128)(2,1)} %get-tuple-element.31.refs_0_), channel_id=1, source_target_pairs={{0,2},{1,3},{2,0},{3,1},{4,6},{5,7},{6,4},{7,5}} | collective-permute-start | bytes 3145736 | tf_op jit(solution)/shard_map/ppermute | solution.py:297
  46.6 2.1 collective-permute-start.18
  47.2 25.0 %collective-permute-start.15 = (bf16[32,128,128]{2,1,0:T(8,128)(2,1)}, bf16[32,128,128]{2,1,0:T(8,128)(2,1)S(1)}, u32[]{:S(2)}, u32[]{:S(2)}) collective-permute-start(bf16[32,128,128]{2,1,0:T(8,128)(2,1)} %get-tuple-element.31.refs_0_), channel_id=1, source_target_pairs={{0,1},{1,0},{2,3},{3,2},{4,5},{5,4},{6,7},{7,6}} | collective-permute-start | bytes 3145736 | tf_op jit(solution)/shard_map/ppermute | solution.py:299
  47.7 3.2 collective-permute-start.20
  49.5 77.5 %collective-permute-start.13 = (bf16[48,128,128]{2,1,0:T(8,128)(2,1)}, bf16[48,128,128]{2,1,0:T(8,128)(2,1)}, u32[]{:S(2)}, u32[]{:S(2)}) collective-permute-start(bf16[48,128,128]{2,1,0:T(8,128)(2,1)} %get-tuple-element.30.refs_0_), channel_id=1, source_target_pairs={{0,2},{1,3},{2,0},{3,1},{4,6},{5,7},{6,4},{7,5}} | collective-permute-start | bytes 4718600 | tf_op jit(solution)/shard_map/ppermute | solution.py:297
  51.8 75.2 %collective-permute-start.7 = (bf16[32,128,128]{2,1,0:T(8,128)(2,1)}, bf16[32,128,128]{2,1,0:T(8,128)(2,1)}, u32[]{:S(2)}, u32[]{:S(2)}) collective-permute-start(bf16[32,128,128]{2,1,0:T(8,128)(2,1)} %get-tuple-element.27.refs_0_), channel_id=1, source_target_pairs={{0,2},{1,3},{2,0},{3,1},{4,6},{5,7},{6,4},{7,5}} | collective-permute-start | bytes 3145736 | tf_op jit(solution)/shard_map/ppermute | solution.py:297
  70.8 89.9 %collective-permute-start.11 = (bf16[48,128,128]{2,1,0:T(8,128)(2,1)}, bf16[48,128,128]{2,1,0:T(8,128)(2,1)}, u32[]{:S(2)}, u32[]{:S(2)}) collective-permute-start(bf16[48,128,128]{2,1,0:T(8,128)(2,1)} %get-tuple-element.29.refs_0_), channel_id=1, source_target_pairs={{0,2},{1,3},{2,0},{3,1},{4,6},{5,7},{6,4},{7,5}} | collective-permute-start | bytes 4718600 | tf_op jit(solution)/shard_map/ppermute | solution.py:297
  73.2 121.1 %collective-permute-start.9 = (bf16[48,128,128]{2,1,0:T(8,128)(2,1)}, bf16[48,128,128]{2,1,0:T(8,128)(2,1)}, u32[]{:S(2)}, u32[]{:S(2)}) collective-permute-start(bf16[48,128,128]{2,1,0:T(8,128)(2,1)} %get-tuple-element.28.refs_0_), channel_id=1, source_target_pairs={{0,2},{1,3},{2,0},{3,1},{4,6},{5,7},{6,4},{7,5}} | collective-permute-start | bytes 4718600 | tf_op jit(solution)/shard_map/ppermute | solution.py:297
  127.0 74.7 %collective-permute-start.17 = (bf16[32,128,128]{2,1,0:T(8,128)(2,1)}, bf16[32,128,128]{2,1,0:T(8,128)(2,1)}, u32[]{:S(2)}, u32[]{:S(2)}) collective-permute-start(bf16[32,128,128]{2,1,0:T(8,128)(2,1)} %collective-permute-done.16.refs_2_), channel_id=1, source_target_pairs={{0,1},{1,0},{2,3},{3,2},{4,5},{5,4},{6,7},{7,6}} | collective-permute-start | bytes 3145736 | tf_op jit(solution)/shard_map/ppermute | solution.py:302
  127.0 109.8 %collective-permute-start.14 = (bf16[48,128,128]{2,1,0:T(8,128)(2,1)}, bf16[48,128,128]{2,1,0:T(8,128)(2,1)}, u32[]{:S(2)}, u32[]{:S(2)}) collective-permute-start(bf16[48,128,128]{2,1,0:T(8,128)(2,1)} %collective-permute-done.13.refs_2_), channel_id=1, source_target_pairs={{0,1},{1,0},{2,3},{3,2},{4,5},{5,4},{6,7},{7,6}} | collective-permute-start | bytes 4718600 | tf_op jit(solution)/shard_map/ppermute | solution.py:302
  160.7 76.0 %collective-permute-start.1 = (bf16[32,128,128]{2,1,0:T(8,128)(2,1)}, bf16[32,128,128]{2,1,0:T(8,128)(2,1)}, u32[]{:S(2)}, u32[]{:S(2)}) collective-permute-start(bf16[32,128,128]{2,1,0:T(8,128)(2,1)} %get-tuple-element.22.refs_0_), channel_id=1, source_target_pairs={{0,2},{1,3},{2,0},{3,1},{4,6},{5,7},{6,4},{7,5}} | collective-permute-start | bytes 3145736 | tf_op jit(solution)/shard_map/ppermute | solution.py:297
  194.4 65.6 %collective-permute-start.12 = (bf16[48,128,128]{2,1,0:T(8,128)(2,1)}, bf16[48,128,128]{2,1,0:T(8,128)(2,1)}, u32[]{:S(2)}, u32[]{:S(2)}) collective-permute-start(bf16[48,128,128]{2,1,0:T(8,128)(2,1)} %collective-permute-done.11.refs_2_), channel_id=1, source_target_pairs={{0,1},{1,0},{2,3},{3,2},{4,5},{5,4},{6,7},{7,6}} | collective-permute-start | bytes 4718600 | tf_op jit(solution)/shard_map/ppermute | solution.py:302
  201.7 81.0 %collective-permute-start.10 = (bf16[48,128,128]{2,1,0:T(8,128)(2,1)}, bf16[48,128,128]{2,1,0:T(8,128)(2,1)S(1)}, u32[]{:S(2)}, u32[]{:S(2)}) collective-permute-start(bf16[48,128,128]{2,1,0:T(8,128)(2,1)} %collective-permute-done.9.refs_2_), channel_id=1, source_target_pairs={{0,1},{1,0},{2,3},{3,2},{4,5},{5,4},{6,7},{7,6}} | collective-permute-start | bytes 4718600 | tf_op jit(solution)/shard_map/ppermute | solution.py:302
  202.2 3.4 %copy-start = (bf16[256,128,128]{2,1,0:T(8,128)(2,1)S(1)}, bf16[256,128,128]{2,1,0:T(8,128)(2,1)}, u32[]{:S(2)}) copy-start(bf16[256,128,128]{2,1,0:T(8,128)(2,1)} %refs_4_.13) | copy-start | bytes 25165828
  208.0 1.0 copy-start.13
  212.8 7.9 %copy-start.4 = (bf16[128,128]{1,0:T(8,128)(2,1)S(1)}, bf16[128,128]{1,0:T(8,128)(2,1)}, u32[]{:S(2)}) copy-start(bf16[128,128]{1,0:T(8,128)(2,1)} %refs_8_.13) | copy-start | bytes 98308
  212.8 7.9 %copy-start.10 = (bf16[32,128,128]{2,1,0:T(8,128)(2,1)S(1)}, bf16[32,128,128]{2,1,0:T(8,128)(2,1)}, u32[]{:S(2)}) copy-start(bf16[32,128,128]{2,1,0:T(8,128)(2,1)} %get-tuple-element.31.refs_0_) | copy-start | bytes 3145732
  212.8 7.9 %copy-start.12 = (bf16[32,128,128]{2,1,0:T(8,128)(2,1)S(1)}, bf16[32,128,128]{2,1,0:T(8,128)(2,1)}, u32[]{:S(2)}) copy-start(bf16[32,128,128]{2,1,0:T(8,128)(2,1)} %copy-done.11) | copy-start | bytes 3145732
  212.8 7.9 %copy-start.29 = (s32[3]{0:T(128)S(1)}, s32[3]{0:T(128)}, u32[]{:S(2)}) copy-start(s32[3]{0:T(128)} %get-tuple-element.19.info_ref) | copy-start | bytes 40
  220.7 16.5 %copy-start.7 = (bf16[48,128,128]{2,1,0:T(8,128)(2,1)S(1)}, bf16[48,128,128]{2,1,0:T(8,128)(2,1)}, u32[]{:S(2)}) copy-start(bf16[48,128,128]{2,1,0:T(8,128)(2,1)} %get-tuple-element.30.refs_0_) | copy-start | bytes 4718596
  236.7 23.2 %copy-start.6 = (bf16[48,128,128]{2,1,0:T(8,128)(2,1)S(1)}, bf16[48,128,128]{2,1,0:T(8,128)(2,1)}, u32[]{:S(2)}) copy-start(bf16[48,128,128]{2,1,0:T(8,128)(2,1)} %get-tuple-element.29.refs_0_) | copy-start | bytes 4718596
  236.7 68.8 %collective-permute-start.8 = (bf16[32,128,128]{2,1,0:T(8,128)(2,1)}, bf16[32,128,128]{2,1,0:T(8,128)(2,1)S(1)}, u32[]{:S(2)}, u32[]{:S(2)}) collective-permute-start(bf16[32,128,128]{2,1,0:T(8,128)(2,1)} %collective-permute-done.7.refs_2_), channel_id=1, source_target_pairs={{0,1},{1,0},{2,3},{3,2},{4,5},{5,4},{6,7},{7,6}} | collective-permute-start | bytes 3145736 | tf_op jit(solution)/shard_map/ppermute | solution.py:302
  236.7 84.7 %collective-permute-start.2 = (bf16[32,128,128]{2,1,0:T(8,128)(2,1)}, bf16[32,128,128]{2,1,0:T(8,128)(2,1)S(1)}, u32[]{:S(2)}, u32[]{:S(2)}) collective-permute-start(bf16[32,128,128]{2,1,0:T(8,128)(2,1)} %collective-permute-done.1.refs_2_), channel_id=1, source_target_pairs={{0,1},{1,0},{2,3},{3,2},{4,5},{5,4},{6,7},{7,6}} | collective-permute-start | bytes 3145736 | tf_op jit(solution)/shard_map/ppermute | solution.py:302
  259.9 22.8 %copy-start.5 = (bf16[48,128,128]{2,1,0:T(8,128)(2,1)S(1)}, bf16[48,128,128]{2,1,0:T(8,128)(2,1)}, u32[]{:S(2)}) copy-start(bf16[48,128,128]{2,1,0:T(8,128)(2,1)} %get-tuple-element.28.refs_0_) | copy-start | bytes 4718596
  282.7 22.8 %copy-start.9 = (bf16[32,128,128]{2,1,0:T(8,128)(2,1)S(1)}, bf16[32,128,128]{2,1,0:T(8,128)(2,1)}, u32[]{:S(2)}) copy-start(bf16[32,128,128]{2,1,0:T(8,128)(2,1)} %get-tuple-element.27.refs_0_) | copy-start | bytes 3145732
  305.5 15.9 %copy-start.8 = (bf16[32,128,128]{2,1,0:T(8,128)(2,1)S(1)}, bf16[32,128,128]{2,1,0:T(8,128)(2,1)}, u32[]{:S(2)}) copy-start(bf16[32,128,128]{2,1,0:T(8,128)(2,1)} %get-tuple-element.22.refs_0_) | copy-start | bytes 3145732
  (19 other events, 15.7 us)
